TPU v7x, 32 devices: a whole 2x2x4 slice. The times are simulated.
32 devices in a mesh: grp: 2 (over y), tile: 4 (over z), coil: 2 (over x), spk: 2 (over core).
Axes of the slice: x: 2, y: 2, z: 4, core: 2. Of those that a mesh axis runs over, the one named last changes fastest.
Arguments:
- coil_maps: float32 [2, 512, 2, 256], P('coil', ('grp', 'tile', 'spk')), parts along dimension 1, may hold values from -6 to 6
- kspace_data: bfloat16 [2, 128, 2, 256], P('coil', ('grp', 'tile', 'spk')), parts along dimension 1, may hold values from -24 to 24
- interp_weights: bfloat16 [128, 6, 256], P(('grp', 'tile', 'spk')), parts along dimension 0, may hold values from 0.099609375 to 1
- sample_bins: int32 [128, 256], P(('grp', 'tile', 'spk')), parts along dimension 0, may hold values from 0 to 65535, as said below
- spoke_count: int32 [16], P(('grp', 'tile', 'spk')), parts along dimension 0, may hold values from 1 to 8, 32 in all
- thresholds: float32 [3], replicated, may hold values from 0.05 to 0.3
Outputs:
- image: float32 [512, 2, 256], P(('grp', 'tile', 'spk')), parts along dimension 0
There are 2 independent parts, one for each index of `grp`. A program takes and returns all parts, laid end to end along the dimension named above; an argument that names none is the same for every part. Nothing has to cross between parts.
Inputs may be any that keep to these rules, and one draw needn't show every extreme that they name: `sample_bins`: sample k of each spoke lies on a straight line through cell (128, 128), at offset k - 128 along the spoke's direction, coordinates taken modulo 256. `spoke_count`: each independent slice has its own 8 counts, and the whole array holds one such block of counts per slice. The 8 counts of each slice sum to 32. In every draw, at least one device of each slice holds 8 live spokes. A device's live spokes are its first ones.
All inputs are finite; a program needn't handle non-finite values.
Results may differ from a plain program's by a relative error of at most 0.0016.
Values may be sent and summed in bfloat16 or wider, within the bound.
No kernel may reach another device: no remote copies, remote signals or barrier semaphores. Data moves between devices by JAX's collectives and lax.ppermute only.
A program may use at most 64 MiB of HBM per device.

v0:
```python
import math

import jax
import jax.numpy as jnp
from jax import lax
from jax.sharding import PartitionSpec as P

N = 256
RO = 256
SPK_DEV = 8
LEVELS = 3
ITERS = 4


HIGH = lax.Precision.HIGHEST
STEP_SIZE = 0.5
RSQRT2 = 0.7071067811865476


def dft_table(length, direction):
    positions = jnp.arange(length, dtype=jnp.int32)
    phases = positions[:, None] * positions[None, :] % length
    angles = phases.astype(jnp.float32) * jnp.float32(2.0 * math.pi / length)
    norm_scale = 1.0 / math.sqrt(length)
    cosine = jnp.cos(angles) * norm_scale
    sine_tab = jnp.sin(angles) * norm_scale
    top_rows = jnp.stack([cosine, -direction * sine_tab], axis=1)
    bottom = jnp.stack([direction * sine_tab, cosine], axis=1)
    return jnp.stack([top_rows, bottom], axis=0)


def haar_matrix(length, levels):
    haar_mat = jnp.eye(length, dtype=jnp.float32)
    positions = jnp.arange(length, dtype=jnp.int32)
    out_i = positions[:, None]
    in_j = positions[None, :]
    for level_num in range(levels):
        span_len = length >> level_num
        half_len = span_len // 2
        low_hit = (out_i < half_len) & ((in_j == 2 * out_i) | (in_j == 2 * out_i + 1))
        high_pos = out_i - half_len
        high_hit = (
            (out_i >= half_len)
            & (out_i < span_len)
            & ((in_j == 2 * high_pos) | (in_j == 2 * high_pos + 1))
        )
        sign_val = jnp.where(in_j == 2 * high_pos + 1, -1.0, 1.0)
        step_mat = jnp.where(low_hit, RSQRT2, jnp.where(high_hit, sign_val * RSQRT2, 0.0))
        step_mat = step_mat + jnp.where((out_i >= span_len) & (in_j == out_i), 1.0, 0.0)
        haar_mat = jnp.dot(step_mat.astype(jnp.float32), haar_mat, precision=HIGH)
    return haar_mat


def haar_labels(length, levels):
    positions = jnp.arange(length, dtype=jnp.int32)
    band_label = jnp.ones((length,), jnp.int32)
    for level_num in range(1, levels + 1):
        band_label = band_label + (positions < length >> level_num).astype(jnp.int32)
    return band_label


def wavelet_shrink(target, thresholds, levels):
    row_count, pair_dim, col_count = target.shape
    block_len = 2**levels
    row_haar = haar_matrix(block_len, levels)
    col_haar = haar_matrix(col_count, levels)
    grouped = target.reshape(row_count // block_len, block_len, pair_dim, col_count)
    coeffs = jnp.einsum("ij,gjpc->gipc", row_haar, grouped, precision=HIGH)
    coeffs = jnp.einsum("gipc,kc->gipk", coeffs, col_haar, precision=HIGH)
    band_min = jnp.minimum(
        haar_labels(block_len, levels)[:, None], haar_labels(col_count, levels)[None, :]
    )
    active = band_min <= levels
    limits = jnp.ones(band_min.shape, jnp.float32)
    for level_num in range(levels):
        limits = jnp.where(band_min == level_num + 1, thresholds[level_num], limits)
    magnitude = jnp.sqrt(coeffs[:, :, 0] ** 2 + coeffs[:, :, 1] ** 2)
    factor = jnp.maximum(magnitude - limits, 0.0) / jnp.maximum(magnitude, limits)
    factor = jnp.where(active, factor, 1.0)
    shrunk = coeffs * factor[:, :, None, :]
    restored = jnp.einsum("gipk,kc->gipc", shrunk, col_haar, precision=HIGH)
    restored = jnp.einsum("ij,gipc->gjpc", row_haar, restored, precision=HIGH)
    return restored.reshape(row_count, pair_dim, col_count)


def complex_mul(left, right):
    real_part = left[:, 0] * right[:, 0] - left[:, 1] * right[:, 1]
    imag_part = left[:, 0] * right[:, 1] + left[:, 1] * right[:, 0]
    return jnp.stack([real_part, imag_part], axis=1)


def conj_mul(left, right):
    real_part = left[:, 0] * right[:, 0] + left[:, 1] * right[:, 1]
    imag_part = left[:, 0] * right[:, 1] - left[:, 1] * right[:, 0]
    return jnp.stack([real_part, imag_part], axis=1)


def interp_tables(load_bins, load_interp):
    grid_ids = jnp.arange(N, dtype=jnp.int32)
    row_bins = load_bins // N
    col_bins = load_bins % N
    zero_val = jnp.zeros((), jnp.bfloat16)
    row_table = jnp.zeros((load_bins.shape[0], load_bins.shape[1], N), jnp.bfloat16)
    col_table = jnp.zeros((load_bins.shape[0], N, load_bins.shape[1]), jnp.bfloat16)
    for tap_index in range(3):
        row_hit = grid_ids[None, None, :] == ((row_bins + tap_index - 1) % N)[:, :, None]
        row_table = row_table + jnp.where(
            row_hit, load_interp[:, tap_index, :][:, :, None], zero_val
        )
        col_hit = grid_ids[None, :, None] == ((col_bins + tap_index - 1) % N)[:, None, :]
        col_table = col_table + jnp.where(
            col_hit, load_interp[:, 3 + tap_index, :][:, None, :], zero_val
        )
    return (row_table, col_table)


def local(coil_maps, kspace_data, interp_weights, sample_bins, spoke_count, thresholds):
    blocks = lax.axis_size(("tile", "spk"))
    row_count = coil_maps.shape[1]
    live_total = blocks * SPK_DEV // 2
    coil_sens = coil_maps[0]
    measured = kspace_data[0]
    my_index = lax.axis_index(("tile", "spk"))
    counts = lax.all_gather(spoke_count, ("tile", "spk"), axis=0, tiled=True)
    prefix = jnp.cumsum(counts) - counts
    per_peer = -(-SPK_DEV // blocks)
    peer_ids = jnp.arange(blocks, dtype=jnp.int32)
    first_slot = (peer_ids - prefix[my_index]) % blocks
    slot_index = first_slot[:, None] + blocks * jnp.arange(per_peer, dtype=jnp.int32)[None, :]
    picked = jnp.clip(slot_index, 0, SPK_DEV - 1)
    values = jnp.concatenate([measured, interp_weights], axis=1)
    got_values = lax.all_to_all(
        values[picked], ("tile", "spk"), split_axis=0, concat_axis=0, tiled=True
    )
    got_bins = lax.all_to_all(
        sample_bins[picked], ("tile", "spk"), split_axis=0, concat_axis=0, tiled=True
    )
    my_share = SPK_DEV // 2
    wanted = my_index + blocks * jnp.arange(my_share, dtype=jnp.int32)
    source = jnp.sum((prefix[None, :] <= wanted[:, None]).astype(jnp.int32), axis=1) - 1
    depth_at = (wanted - prefix[source]) // blocks
    loaded = got_values[source, depth_at]
    load_bins = got_bins[source, depth_at]
    load_data = loaded[:, 0:2]
    load_interp = loaded[:, 2:8]
    row_table, col_table = interp_tables(load_bins, load_interp)
    n_load = row_table.shape[0]
    offset = jnp.abs(jnp.arange(RO, dtype=jnp.int32) - RO // 2).astype(jnp.float32)
    density = (offset + 0.5) * (N / (3.0 * RO * live_total))
    target_data = load_data.astype(jnp.float32)
    fwd_table = dft_table(N, 1.0)
    inv_table = dft_table(N, -1.0)

    def grid_rows(weighted):

        def grid_term(row_start, piece_rows):

            def grid_one_spoke(spoke_index, partial_value):
                row_one = lax.dynamic_index_in_dim(row_table, spoke_index, 0, keepdims=False)
                col_one = lax.dynamic_index_in_dim(col_table, spoke_index, 0, keepdims=False)
                col_slice = col_one.astype(jnp.float32)
                residue = lax.dynamic_index_in_dim(weighted, spoke_index, 0, keepdims=False)
                smeared = (col_slice[:, None, :] * residue[None, :, :]).astype(jnp.bfloat16)
                added = jnp.dot(
                    smeared.reshape(piece_rows * 2, RO), row_one, preferred_element_type=jnp.float32
                )
                return partial_value + added.reshape(piece_rows, 2, N)

            return lax.fori_loop(
                0, my_share, grid_one_spoke, jnp.zeros((piece_rows, 2, N), jnp.float32)
            )

        return grid_term

    estimate = jnp.zeros((row_count, 2, N), jnp.float32)
    for iteration in range(ITERS):
        if iteration == 0:
            weighted = -density[None, None, :] * target_data
        else:
            coil_image = complex_mul(coil_sens, estimate)
            half_done = jnp.einsum("rpc,pcqv->rqv", coil_image, fwd_table, precision=HIGH)
            turned = lax.all_to_all(
                half_done, ("tile", "spk"), split_axis=2, concat_axis=0, tiled=True
            )
            kspace = jnp.einsum("rpv,prqu->vqu", turned, fwd_table, precision=HIGH).astype(
                jnp.bfloat16
            )
            piece = lax.all_gather(kspace, ("tile", "spk"), axis=0, tiled=True)
            fold_piece_rows = piece.shape[0]
            flat_piece = piece.reshape(fold_piece_rows * 2, N)

            def fold_one_spoke(spoke_index, partial_value):
                row_one = lax.dynamic_index_in_dim(row_table, spoke_index, 0, keepdims=False)
                col_one = lax.dynamic_index_in_dim(col_table, spoke_index, 0, keepdims=False)
                inner_sum = lax.dot_general(
                    flat_piece,
                    row_one,
                    (((1,), (1,)), ((), ())),
                    preferred_element_type=jnp.float32,
                )
                inner_sum = inner_sum.reshape(fold_piece_rows, 2, RO)
                col_slice = col_one.astype(jnp.float32)
                added = jnp.sum(inner_sum * col_slice[:, None, :], axis=0)
                current = lax.dynamic_index_in_dim(partial_value, spoke_index, 0, keepdims=False)
                return lax.dynamic_update_index_in_dim(
                    partial_value, current + added, spoke_index, 0
                )

            sample_model = lax.fori_loop(
                0, my_share, fold_one_spoke, jnp.zeros((n_load, 2, RO), jnp.float32)
            )
            weighted = density[None, None, :] * (sample_model - target_data)
        grid_term = grid_rows(weighted)
        owned_rows = lax.psum_scatter(
            grid_term(jnp.int32(0), row_count * lax.axis_size(("tile", "spk"))),
            ("tile", "spk"),
            scatter_dimension=0,
            tiled=True,
        )
        partial_back = jnp.einsum("vpu,puqr->vqr", owned_rows, inv_table, precision=HIGH)
        returned = lax.all_to_all(
            partial_back, ("tile", "spk"), split_axis=2, concat_axis=0, tiled=True
        )
        coil_back = jnp.einsum("vpr,pvqc->rqc", returned, inv_table, precision=HIGH)
        gradient = lax.psum(conj_mul(coil_sens, coil_back), "coil")
        estimate = wavelet_shrink(estimate - STEP_SIZE * gradient, thresholds, LEVELS)
    return estimate


def solution(mesh):
    placed = (
        P("coil", ("grp", "tile", "spk"), None, None),
        P("coil", ("grp", "tile", "spk"), None, None),
        P(("grp", "tile", "spk"), None, None),
        P(("grp", "tile", "spk"), None),
        P(("grp", "tile", "spk")),
        P(),
    )
    return jax.shard_map(
        local,
        mesh=mesh,
        in_specs=placed,
        out_specs=P(("grp", "tile", "spk"), None, None),
        check_vma=False,
    )
```

profile of v0, /device:TPU:0, one launch (start us, length us, event | category | flops | bytes accessed | tf_op | source)
XLA Modules:
  0.0 512.3 jit_solution(6684872715194408570)
XLA Ops:
  9.2 10.6 %all-reduce = s32[8]{0:T(128)S(1)} all-reduce(s32[8]{0:T(128)S(1)} %dynamic-update-slice), channel_id=1, replica_groups=mesh['grp'=2,'tile'=4,'coil'=2,'spk'=2] {'tile','spk'}, use_global_device_ids=true, to_apply=%add | all-reduce | flops 8 | bytes 64
  22.5 3.3 all-to-all-start
  34.2 5.0 all-to-all-start.1
  39.9 5.1 all-to-all-done.1
  47.7 7.5 %while.98 = (s32[]{:T(128)}, f32[256,2,256]{2,0,1:T(8,128)}, bf16[4,256,256]{2,1,0:T(8,128)(2,1)S(1)}, f32[4,2,256]{2,1,0:T(2,128)S(1)}, bf16[4,256,256]{2,1,0:T(8,128)(2,1)S(1)}, /*index=5*/s32[]{:T(128)}, s32[]{:T(128)}) while((s32[]{:T(128)}, f32[256,2,256]{2,0,1:T(8,128)}, bf16[4,256,256]{2,1,0:T(8,128)(2,1)S(1)}, ...), condition=%wide.region_3.4_spmd.clone, body=%wide.region_2.3_spmd.clone.sunk | while | flops 67698688 | bytes 1841251 | solution.py:169
  48.8 2.1 convolution_add_fusion.8
  51.0 2.1 convolution_add_fusion.8
  53.1 2.1 convolution_add_fusion.8
  57.0 2.7 select_select_fusion
  60.5 24.4 %reduce-scatter.5.cloned.1.call-done = f32[32,2,256]{2,0,1:T(8,128)} async-done(((f32[256,2,256]{2,0,1:T(8,128)}), f32[32,2,256]{2,0,1:T(8,128)}) %reduce-scatter.5.cloned.1.call-update) | async-done | bytes 65552 | tf_op jit(solution)/shard_map/reduce_scatter | solution.py:214
  89.2 3.4 all-to-all-start.2
  94.6 3.8 all-to-all-done.2
  107.4 18.6 %all-reduce.6.cloned.1.call-done = f32[32,2,256]{2,0,1:T(8,128)} async-done(((f32[32,2,256]{2,0,1:T(8,128)}), f32[32,2,256]{2,0,1:T(8,128)}) %all-reduce.6.cloned.1.call-update) | async-done | bytes 65552 | tf_op jit(solution)/shard_map/psum | solution.py:225
  133.2 4.6 all-to-all-start.3
  138.6 5.2 %all-to-all-done.3 = f32[8,1,2048]{2,1,0:T(1,128)} async-done(((f32[8,1,2048]{2,1,0:T(1,128)}), f32[8,1,2048]{2,1,0:T(1,128)}, u32[]{:S(2)}, u32[]{:S(2)}) %all-to-all-start.3) | async-done | bytes 65568 | tf_op jit(solution)/shard_map/all_to_all | solution.py:182
  143.8 2.2 reduce.1
  152.9 14.2 %all_gather.13 = bf16[256,2,256]{2,0,1:T(8,128)(2,1)S(1)} all-gather(bf16[32,2,256]{2,0,1:T(8,128)(2,1)S(1)} %fusion.32), channel_id=1, replica_groups=mesh['grp'=2,'tile'=4,'coil'=2,'spk'=2] {'tile','spk'}, dimensions={0}, use_global_device_ids=true | all-gather | bytes 294912 | tf_op jit(solution)/shard_map/all_gather | solution.py:188
  168.1 12.7 %while.95 = (s32[]{:T(128)}, f32[4,2,256]{2,1,0:T(2,128)}, bf16[4,256,256]{2,1,0:T(8,128)(2,1)S(1)}, bf16[512,256]{1,0:T(8,128)(2,1)S(1)}, bf16[4,256,256]{2,1,0:T(8,128)(2,1)S(1)}, /*index=5*/s32[]{:T(128)}) while((s32[]{:T(128)}, f32[4,2,256]{2,1,0:T(2,128)}, bf16[4,256,256]{2,1,0:T(8,128)(2,1)S(1)}, bf16[512,256]{1,0:T(8,128)(2,1)S(1)}, ...), condition=%wide.region_8.9_spmd, body=%wide.region_6.8_spmd.sunk | while | flops 67436544 | bytes 6300293 | solution.py:209
  182.3 7.5 %while.99 = (s32[]{:T(128)}, f32[256,2,256]{2,0,1:T(8,128)}, bf16[4,256,256]{2,1,0:T(8,128)(2,1)S(1)}, f32[4,2,256]{2,1,0:T(2,128)S(1)}, bf16[4,256,256]{2,1,0:T(8,128)(2,1)S(1)}, /*index=5*/s32[]{:T(128)}, s32[]{:T(128)}) while((s32[]{:T(128)}, f32[256,2,256]{2,0,1:T(8,128)}, bf16[4,256,256]{2,1,0:T(8,128)(2,1)S(1)}, ...), condition=%wide.region_10.11_spmd.clone, body=%wide.region_9.10_spmd.clone.sunk | while | flops 67698688 | bytes 1841251 | solution.py:169
  183.4 2.1 convolution_add_fusion.9
  185.5 2.1 convolution_add_fusion.9
  187.6 2.1 convolution_add_fusion.9
  189.8 28.9 %reduce-scatter.7.cloned.1.call-done = f32[32,2,256]{2,0,1:T(8,128)} async-done(((f32[256,2,256]{2,0,1:T(8,128)}), f32[32,2,256]{2,0,1:T(8,128)}) %reduce-scatter.7.cloned.1.call-update) | async-done | bytes 65552 | tf_op jit(solution)/shard_map/reduce_scatter | solution.py:214
  220.7 8.3 %all_to_all.136 = f32[8,1,2048]{2,1,0:T(1,128)S(1)} all-to-all(f32[8,1,2048]{2,1,0:T(1,128)S(1)} %reshape.884), channel_id=1, replica_groups=mesh['grp'=2,'tile'=4,'coil'=2,'spk'=2] {'tile','spk'}, dimensions={0} | all-to-all | bytes 131072 | tf_op jit(solution)/shard_map/all_to_all | solution.py:221
  231.7 19.7 %all-reduce.8.cloned.1.call-done = f32[32,2,256]{2,0,1:T(8,128)} async-done(((f32[32,2,256]{2,0,1:T(8,128)}), f32[32,2,256]{2,0,1:T(8,128)}) %all-reduce.8.cloned.1.call-update) | async-done | bytes 65552 | tf_op jit(solution)/shard_map/psum | solution.py:225
  258.9 4.6 all-to-all-start.5
  263.5 6.0 %all-to-all-done.5 = f32[8,1,2048]{2,1,0:T(1,128)} async-done(((f32[8,1,2048]{2,1,0:T(1,128)}), f32[8,1,2048]{2,1,0:T(1,128)}, u32[]{:S(2)}, u32[]{:S(2)}) %all-to-all-start.5) | async-done | bytes 65568 | tf_op jit(solution)/shard_map/all_to_all | solution.py:182
  269.5 2.2 reduce.3
  278.6 14.2 %all_gather.14 = bf16[256,2,256]{2,0,1:T(8,128)(2,1)S(1)} all-gather(bf16[32,2,256]{2,0,1:T(8,128)(2,1)S(1)} %fusion.33), channel_id=1, replica_groups=mesh['grp'=2,'tile'=4,'coil'=2,'spk'=2] {'tile','spk'}, dimensions={0}, use_global_device_ids=true | all-gather | bytes 294912 | tf_op jit(solution)/shard_map/all_gather | solution.py:188
  293.8 12.7 %while.96 = (s32[]{:T(128)}, f32[4,2,256]{2,1,0:T(2,128)}, bf16[4,256,256]{2,1,0:T(8,128)(2,1)S(1)}, bf16[512,256]{1,0:T(8,128)(2,1)S(1)}, bf16[4,256,256]{2,1,0:T(8,128)(2,1)S(1)}, /*index=5*/s32[]{:T(128)}) while((s32[]{:T(128)}, f32[4,2,256]{2,1,0:T(2,128)}, bf16[4,256,256]{2,1,0:T(8,128)(2,1)S(1)}, bf16[512,256]{1,0:T(8,128)(2,1)S(1)}, ...), condition=%wide.region_15.16_spmd, body=%wide.region_13.15_spmd.sunk | while | flops 67436544 | bytes 6300293 | solution.py:209
  307.9 7.5 %while.100 = (s32[]{:T(128)}, f32[256,2,256]{2,0,1:T(8,128)}, bf16[4,256,256]{2,1,0:T(8,128)(2,1)S(1)}, f32[4,2,256]{2,1,0:T(2,128)S(1)}, bf16[4,256,256]{2,1,0:T(8,128)(2,1)S(1)}, /*index=5*/s32[]{:T(128)}, s32[]{:T(128)}) while((s32[]{:T(128)}, f32[256,2,256]{2,0,1:T(8,128)}, bf16[4,256,256]{2,1,0:T(8,128)(2,1)S(1)}, ...), condition=%wide.region_17.18_spmd.clone, body=%wide.region_16.17_spmd.clone.sunk | while | flops 67698688 | bytes 1841251 | solution.py:169
  309.0 2.1 convolution_add_fusion.10
  311.1 2.1 convolution_add_fusion.10
  315.6 28.8 %reduce-scatter.9.cloned.1.call-done = f32[32,2,256]{2,0,1:T(8,128)} async-done(((f32[256,2,256]{2,0,1:T(8,128)}), f32[32,2,256]{2,0,1:T(8,128)}) %reduce-scatter.9.cloned.1.call-update) | async-done | bytes 65552 | tf_op jit(solution)/shard_map/reduce_scatter | solution.py:214
  346.4 8.3 %all_to_all.137 = f32[8,1,2048]{2,1,0:T(1,128)S(1)} all-to-all(f32[8,1,2048]{2,1,0:T(1,128)S(1)} %reshape.888), channel_id=1, replica_groups=mesh['grp'=2,'tile'=4,'coil'=2,'spk'=2] {'tile','spk'}, dimensions={0} | all-to-all | bytes 131072 | tf_op jit(solution)/shard_map/all_to_all | solution.py:221
  357.4 19.5 %all-reduce.10.cloned.1.call-done = f32[32,2,256]{2,0,1:T(8,128)} async-done(((f32[32,2,256]{2,0,1:T(8,128)}), f32[32,2,256]{2,0,1:T(8,128)}) %all-reduce.10.cloned.1.call-update) | async-done | bytes 65552 | tf_op jit(solution)/shard_map/psum | solution.py:225
  384.4 4.6 all-to-all-start.7
  389.0 6.0 %all-to-all-done.7 = f32[8,1,2048]{2,1,0:T(1,128)} async-done(((f32[8,1,2048]{2,1,0:T(1,128)}), f32[8,1,2048]{2,1,0:T(1,128)}, u32[]{:S(2)}, u32[]{:S(2)}) %all-to-all-start.7) | async-done | bytes 65568 | tf_op jit(solution)/shard_map/all_to_all | solution.py:182
  395.0 2.2 reduce.5
  404.1 14.2 %all_gather.15 = bf16[256,2,256]{2,0,1:T(8,128)(2,1)S(1)} all-gather(bf16[32,2,256]{2,0,1:T(8,128)(2,1)S(1)} %fusion.34), channel_id=1, replica_groups=mesh['grp'=2,'tile'=4,'coil'=2,'spk'=2] {'tile','spk'}, dimensions={0}, use_global_device_ids=true | all-gather | bytes 294912 | tf_op jit(solution)/shard_map/all_gather | solution.py:188
  419.3 12.7 %while.97 = (s32[]{:T(128)}, f32[4,2,256]{2,1,0:T(2,128)}, bf16[4,256,256]{2,1,0:T(8,128)(2,1)S(1)}, bf16[512,256]{1,0:T(8,128)(2,1)S(1)}, bf16[4,256,256]{2,1,0:T(8,128)(2,1)S(1)}, /*index=5*/s32[]{:T(128)}) while((s32[]{:T(128)}, f32[4,2,256]{2,1,0:T(2,128)}, bf16[4,256,256]{2,1,0:T(8,128)(2,1)S(1)}, bf16[512,256]{1,0:T(8,128)(2,1)S(1)}, ...), condition=%wide.region_22.23_spmd, body=%wide.region_20.22_spmd.sunk | while | flops 67436544 | bytes 6300293 | solution.py:209
  433.5 7.5 %while.101 = (s32[]{:T(128)}, f32[256,2,256]{2,0,1:T(8,128)}, bf16[4,256,256]{2,1,0:T(8,128)(2,1)S(1)}, f32[4,2,256]{2,1,0:T(2,128)S(1)}, bf16[4,256,256]{2,1,0:T(8,128)(2,1)S(1)}, /*index=5*/s32[]{:T(128)}, s32[]{:T(128)}) while((s32[]{:T(128)}, f32[256,2,256]{2,0,1:T(8,128)}, bf16[4,256,256]{2,1,0:T(8,128)(2,1)S(1)}, ...), condition=%wide.region_24.25_spmd.clone, body=%wide.region_23.24_spmd.clone.sunk | while | flops 67698688 | bytes 1841251 | solution.py:169
  434.6 2.1 convolution_add_fusion.11
  436.7 2.1 convolution_add_fusion.11
  438.9 2.1 convolution_add_fusion.11
  441.0 28.9 %reduce-scatter.11.cloned.1.call-done = f32[32,2,256]{2,0,1:T(8,128)} async-done(((f32[256,2,256]{2,0,1:T(8,128)}), f32[32,2,256]{2,0,1:T(8,128)}) %reduce-scatter.11.cloned.1.call-update) | async-done | bytes 65552 | tf_op jit(solution)/shard_map/reduce_scatter | solution.py:214
  472.0 8.3 %all_to_all.138 = f32[8,1,2048]{2,1,0:T(1,128)S(1)} all-to-all(f32[8,1,2048]{2,1,0:T(1,128)S(1)} %reshape.892), channel_id=1, replica_groups=mesh['grp'=2,'tile'=4,'coil'=2,'spk'=2] {'tile','spk'}, dimensions={0} | all-to-all | bytes 131072 | tf_op jit(solution)/shard_map/all_to_all | solution.py:221
  483.0 19.5 %all-reduce.12.cloned.1.call-done = f32[32,2,256]{2,0,1:T(8,128)} async-done(((f32[32,2,256]{2,0,1:T(8,128)}), f32[32,2,256]{2,0,1:T(8,128)}) %all-reduce.12.cloned.1.call-update) | async-done | bytes 65552 | tf_op jit(solution)/shard_map/psum | solution.py:225
  (406 shorter events, 145.9 us)
Async XLA Ops:
  6.5 14.8 %copy-start = (s32[8,256]{1,0:T(8,128)S(1)}, s32[8,256]{1,0:T(8,128)}, u32[]{:S(2)}) copy-start(s32[8,256]{1,0:T(8,128)} %param.23) | copy-start | bytes 24580
  22.5 11.7 %all-to-all-start = ((s32[8,1,256]{2,1,0:T(1,128)}), s32[8,1,256]{2,1,0:T(1,128)S(1)}, u32[]{:S(2)}, u32[]{:S(2)}) async-start(s32[8,1,256]{2,1,0:T(1,128)} %copy.115), calls=%async_computation | async-start | bytes 16384 | tf_op jit(solution)/shard_map/all_to_all | solution.py:135
  27.9 31.9 %copy-start.26 = (s32[8]{0:T(128)}, s32[8]{0:T(128)S(1)}, u32[]{:S(2)}) copy-start(s32[8]{0:T(128)S(1)} %get-tuple-element.881) | copy-start | bytes 100
  27.9 31.9 %copy-start.28 = (s32[8]{0:T(128)}, s32[8]{0:T(128)S(1)}, u32[]{:S(2)}) copy-start(s32[8]{0:T(128)S(1)} %get-tuple-element.882) | copy-start | bytes 100
  28.9 0.7 copy-start.19
  29.7 1.3 copy-start.23
  31.2 120.2 %copy-start.1 = (f32[1,256,2,256]{3,1,2,0:T(8,128)}, f32[1,256,2,256]{3,1,2,0:T(8,128)S(1)}, u32[]{:S(2)}) copy-start(f32[1,256,2,256]{3,1,2,0:T(8,128)S(1)} %get-tuple-element.830) | copy-start | bytes 1572868
  31.2 120.2 %copy-start.4 = (f32[1,256,2,256]{3,1,2,0:T(8,128)}, f32[1,256,2,256]{3,1,2,0:T(8,128)S(1)}, u32[]{:S(2)}) copy-start(f32[1,256,2,256]{3,1,2,0:T(8,128)S(1)} %get-tuple-element.833) | copy-start | bytes 1572868
  34.2 10.8 %all-to-all-start.1 = ((bf16[8,1,8,256]{3,2,1,0:T(8,128)(2,1)}), bf16[8,1,8,256]{3,2,1,0:T(8,128)(2,1)S(1)}, u32[]{:S(2)}, u32[]{:S(2)}) async-start(bf16[8,1,8,256]{3,2,1,0:T(8,128)(2,1)} %bitcast.26), calls=%async_computation.1 | async-start | bytes 65536 | tf_op jit(solution)/shard_map/all_to_all | solution.py:132
  39.2 45.7 %reduce-scatter.5.cloned.1.call-start = ((), (), s32[]{:S(2)}) async-start(), calls=%async_computation.13 | async-start | bytes 589824 | tf_op jit(solution)/shard_map/reduce_scatter | solution.py:214
  89.2 9.2 %all-to-all-start.2 = ((f32[8,1,2048]{2,1,0:T(1,128)}), f32[8,1,2048]{2,1,0:T(1,128)S(1)}, u32[]{:S(2)}, u32[]{:S(2)}) async-start(f32[8,1,2048]{2,1,0:T(1,128)} %reshape.880), calls=%async_computation.3 | async-start | bytes 131072 | tf_op jit(solution)/shard_map/all_to_all | solution.py:221
  92.6 33.5 %all-reduce.6.cloned.1.call-start = ((), (), s32[]{:S(2)}) async-start(), calls=%async_computation.14 | async-start | bytes 131072 | tf_op jit(solution)/shard_map/psum | solution.py:225
  105.8 0.7 copy-start.31
  133.2 10.6 %all-to-all-start.3 = ((f32[8,1,2048]{2,1,0:T(1,128)}), f32[8,1,2048]{2,1,0:T(1,128)}, u32[]{:S(2)}, u32[]{:S(2)}) async-start(f32[8,1,2048]{2,1,0:T(1,128)} %reshape.882), calls=%async_computation.4 | async-start | bytes 131072 | tf_op jit(solution)/shard_map/all_to_all | solution.py:182
  137.8 80.9 %reduce-scatter.7.cloned.1.call-start = ((), (), s32[]{:S(2)}) async-start(), calls=%async_computation.15 | async-start | bytes 589824 | tf_op jit(solution)/shard_map/reduce_scatter | solution.py:214
  169.7 1.6 copy-start.10
  172.8 1.6 copy-start.10
  174.5 0.7 copy-start.9
  176.0 1.6 copy-start.10
  177.7 0.7 copy-start.9
  179.2 1.6 copy-start.10
  189.7 61.7 %all-reduce.8.cloned.1.call-start = ((), (), s32[]{:S(2)}) async-start(), calls=%async_computation.16 | async-start | bytes 131072 | tf_op jit(solution)/shard_map/psum | solution.py:225
  251.5 1.4 copy-start.15
  252.5 1.0 copy-start.5
  252.9 1.1 copy-start.2
  258.9 10.6 %all-to-all-start.5 = ((f32[8,1,2048]{2,1,0:T(1,128)}), f32[8,1,2048]{2,1,0:T(1,128)}, u32[]{:S(2)}, u32[]{:S(2)}) async-start(f32[8,1,2048]{2,1,0:T(1,128)} %reshape.886), calls=%async_computation.7 | async-start | bytes 131072 | tf_op jit(solution)/shard_map/all_to_all | solution.py:182
  263.5 81.0 %reduce-scatter.9.cloned.1.call-start = ((), (), s32[]{:S(2)}) async-start(), calls=%async_computation.17 | async-start | bytes 589824 | tf_op jit(solution)/shard_map/reduce_scatter | solution.py:214
  295.3 1.6 copy-start.12
  296.9 0.7 copy-start.11
  298.5 1.6 copy-start.12
  301.6 1.6 copy-start.12
  303.3 0.7 copy-start.11
  304.8 1.6 copy-start.12
  315.4 61.6 %all-reduce.10.cloned.1.call-start = ((), (), s32[]{:S(2)}) async-start(), calls=%async_computation.18 | async-start | bytes 131072 | tf_op jit(solution)/shard_map/psum | solution.py:225
  377.0 1.4 copy-start.16
  378.0 1.0 copy-start.6
  378.4 1.1 copy-start.3
  384.4 10.6 %all-to-all-start.7 = ((f32[8,1,2048]{2,1,0:T(1,128)}), f32[8,1,2048]{2,1,0:T(1,128)}, u32[]{:S(2)}, u32[]{:S(2)}) async-start(f32[8,1,2048]{2,1,0:T(1,128)} %reshape.890), calls=%async_computation.10 | async-start | bytes 131072 | tf_op jit(solution)/shard_map/all_to_all | solution.py:182
  389.0 81.0 %reduce-scatter.11.cloned.1.call-start = ((), (), s32[]{:S(2)}) async-start(), calls=%async_computation.19 | async-start | bytes 589824 | tf_op jit(solution)/shard_map/reduce_scatter | solution.py:214
  419.3 0.7 copy-start.7
  420.9 1.6 copy-start.8
  422.5 0.7 copy-start.7
  424.0 1.6 copy-start.8
  425.7 0.7 copy-start.7
  427.2 1.6 copy-start.8
  428.9 0.7 copy-start.7
  430.4 1.6 copy-start.8
  441.0 61.5 %all-reduce.12.cloned.1.call-start = ((), (), s32[]{:S(2)}) async-start(), calls=%async_computation.20 | async-start | bytes 131072 | tf_op jit(solution)/shard_map/psum | solution.py:225
  (20 other events, 13.5 us)
Sparse Core Ops, SparseCore 0:
  55.3 29.5 reduce-scatter.4
  106.6 19.3 all-reduce.5
  189.9 28.8 reduce-scatter.6
  231.9 19.5 all-reduce.7
  315.5 28.9 reduce-scatter.8
  357.6 19.3 all-reduce.9
  441.1 28.8 reduce-scatter.10
  483.1 19.3 all-reduce.11
where the time goes:
time: 516 us; the launch traced here: 512 us
  waiting for transfers between devices  215 us (42%)
  blocking collectives  78.2 us (15%)
  local copies, waits for them, and re-layouts  69.4 us (13%)
  matrix products  62 us (12%)
  other arithmetic  46.1 us (9%)
  starting transfers between devices  26.2 us (5%)
  between operations  15.1 us (3%)
    reduce_scatter x4, waiting for transfers between devices, local(): lax.psum_scatter(grid_term(jnp.int32(0), row_count * lax.axis_size(('tile...  111 us
    psum x4, waiting for transfers between devices, local(): gradient = lax.psum(conj_mul(coil_sens, coil_back), 'coil')  77.4 us
    all_gather x3, blocking collectives, local(): piece = lax.all_gather(kspace, ('tile', 'spk'), axis=0, tiled=True)  42.6 us
    dot_general x16, matrix products, grid_one_spoke(): jnp.dot(smeared.reshape(piece_rows * 2, RO), row_one, preferred_element_t...  29.2 us
    all_to_all x3, blocking collectives, local(): lax.all_to_all(partial_back, ('tile', 'spk'), split_axis=2, concat_axis=0...  24.9 us
    unnamed x82, local copies, waits for them, and re-layouts  24.4 us
    all_to_all x3, waiting for transfers between devices, local(): lax.all_to_all(half_done, ('tile', 'spk'), split_axis=2, concat_axis=0, t...  17.1 us
    dynamic_update_slice x12, other arithmetic, fold_one_spoke(): lax.dynamic_update_index_in_dim(partial_value, current + added, spoke_ind...  15.1 us
  transfers between devices with their start and end apart: 14, of which 13 were waited for; matrix products, arithmetic and copies ran while one was open for 3% of the time, Pallas kernels for 0%

commit v1 on v0

v1 whole, which is shorter than its diff:
```python
import functools
import math

import jax
import jax.numpy as jnp
import numpy as np
from jax import lax
from jax.experimental import pallas as pl
from jax.experimental.pallas import tpu as pltpu
from jax.sharding import PartitionSpec as P

LEVELS = 3
ITERS = 4
STEP_SIZE = 0.5
GROUP = 4
F32 = jnp.float32
BF16 = jnp.bfloat16


def split_host(table):
    high = table.astype(BF16)
    low = (table - high.astype(np.float64)).astype(BF16)
    return high, low


def dft_tables(n):
    idx = np.arange(n)
    angles = 2.0 * math.pi / n * (np.outer(idx, idx) % n)
    scale = 1.0 / math.sqrt(n)
    parts = [np.cos(angles) * scale, np.sin(angles) * scale, -np.sin(angles) * scale]
    pairs = [split_host(part) for part in parts]
    return np.stack([pair[0] for pair in pairs] + [pair[1] for pair in pairs])


def haar_signs(n):
    mat = np.eye(n)
    for level in range(LEVELS):
        span, half = n >> level, n >> (level + 1)
        step = np.eye(n)
        step[:span] = 0.0
        for i in range(half):
            step[i, 2 * i] = step[i, 2 * i + 1] = 1.0
            step[half + i, 2 * i], step[half + i, 2 * i + 1] = 1.0, -1.0
        mat = step @ mat
    return mat


def haar_tables(n):
    col = haar_signs(n)
    row = np.kron(np.eye(n // 2**LEVELS), haar_signs(2**LEVELS))
    return np.stack([col, col.T, row.T, row]).astype(BF16)


def split2(x):
    high = x.astype(BF16)
    return high, (x - high.astype(F32)).astype(BF16)


def split3(x):
    high = x.astype(BF16)
    rest = x - high.astype(F32)
    mid = rest.astype(BF16)
    return high, mid, (rest - mid.astype(F32)).astype(BF16)


def mm(a, b):
    return jnp.dot(a, b, preferred_element_type=F32)


def right_dft(re, im, dft, sign):
    top = jnp.concatenate([re, sign * im], axis=1)
    bottom = jnp.concatenate([im, -sign * re], axis=1)
    high, low = split2(jnp.concatenate([top, bottom], axis=0))
    t_high = jnp.concatenate([dft[0], dft[1]], axis=0)
    t_low = jnp.concatenate([dft[3], dft[4]], axis=0)
    return mm(high, t_high) + mm(low, t_high) + mm(high, t_low)


def left_dft(stacked, dft, sign):
    plus, minus = (1, 2) if sign > 0 else (2, 1)
    high, low = split2(stacked)

    def table(base):
        top = jnp.concatenate([dft[base], dft[base + plus]], axis=1)
        bottom = jnp.concatenate([dft[base + minus], dft[base]], axis=1)
        return jnp.concatenate([top, bottom], axis=0)

    t_high, t_low = table(0), table(3)
    return mm(t_high, high) + mm(t_high, low) + mm(t_low, high)


def labels(positions, length):
    out = jnp.ones(positions.shape, F32)
    for level in range(1, LEVELS + 1):
        out = out + jnp.where(positions < length >> level, 1.0, 0.0)
    return out


def exact_left(signs, parts):
    return sum(mm(signs, part) for part in parts)


def exact_right(parts, signs):
    return sum(mm(part, signs) for part in parts)


def shrink(re, im, thr_ref, haar, last_rows=None):
    n = re.shape[0]
    block = 2**LEVELS
    col_pos = lax.broadcasted_iota(jnp.int32, (n, 1), 0)
    row_pos = lax.broadcasted_iota(jnp.int32, (1, n), 1) % block
    col_label, row_label = labels(col_pos, n), labels(row_pos, block)
    col_scale = jnp.exp2(-0.5 * jnp.minimum(col_label, LEVELS))
    row_scale = jnp.exp2(-0.5 * jnp.minimum(row_label, LEVELS))
    band = jnp.minimum(col_label, row_label)
    limits = jnp.full((n, n), 1.0, F32)
    for level in range(LEVELS):
        limits = jnp.where(band == level + 1, thr_ref[level], limits)
    scale = col_scale * row_scale
    coeffs = []
    for part in (re, im):
        half = exact_left(haar[0], split3(part))
        coeffs.append(exact_right(split3(half), haar[2]) * scale)
    magnitude = jnp.sqrt(coeffs[0] * coeffs[0] + coeffs[1] * coeffs[1])
    factor = jnp.maximum(magnitude - limits, 0.0) / jnp.maximum(magnitude, limits)
    factor = jnp.where(band <= LEVELS, factor, 1.0) * scale
    out = []
    for part in coeffs:
        half = exact_left(haar[1], split3(part * factor))
        if last_rows is None:
            out.append(exact_right(split3(half), haar[3]))
        else:
            out.append(
                sum(
                    lax.dot_general(last_rows, p, (((1,), (1,)), ((), ())), preferred_element_type=F32)
                    for p in split3(half)
                )
            )
    return out


def density_of(ro, n, live_total):
    lane = lax.broadcasted_iota(jnp.int32, (1, ro), 1)
    offset = jnp.abs(lane - ro // 2).astype(F32)
    return (offset + 0.5) * (n / (3.0 * ro * live_total))


def smear(col_table, weighted):
    col = col_table.astype(F32)
    both = [(col * weighted[p : p + 1]).astype(BF16) for p in range(2)]
    return jnp.concatenate(both, axis=0)


def grid_dot(smeared, row_table):
    return lax.dot_general(smeared, row_table, (((1,), (1,)), ((), ())), preferred_element_type=F32)


def adjoint(gridded, dft):
    half = left_dft(gridded, dft, -1)
    n = gridded.shape[0] // 2
    return right_dft(half[:n], half[n:], dft, -1)


def first_kernel(share, first_of, places_of, live_total, pieces, n, *refs):
    piece_refs, refs = refs[:pieces], refs[pieces:]
    dft_ref, row_out, col_out, data_out, back_out = refs[:5]
    slots, rows_s, cols_s, grid_s, list_s, row_sem, col_sem = refs[5:]
    spk_dev, fields, ro = piece_refs[0].shape
    groups = share // GROUP
    for piece, place in zip(piece_refs, places_of(), strict=True):
        slots[pl.ds(place * spk_dev, spk_dev), 0:fields, :] = piece[...].astype(F32)
    taken = jnp.int32(0)
    for block in range(pieces):
        count = jnp.max(slots[block * spk_dev, fields - 1 : fields, :]).astype(jnp.int32)
        for depth in range(spk_dev):
            list_s[taken] = block * spk_dev + depth
            taken = taken + (depth < count).astype(jnp.int32)
    start = first_of()
    density = density_of(ro, n, live_total)
    cells = lax.broadcasted_iota(jnp.int32, (n, ro), 0).astype(F32)
    grid_s[...] = jnp.zeros_like(grid_s)

    def table(at, weights):
        before = jnp.where(at == 0, n - 1.0, at - 1)
        after = jnp.where(at == n - 1, 0.0, at + 1)
        out = jnp.where(cells == after, weights[2:3], 0.0)
        out = jnp.where(cells == at, weights[1:2], out)
        return jnp.where(cells == before, weights[0:1], out).astype(BF16)

    def group_step(group, carry):
        smeared = []
        for j in range(GROUP):
            slot = slots[list_s[start + group * GROUP + j]]
            rows_s[group, :, j * ro : (j + 1) * ro] = table(slot[6:7], slot[0:3])
            col_table = table(slot[7:8], slot[3:6])
            cols_s[group, :, j * ro : (j + 1) * ro] = col_table
            data = slot[8:10]
            data_out[group * GROUP + j] = data
            smeared.append(smear(col_table, -density * data))
        grid_s[...] += grid_dot(jnp.concatenate(smeared, axis=1), rows_s[group])
        pltpu.make_async_copy(rows_s.at[group], row_out.at[group], row_sem.at[group]).start()
        pltpu.make_async_copy(cols_s.at[group], col_out.at[group], col_sem.at[group]).start()
        return carry

    lax.fori_loop(0, groups, group_step, 0)
    back_out[...] = adjoint(grid_s[...], dft_ref)

    def drain(group, carry):
        pltpu.make_async_copy(rows_s.at[group], row_out.at[group], row_sem.at[group]).wait()
        pltpu.make_async_copy(cols_s.at[group], col_out.at[group], col_sem.at[group]).wait()
        return carry

    lax.fori_loop(0, groups, drain, 0)


def step_kernel(share, live_total, n_parts, *refs):
    thr_ref, est_ref, part_refs, refs = refs[0], refs[1], refs[2 : 2 + n_parts], refs[2 + n_parts :]
    map_ref, data_ref, dft_ref, haar_ref, row_hbm, col_hbm, est_out, part_out = refs[:8]
    rows_s, cols_s, weighted_s, grid_s, row_sem, col_sem = refs[8:]
    groups = share // GROUP
    n = map_ref.shape[1]
    ro = data_ref.shape[-1]

    def copies(group):
        return (
            pltpu.make_async_copy(row_hbm.at[group], rows_s.at[group], row_sem.at[group]),
            pltpu.make_async_copy(col_hbm.at[group], cols_s.at[group], col_sem.at[group]),
        )

    for group in range(groups):
        for copy in copies(group):
            copy.start()
    target = []
    for p in range(2):
        gradient = sum(part[p] for part in part_refs)
        target.append(est_ref[p] - STEP_SIZE * gradient)
    re, im = shrink(target[0], target[1], thr_ref, haar_ref)
    est_out[0] = re
    est_out[1] = im
    mre, mim = map_ref[0], map_ref[1]
    half = right_dft(mre * re - mim * im, mre * im + mim * re, dft_ref, 1)
    kspace = left_dft(half, dft_ref, 1).astype(BF16)
    density = density_of(ro, n, live_total)
    grid_s[...] = jnp.zeros_like(grid_s)

    def sample_group(group, carry):
        for copy in copies(group):
            copy.wait()
        for j in range(GROUP):
            inner = mm(kspace, rows_s[group, :, j * ro : (j + 1) * ro])
            col = cols_s[group, :, j * ro : (j + 1) * ro].astype(F32)
            data = data_ref[group * GROUP + j]
            model = [jnp.sum(inner[p * n : (p + 1) * n] * col, axis=0, keepdims=True) for p in range(2)]
            weighted_s[group * GROUP + j] = density * (jnp.concatenate(model, axis=0) - data)
        return carry

    lax.fori_loop(0, groups, sample_group, 0)

    def grid_group(group, carry):
        smeared = [
            smear(cols_s[group, :, j * ro : (j + 1) * ro], weighted_s[group * GROUP + j]) for j in range(GROUP)
        ]
        grid_s[...] += grid_dot(jnp.concatenate(smeared, axis=1), rows_s[group])
        return carry

    lax.fori_loop(0, groups, grid_group, 0)
    back = adjoint(grid_s[...], dft_ref)
    conj_map(map_ref[0], map_ref[1], back, part_out)


def conj_map(mre, mim, back, part_out):
    n = mre.shape[0]
    bre, bim = back[:n], back[n:]
    part_out[0] = mre * bre + mim * bim
    part_out[1] = mre * bim - mim * bre


def map_kernel(places_of, pieces, *refs):
    piece_refs, (back_ref, map_out, part_out, full) = refs[:pieces], refs[pieces:]
    rows = piece_refs[0].shape[0]
    for piece, place in zip(piece_refs, places_of(), strict=True):
        for p in range(2):
            full[p, pl.ds(place * rows, rows), :] = piece[:, p, :]
    for p in range(2):
        map_out[p] = full[p].T
    conj_map(map_out[0], map_out[1], back_ref[...], part_out)


def last_kernel(n_parts, rows, mine_of, thr_ref, est_ref, *refs):
    part_refs, (haar_ref, out_ref) = refs[:n_parts], refs[n_parts:]
    n = est_ref.shape[1]
    target = []
    for p in range(2):
        gradient = sum(part[p] for part in part_refs)
        target.append(est_ref[p] - STEP_SIZE * gradient)
    mine = mine_of()
    pick = lax.broadcasted_iota(jnp.int32, (rows, n), 1) == (
        lax.broadcasted_iota(jnp.int32, (rows, n), 0) + mine * rows
    )
    own = mm(jnp.where(pick, 1.0, 0.0).astype(BF16), haar_ref[2]).astype(BF16)
    re, im = shrink(target[0], target[1], thr_ref, haar_ref, own)
    out_ref[:, 0, :] = re
    out_ref[:, 1, :] = im


def local(coil_maps, kspace_data, interp_weights, sample_bins, spoke_count, thresholds):
    n_tile, n_coil, n_spk = (lax.axis_size(name) for name in ("tile", "coil", "spk"))
    blocks = n_tile * n_spk
    rows, _, n = coil_maps.shape[1:]
    spk_dev, ro = sample_bins.shape
    live_total = blocks * spk_dev // 2
    own_map = coil_maps[0]
    by_core = n_coil == n_spk == 2
    cells = jnp.stack([sample_bins // n, sample_bins % n], axis=1).astype(BF16)
    count = jnp.broadcast_to(spoke_count.astype(BF16)[:, None, None], (spk_dev, 1, ro))
    bundle = jnp.concatenate([interp_weights, cells, kspace_data[0], count], axis=1)

    if by_core:
        onto = [(0, 2), (3, 1), (1, 0), (2, 3)]
        across = [(1, 2), (2, 1)]
        is_own = lax.axis_index("coil") == lax.axis_index("spk")

        def collect(value):
            near = lax.ppermute(value, ("coil", "spk"), onto)
            far = lax.ppermute(value, ("coil", "spk"), across)
            return [jnp.where(is_own, value, far), near]

        def spread(values):
            out = list(values)
            for shift in range(1, n_tile):
                out += [lax.ppermute(v, "tile", [(i, (i + shift) % n_tile) for i in range(n_tile)]) for v in values]
            return out

        def places_of():
            tile, coil = lax.axis_index("tile"), lax.axis_index("coil")
            sent = [(tile - shift + n_tile) % n_tile for shift in range(n_tile)]
            return [at * 2 + block for at in sent for block in (coil, 1 - coil)]

        spokes = spread(collect(bundle))
        maps = spread(collect(own_map))
        share, first_of = live_total, lambda: jnp.int32(0)

        def parts_of(part):
            return [part, lax.ppermute(part, "spk", [(0, 1), (1, 0)])]
    else:
        spokes = list(lax.all_gather(bundle, ("tile", "spk"), axis=0, tiled=False))
        maps = list(lax.all_gather(own_map, ("tile", "spk"), axis=0, tiled=False))
        places_of = lambda: list(range(blocks))
        share = live_total // blocks
        first_of = lambda: (lax.axis_index("tile") * n_spk + lax.axis_index("spk")) * share

        def parts_of(part):
            return [lax.psum(part, ("tile", "coil", "spk"))]

    groups = share // GROUP
    dft = jnp.asarray(dft_tables(n))
    haar = jnp.asarray(haar_tables(n))
    tables = jax.ShapeDtypeStruct((groups, n, GROUP * ro), BF16)
    image = jax.ShapeDtypeStruct((2, n, n), F32)
    vmem = pl.BlockSpec(memory_space=pltpu.VMEM)
    smem = pl.BlockSpec(memory_space=pltpu.SMEM)
    hbm = pl.BlockSpec(memory_space=pl.ANY)
    table_scratch = [pltpu.VMEM(tables.shape, BF16)] * 2
    sems = [pltpu.SemaphoreType.DMA((groups,))] * 2
    row_tab, col_tab, data, back = pl.pallas_call(
        functools.partial(first_kernel, share, first_of, places_of, live_total, blocks, n),
        out_shape=[tables, tables, jax.ShapeDtypeStruct((share, 2, ro), F32), jax.ShapeDtypeStruct((2 * n, n), F32)],
        in_specs=[vmem] * (blocks + 1),
        out_specs=[hbm, hbm, vmem, vmem],
        scratch_shapes=[
            pltpu.VMEM((blocks * spk_dev, 16, ro), F32),
            *table_scratch,
            pltpu.VMEM((2 * n, n), F32),
            pltpu.SMEM((blocks * spk_dev + 1,), jnp.int32),
            *sems,
        ],
    )(*spokes, dft)
    map_t, part = pl.pallas_call(
        functools.partial(map_kernel, places_of, blocks),
        out_shape=[image, image],
        in_specs=[vmem] * (blocks + 1),
        out_specs=[vmem, vmem],
        scratch_shapes=[pltpu.VMEM((2, n, n), F32)],
    )(*maps, back)
    estimate = jnp.zeros((2, n, n), F32)
    parts = parts_of(part)
    for _ in range(1, ITERS):
        estimate, part = pl.pallas_call(
            functools.partial(step_kernel, share, live_total, len(parts)),
            out_shape=[image, image],
            in_specs=[smem] + [vmem] * (len(parts) + 5) + [hbm, hbm],
            out_specs=[vmem, vmem],
            scratch_shapes=[
                *table_scratch,
                pltpu.VMEM((share, 2, ro), F32),
                pltpu.VMEM((2 * n, n), F32),
                *sems,
            ],
        )(thresholds, estimate, *parts, map_t, data, dft, haar, row_tab, col_tab)
        parts = parts_of(part)
    mine_of = lambda: lax.axis_index("tile") * n_spk + lax.axis_index("spk")
    return pl.pallas_call(
        functools.partial(last_kernel, len(parts), rows, mine_of),
        out_shape=jax.ShapeDtypeStruct((rows, 2, n), F32),
        in_specs=[smem] + [vmem] * (len(parts) + 2),
        out_specs=vmem,
    )(thresholds, estimate, *parts, haar)


def solution(mesh):
    placed = (
        P("coil", ("grp", "tile", "spk"), None, None),
        P("coil", ("grp", "tile", "spk"), None, None),
        P(("grp", "tile", "spk"), None, None),
        P(("grp", "tile", "spk"), None),
        P(("grp", "tile", "spk")),
        P(),
    )
    return jax.shard_map(
        local,
        mesh=mesh,
        in_specs=placed,
        out_specs=P(("grp", "tile", "spk"), None, None),
        check_vma=False,
    )
```

time: 516 us -> 112 us (0.22)
  waiting for transfers between devices: 215 us -> 9.33 us
  blocking collectives: 78.2 us -> 0 us
  Pallas kernels: 0 us -> 65.8 us
  local copies, waits for them, and re-layouts: 69.4 us -> 5.62 us
  matrix products: 62 us -> 0 us
  other arithmetic: 46.1 us -> 1.59 us
  between operations: 15.1 us -> 0.96 us
    reduce_scatter x4 -> x0, waiting for transfers between devices: 111 us -> none  [local(): lax.psum_scatter(grid_term(jnp.int32(0), row_count * lax.axis_size(('tile...]
    psum x4 -> x0, waiting for transfers between devices: 77.4 us -> none  [local(): gradient = lax.psum(conj_mul(coil_sens, coil_back), 'coil')]
    pallas_call x0 -> x6, Pallas kernels: none -> 65.8 us  [the longest x3 47.7 us: local(): pl.pallas_call(functools.partial(step_kernel, share, live_total, len(part...]
    dot_general x64 -> x0, matrix products: 62 us -> none  [the longest x16 29.2 us: grid_one_spoke(): jnp.dot(smeared.reshape(piece_rows * 2, RO), row_one, preferred_element_t...]
    all_gather x3 -> x0, blocking collectives: 42.6 us -> none  [local(): piece = lax.all_gather(kspace, ('tile', 'spk'), axis=0, tiled=True)]
    ppermute x0 -> x20, starting transfers between devices: none -> 27.9 us  [the longest x12 21.8 us: spread(): lax.ppermute(v, 'tile', [(i, (i + shift) % n_tile) for i in range(n_tile)])]
    all_to_all x6 -> x0, waiting for transfers between devices: 26 us -> none  [the longest x3 17.1 us: local(): lax.all_to_all(half_done, ('tile', 'spk'), split_axis=2, concat_axis=0, t...]
    all_to_all x6 -> x0, starting transfers between devices: 25.5 us -> none  [the longest x3 13.8 us: local(): lax.all_to_all(half_done, ('tile', 'spk'), split_axis=2, concat_axis=0, t...]
  transfers between devices with their start and end apart: 14 -> 20, of which waited for: 13 -> 5; matrix products, arithmetic and copies ran while one was open for 3% -> 1% of each run, Pallas kernels for 0% -> 10%
where the time goes in v1:
time: 112 us; the launch traced here: 111 us
  Pallas kernels  65.8 us (59%)
  starting transfers between devices  27.9 us (25%)
  waiting for transfers between devices  9.33 us (8%)
  local copies, waits for them, and re-layouts  5.62 us (5%)
  other arithmetic  1.59 us (1%)
    pallas_call x3, Pallas kernels, local(): pl.pallas_call(functools.partial(step_kernel, share, live_total, len(part...  47.7 us
    ppermute x12, starting transfers between devices, spread(): lax.ppermute(v, 'tile', [(i, (i + shift) % n_tile) for i in range(n_tile)])  21.8 us
    pallas_call x1, Pallas kernels, local(): pl.pallas_call(functools.partial(first_kernel, share, first_of, places_of...  11.2 us
    ppermute x4, waiting for transfers between devices, parts_of(): return [part, lax.ppermute(part, 'spk', [(0, 1), (1, 0)])]  8.11 us
    ppermute x2, starting transfers between devices, collect(): near = lax.ppermute(value, ('coil', 'spk'), onto)  4.28 us
    pallas_call x1, Pallas kernels, local(): pl.pallas_call(functools.partial(last_kernel, len(parts), rows, mine_of),...  4.26 us
    unnamed x41, local copies, waits for them, and re-layouts  3.91 us
    pallas_call x1, Pallas kernels, local(): pl.pallas_call(functools.partial(map_kernel, places_of, blocks), out_shap...  2.68 us
  transfers between devices with their start and end apart: 20, of which 5 were waited for; matrix products, arithmetic and copies ran while one was open for 1% of the time, Pallas kernels for 10%

profile of v1, /device:TPU:0, one launch (start us, length us, event | category | flops | bytes accessed | tf_op | source)
XLA Modules:
  0.0 111.2 jit_solution(5797446766663447236)
XLA Ops:
  0.7 0.7 fusion.4
  1.4 0.7 copy.13
  2.2 0.8 concatenate.4
  2.9 3.0 %collective-permute-start.9 = (bf16[8,11,256]{2,1,0:T(8,128)(2,1)S(1)}, bf16[8,11,256]{2,1,0:T(8,128)(2,1)S(1)}, u32[]{:S(2)}, u32[]{:S(2)}) collective-permute-start(bf16[8,11,256]{2,1,0:T(8,128)(2,1)S(1)} %concatenate.4), channel_id=1, source_target_pairs={{0,2},{3,1},{1,0},{2,3},{4,6},{7,5},{5,4},{6,7},{8,10},{11,9},{9,8... | collective-permute-start | bytes 135176 | tf_op jit(solution)/shard_map/ppermute | solution.py:324
  5.9 0.7 collective-permute-start.8
  6.6 1.3 %collective-permute-start.1 = (f32[32,2,256]{2,1,0:T(2,128)}, f32[32,2,256]{2,1,0:T(2,128)S(1)}, u32[]{:S(2)}, u32[]{:S(2)}) collective-permute-start(f32[32,2,256]{2,1,0:T(2,128)} %bitcast.8), channel_id=1, source_target_pairs={{0,2},{3,1},{1,0},{2,3},{4,6},{7,5},{5,4},{6,7},{8,10},{11,9},{9,8... | collective-permute-start | bytes 196616 | tf_op jit(solution)/shard_map/ppermute | solution.py:324
  7.9 0.7 collective-permute-start
  8.6 4.3 %collective-permute-start.15 = (bf16[8,11,256]{2,1,0:T(8,128)(2,1)S(1)}, bf16[8,11,256]{2,1,0:T(8,128)(2,1)S(1)}, u32[]{:S(2)}, u32[]{:S(2)}) collective-permute-start(bf16[8,11,256]{2,1,0:T(8,128)(2,1)S(1)} %collective-permute-done.9.refs_1_), channel_id=1, source_target_pairs={{0,12},{4,0},{8,4},{12,8},{1,13},{5,1},{9,5},{13,9},{2,14},{6,2},{... | collective-permute-start | bytes 135176 | tf_op jit(solution)/shard_map/ppermute | solution.py:331
  12.8 0.0 collective-permute-start.13
  12.8 0.0 collective-permute-done.8
  12.9 0.5 collective-permute-start.14
  13.4 0.0 collective-permute-done.1.refs_1_
  13.4 2.6 %collective-permute-start.12 = (bf16[8,11,256]{2,1,0:T(8,128)(2,1)S(1)}, bf16[8,11,256]{2,1,0:T(8,128)(2,1)S(1)}, u32[]{:S(2)}, u32[]{:S(2)}) collective-permute-start(bf16[8,11,256]{2,1,0:T(8,128)(2,1)S(1)} %broadcast_select_fusion.refs_0_), channel_id=1, source_target_pairs={{0,8},{4,12},{8,0},{12,4},{1,9},{5,13},{9,1},{13,5},{2,10},{6,14},... | collective-permute-start | bytes 135176 | tf_op jit(solution)/shard_map/ppermute | solution.py:331
  15.9 0.0 collective-permute-done
  15.9 1.9 %collective-permute-start.10 = (bf16[8,11,256]{2,1,0:T(8,128)(2,1)S(1)}, bf16[8,11,256]{2,1,0:T(8,128)(2,1)S(1)}, u32[]{:S(2)}, u32[]{:S(2)}) collective-permute-start(bf16[8,11,256]{2,1,0:T(8,128)(2,1)S(1)} %broadcast_select_fusion.refs_0_), channel_id=1, source_target_pairs={{0,4},{4,8},{8,12},{12,0},{1,5},{5,9},{9,13},{13,1},{2,6},{6,10},{... | collective-permute-start | bytes 135176 | tf_op jit(solution)/shard_map/ppermute | solution.py:331
  17.9 0.1 collective-permute-start.11
  17.9 1.2 %collective-permute-done.13.refs_5_ = bf16[8,11,256]{2,1,0:T(8,128)(2,1)S(1)} collective-permute-done((bf16[8,11,256]{2,1,0:T(8,128)(2,1)S(1)}, bf16[8,11,256]{2,1,0:T(8,128)(2,1)S(1)}, u32[]{:S(2)}, u32[]{:S(2)}) %collective-permute-start.13) | collective-permute-done | bytes 45088 | tf_op jit(solution)/shard_map/ppermute | solution.py:331
  19.1 5.6 %collective-permute-start.7 = (f32[32,2,256]{2,1,0:T(2,128)S(1)}, f32[32,2,256]{2,1,0:T(2,128)S(1)}, u32[]{:S(2)}, u32[]{:S(2)}) collective-permute-start(f32[32,2,256]{2,1,0:T(2,128)S(1)} %collective-permute-done.1.refs_1_), channel_id=1, source_target_pairs={{0,12},{4,0},{8,4},{12,8},{1,13},{5,1},{9,5},{13,9},{2,14},{6,2},{... | collective-permute-start | bytes 196616 | tf_op jit(solution)/shard_map/ppermute | solution.py:331
  24.7 0.9 broadcast_select_fusion.1.refs_0_
  25.6 0.0 copy-start.5
  25.6 1.4 %collective-permute-start.6 = (f32[32,2,256]{2,1,0:T(2,128)S(1)}, f32[32,2,256]{2,1,0:T(2,128)S(1)}, u32[]{:S(2)}, u32[]{:S(2)}) collective-permute-start(f32[32,2,256]{2,1,0:T(2,128)S(1)} %broadcast_select_fusion.1.refs_0_), channel_id=1, source_target_pairs={{0,12},{4,0},{8,4},{12,8},{1,13},{5,1},{9,5},{13,9},{2,14},{6,2},{... | collective-permute-start | bytes 196616 | tf_op jit(solution)/shard_map/ppermute | solution.py:331
  27.0 1.1 collective-permute-start.5
  28.1 1.9 %collective-permute-start.3 = (f32[32,2,256]{2,1,0:T(2,128)S(1)}, f32[32,2,256]{2,1,0:T(2,128)S(1)}, u32[]{:S(2)}, u32[]{:S(2)}) collective-permute-start(f32[32,2,256]{2,1,0:T(2,128)S(1)} %collective-permute-done.1.refs_1_), channel_id=1, source_target_pairs={{0,4},{4,8},{8,12},{12,0},{1,5},{5,9},{9,13},{13,1},{2,6},{6,10},{... | collective-permute-start | bytes 196616 | tf_op jit(solution)/shard_map/ppermute | solution.py:331
  30.0 0.6 collective-permute-start.4
  30.7 1.8 %collective-permute-start.2 = (f32[32,2,256]{2,1,0:T(2,128)S(1)}, f32[32,2,256]{2,1,0:T(2,128)S(1)}, u32[]{:S(2)}, u32[]{:S(2)}) collective-permute-start(f32[32,2,256]{2,1,0:T(2,128)S(1)} %broadcast_select_fusion.1.refs_0_), channel_id=1, source_target_pairs={{0,4},{4,8},{8,12},{12,0},{1,5},{5,9},{9,13},{13,1},{2,6},{6,10},{... | collective-permute-start | bytes 196616 | tf_op jit(solution)/shard_map/ppermute | solution.py:331
  32.5 11.2 %shard_map.82 = (bf16[8,256,1024]{2,1,0:T(8,128)(2,1)}, bf16[8,256,1024]{2,1,0:T(8,128)(2,1)}, f32[32,2,256]{2,1,0:T(2,128)}, f32[512,256]{1,0:T(8,128)}) custom-call(bf16[8,11,256]{2,1,0:T(8,128)(2,1)} %copy-done.4, bf16[8,11,256]{2,1,0:T(8,128)(2,1)} %copy-done.7, bf16[8,11,256]{2,1,0:T(8,128)(2,1)} %copy-done.13, bf16[8,11,256]{2,1,0:T(8,128)(2,1)} %copy-done.15, ...), custom_call_target="tpu_custom_call" | custom-call | tf_op jit(solution)/shard_map/pallas_call | solution.py:365
  43.8 0.5 copy-done.16
  44.3 0.0 copy-done.17
  44.3 0.0 copy-done.14
  44.4 0.0 copy-done.18
  44.4 0.0 copy-done.19
  44.4 2.7 %shard_map.83 = (f32[2,256,256]{2,1,0:T(8,128)}, f32[2,256,256]{2,1,0:T(8,128)}) custom-call(f32[32,2,256]{2,1,0:T(2,128)} %copy-done.5, f32[32,2,256]{2,1,0:T(2,128)} %copy-done.6, f32[32,2,256]{2,1,0:T(2,128)} %copy-done.19, f32[32,2,256]{2,1,0:T(2,128)} %copy-done.17, f32[32,2,256]{2,1,0:T(2,128)} %copy-done.18, f32[32,2,256]{2,1,0:T(2,128)} %copy-done.16, ...), custom_call_target="tpu_custom_call" | custom-call | tf_op jit(solution)/shard_map/pallas_call | solution.py:378
  47.1 2.1 %collective-permute-done.16.refs_3_ = f32[2,256,256]{2,1,0:T(8,128)S(1)} collective-permute-done((f32[2,256,256]{2,1,0:T(8,128)}, f32[2,256,256]{2,1,0:T(8,128)S(1)}, u32[]{:S(2)}, u32[]{:S(2)}) %collective-permute-start.16) | collective-permute-done | bytes 524320 | tf_op jit(solution)/shard_map/ppermute | solution.py:344
  49.2 0.9 broadcast_in_dim.11.refs_1_
  50.1 0.1 copy-done.1
  50.2 15.8 %shard_map.84 = (f32[2,256,256]{2,1,0:T(8,128)}, f32[2,256,256]{2,1,0:T(8,128)}) custom-call(f32[3]{0:T(128)} %thr_ref.1, f32[2,256,256]{2,1,0:T(8,128)} %broadcast_in_dim.11.refs_1_, f32[2,256,256]{2,1,0:T(8,128)} %get-tuple-element.18.refs_2_, f32[2,256,256]{2,1,0:T(8,128)} %copy-done.1, f32[2,256,256]{2,1,0:T(8,128)} %get-tuple-element.19.refs_4_, ...), custom_call_target="tpu_custom_call" | custom-call | tf_op jit(solution)/shard_map/pallas_call | solution.py:388
  66.1 0.2 collective-permute-start.17
  66.3 2.0 %collective-permute-done.17.refs_3_ = f32[2,256,256]{2,1,0:T(8,128)S(1)} collective-permute-done((f32[2,256,256]{2,1,0:T(8,128)}, f32[2,256,256]{2,1,0:T(8,128)S(1)}, u32[]{:S(2)}, u32[]{:S(2)}) %collective-permute-start.17) | collective-permute-done | bytes 524320 | tf_op jit(solution)/shard_map/ppermute | solution.py:344
  68.3 0.8 copy-done.2
  69.1 16.0 %shard_map.85 = (f32[2,256,256]{2,1,0:T(8,128)}, f32[2,256,256]{2,1,0:T(8,128)}) custom-call(f32[3]{0:T(128)} %thr_ref.1, f32[2,256,256]{2,1,0:T(8,128)} %get-tuple-element.23.refs_1_, f32[2,256,256]{2,1,0:T(8,128)} %get-tuple-element.24.refs_2_, f32[2,256,256]{2,1,0:T(8,128)} %copy-done.2, f32[2,256,256]{2,1,0:T(8,128)} %get-tuple-element.19.refs_4_, ...), custom_call_target="tpu_custom_call" | custom-call | tf_op jit(solution)/shard_map/pallas_call | solution.py:388
  85.1 0.2 collective-permute-start.18
  85.3 2.0 %collective-permute-done.18.refs_3_ = f32[2,256,256]{2,1,0:T(8,128)S(1)} collective-permute-done((f32[2,256,256]{2,1,0:T(8,128)}, f32[2,256,256]{2,1,0:T(8,128)S(1)}, u32[]{:S(2)}, u32[]{:S(2)}) %collective-permute-start.18) | collective-permute-done | bytes 524320 | tf_op jit(solution)/shard_map/ppermute | solution.py:344
  87.3 0.8 copy-done
  88.1 15.9 %shard_map.86 = (f32[2,256,256]{2,1,0:T(8,128)}, f32[2,256,256]{2,1,0:T(8,128)}) custom-call(f32[3]{0:T(128)} %thr_ref.1, f32[2,256,256]{2,1,0:T(8,128)} %get-tuple-element.25.refs_1_, f32[2,256,256]{2,1,0:T(8,128)} %get-tuple-element.26.refs_2_, f32[2,256,256]{2,1,0:T(8,128)} %copy-done, f32[2,256,256]{2,1,0:T(8,128)} %get-tuple-element.19.refs_4_, ...), custom_call_target="tpu_custom_call" | custom-call | tf_op jit(solution)/shard_map/pallas_call | solution.py:388
  103.9 0.2 collective-permute-start.19
  104.1 2.0 %collective-permute-done.19.refs_1_ = f32[2,256,256]{2,1,0:T(8,128)S(1)} collective-permute-done((f32[2,256,256]{2,1,0:T(8,128)}, f32[2,256,256]{2,1,0:T(8,128)S(1)}, u32[]{:S(2)}, u32[]{:S(2)}) %collective-permute-start.19) | collective-permute-done | bytes 524320 | tf_op jit(solution)/shard_map/ppermute | solution.py:344
  106.1 0.8 copy-done.3
  106.9 4.3 %shard_map.87 = f32[32,2,256]{2,1,0:T(2,128)} custom-call(f32[3]{0:T(128)} %thr_ref.1, f32[2,256,256]{2,1,0:T(8,128)} %get-tuple-element.27.est_ref, f32[2,256,256]{2,1,0:T(8,128)} %get-tuple-element.28.refs_0_, f32[2,256,256]{2,1,0:T(8,128)} %copy-done.3, bf16[4,256,256]{2,1,0:T(8,128)(2,1)} %constant.41.clone.refs_7_.refs_2_), custom_call_target="tpu_custom_call" | custom-call | tf_op jit(solution)/shard_map/pallas_call | solution.py:402
  (47 shorter events, 0.1 us)
Async XLA Ops:
  2.9 5.6 %collective-permute-start.9 = (bf16[8,11,256]{2,1,0:T(8,128)(2,1)S(1)}, bf16[8,11,256]{2,1,0:T(8,128)(2,1)S(1)}, u32[]{:S(2)}, u32[]{:S(2)}) collective-permute-start(bf16[8,11,256]{2,1,0:T(8,128)(2,1)S(1)} %concatenate.4), channel_id=1, source_target_pairs={{0,2},{3,1},{1,0},{2,3},{4,6},{7,5},{5,4},{6,7},{8,10},{11,9},{9,8... | collective-permute-start | bytes 135176 | tf_op jit(solution)/shard_map/ppermute | solution.py:324
  5.9 6.9 %collective-permute-start.8 = (bf16[8,11,256]{2,1,0:T(8,128)(2,1)S(1)}, bf16[8,11,256]{2,1,0:T(8,128)(2,1)S(1)}, u32[]{:S(2)}, u32[]{:S(2)}) collective-permute-start(bf16[8,11,256]{2,1,0:T(8,128)(2,1)S(1)} %concatenate.4), channel_id=1, source_target_pairs={{1,2},{2,1},{5,6},{6,5},{9,10},{10,9},{13,14},{14,13},{17,18},{18,... | collective-permute-start | bytes 135176 | tf_op jit(solution)/shard_map/ppermute | solution.py:325
  6.6 6.8 %collective-permute-start.1 = (f32[32,2,256]{2,1,0:T(2,128)}, f32[32,2,256]{2,1,0:T(2,128)S(1)}, u32[]{:S(2)}, u32[]{:S(2)}) collective-permute-start(f32[32,2,256]{2,1,0:T(2,128)} %bitcast.8), channel_id=1, source_target_pairs={{0,2},{3,1},{1,0},{2,3},{4,6},{7,5},{5,4},{6,7},{8,10},{11,9},{9,8... | collective-permute-start | bytes 196616 | tf_op jit(solution)/shard_map/ppermute | solution.py:324
  7.9 8.1 %collective-permute-start = (f32[32,2,256]{2,1,0:T(2,128)}, f32[32,2,256]{2,1,0:T(2,128)S(1)}, u32[]{:S(2)}, u32[]{:S(2)}) collective-permute-start(f32[32,2,256]{2,1,0:T(2,128)} %bitcast.9), channel_id=1, source_target_pairs={{1,2},{2,1},{5,6},{6,5},{9,10},{10,9},{13,14},{14,13},{17,18},{18,... | collective-permute-start | bytes 196616 | tf_op jit(solution)/shard_map/ppermute | solution.py:325
  8.5 23.9 %copy-start.7 = (bf16[8,11,256]{2,1,0:T(8,128)(2,1)}, bf16[8,11,256]{2,1,0:T(8,128)(2,1)S(1)}, u32[]{:S(2)}) copy-start(bf16[8,11,256]{2,1,0:T(8,128)(2,1)S(1)} %collective-permute-done.9.refs_1_) | copy-start | bytes 135172
  8.6 9.3 %collective-permute-start.15 = (bf16[8,11,256]{2,1,0:T(8,128)(2,1)S(1)}, bf16[8,11,256]{2,1,0:T(8,128)(2,1)S(1)}, u32[]{:S(2)}, u32[]{:S(2)}) collective-permute-start(bf16[8,11,256]{2,1,0:T(8,128)(2,1)S(1)} %collective-permute-done.9.refs_1_), channel_id=1, source_target_pairs={{0,12},{4,0},{8,4},{12,8},{1,13},{5,1},{9,5},{13,9},{2,14},{6,2},{... | collective-permute-start | bytes 135176 | tf_op jit(solution)/shard_map/ppermute | solution.py:331
  12.8 6.3 %collective-permute-start.13 = (bf16[8,11,256]{2,1,0:T(8,128)(2,1)S(1)}, bf16[8,11,256]{2,1,0:T(8,128)(2,1)S(1)}, u32[]{:S(2)}, u32[]{:S(2)}) collective-permute-start(bf16[8,11,256]{2,1,0:T(8,128)(2,1)S(1)} %collective-permute-done.9.refs_1_), channel_id=1, source_target_pairs={{0,8},{4,12},{8,0},{12,4},{1,9},{5,13},{9,1},{13,5},{2,10},{6,14},... | collective-permute-start | bytes 135176 | tf_op jit(solution)/shard_map/ppermute | solution.py:331
  12.8 19.6 %copy-start.4 = (bf16[8,11,256]{2,1,0:T(8,128)(2,1)}, bf16[8,11,256]{2,1,0:T(8,128)(2,1)S(1)}, u32[]{:S(2)}) copy-start(bf16[8,11,256]{2,1,0:T(8,128)(2,1)S(1)} %broadcast_select_fusion.refs_0_) | copy-start | bytes 135172
  12.9 14.1 %collective-permute-start.14 = (bf16[8,11,256]{2,1,0:T(8,128)(2,1)S(1)}, bf16[8,11,256]{2,1,0:T(8,128)(2,1)S(1)}, u32[]{:S(2)}, u32[]{:S(2)}) collective-permute-start(bf16[8,11,256]{2,1,0:T(8,128)(2,1)S(1)} %broadcast_select_fusion.refs_0_), channel_id=1, source_target_pairs={{0,12},{4,0},{8,4},{12,8},{1,13},{5,1},{9,5},{13,9},{2,14},{6,2},{... | collective-permute-start | bytes 135176 | tf_op jit(solution)/shard_map/ppermute | solution.py:331
  13.4 30.4 %copy-start.6 = (f32[32,2,256]{2,1,0:T(2,128)}, f32[32,2,256]{2,1,0:T(2,128)S(1)}, u32[]{:S(2)}) copy-start(f32[32,2,256]{2,1,0:T(2,128)S(1)} %collective-permute-done.1.refs_1_) | copy-start | bytes 196612
  13.4 14.7 %collective-permute-start.12 = (bf16[8,11,256]{2,1,0:T(8,128)(2,1)S(1)}, bf16[8,11,256]{2,1,0:T(8,128)(2,1)S(1)}, u32[]{:S(2)}, u32[]{:S(2)}) collective-permute-start(bf16[8,11,256]{2,1,0:T(8,128)(2,1)S(1)} %broadcast_select_fusion.refs_0_), channel_id=1, source_target_pairs={{0,8},{4,12},{8,0},{12,4},{1,9},{5,13},{9,1},{13,5},{2,10},{6,14},... | collective-permute-start | bytes 135176 | tf_op jit(solution)/shard_map/ppermute | solution.py:331
  15.9 14.1 %collective-permute-start.10 = (bf16[8,11,256]{2,1,0:T(8,128)(2,1)S(1)}, bf16[8,11,256]{2,1,0:T(8,128)(2,1)S(1)}, u32[]{:S(2)}, u32[]{:S(2)}) collective-permute-start(bf16[8,11,256]{2,1,0:T(8,128)(2,1)S(1)} %broadcast_select_fusion.refs_0_), channel_id=1, source_target_pairs={{0,4},{4,8},{8,12},{12,0},{1,5},{5,9},{9,13},{13,1},{2,6},{6,10},{... | collective-permute-start | bytes 135176 | tf_op jit(solution)/shard_map/ppermute | solution.py:331
  17.9 14.6 %copy-start.8 = (bf16[8,11,256]{2,1,0:T(8,128)(2,1)}, bf16[8,11,256]{2,1,0:T(8,128)(2,1)S(1)}, u32[]{:S(2)}) copy-start(bf16[8,11,256]{2,1,0:T(8,128)(2,1)S(1)} %collective-permute-done.15.refs_7_) | copy-start | bytes 135172
  17.9 7.7 %collective-permute-start.11 = (bf16[8,11,256]{2,1,0:T(8,128)(2,1)S(1)}, bf16[8,11,256]{2,1,0:T(8,128)(2,1)S(1)}, u32[]{:S(2)}, u32[]{:S(2)}) collective-permute-start(bf16[8,11,256]{2,1,0:T(8,128)(2,1)S(1)} %collective-permute-done.9.refs_1_), channel_id=1, source_target_pairs={{0,4},{4,8},{8,12},{12,0},{1,5},{5,9},{9,13},{13,1},{2,6},{6,10},{... | collective-permute-start | bytes 135176 | tf_op jit(solution)/shard_map/ppermute | solution.py:331
  19.1 13.4 %copy-start.9 = (bf16[8,11,256]{2,1,0:T(8,128)(2,1)}, bf16[8,11,256]{2,1,0:T(8,128)(2,1)S(1)}, u32[]{:S(2)}) copy-start(bf16[8,11,256]{2,1,0:T(8,128)(2,1)S(1)} %collective-permute-done.13.refs_5_) | copy-start | bytes 135172
  19.1 11.5 %collective-permute-start.7 = (f32[32,2,256]{2,1,0:T(2,128)S(1)}, f32[32,2,256]{2,1,0:T(2,128)S(1)}, u32[]{:S(2)}, u32[]{:S(2)}) collective-permute-start(f32[32,2,256]{2,1,0:T(2,128)S(1)} %collective-permute-done.1.refs_1_), channel_id=1, source_target_pairs={{0,12},{4,0},{8,4},{12,8},{1,13},{5,1},{9,5},{13,9},{2,14},{6,2},{... | collective-permute-start | bytes 196616 | tf_op jit(solution)/shard_map/ppermute | solution.py:331
  25.6 18.2 %copy-start.5 = (f32[32,2,256]{2,1,0:T(2,128)}, f32[32,2,256]{2,1,0:T(2,128)S(1)}, u32[]{:S(2)}) copy-start(f32[32,2,256]{2,1,0:T(2,128)S(1)} %broadcast_select_fusion.1.refs_0_) | copy-start | bytes 196612
  25.6 6.9 %copy-start.15 = (bf16[8,11,256]{2,1,0:T(8,128)(2,1)}, bf16[8,11,256]{2,1,0:T(8,128)(2,1)S(1)}, u32[]{:S(2)}) copy-start(bf16[8,11,256]{2,1,0:T(8,128)(2,1)S(1)} %collective-permute-done.11.refs_3_) | copy-start | bytes 135172
  25.6 18.1 %collective-permute-start.6 = (f32[32,2,256]{2,1,0:T(2,128)S(1)}, f32[32,2,256]{2,1,0:T(2,128)S(1)}, u32[]{:S(2)}, u32[]{:S(2)}) collective-permute-start(f32[32,2,256]{2,1,0:T(2,128)S(1)} %broadcast_select_fusion.1.refs_0_), channel_id=1, source_target_pairs={{0,12},{4,0},{8,4},{12,8},{1,13},{5,1},{9,5},{13,9},{2,14},{6,2},{... | collective-permute-start | bytes 196616 | tf_op jit(solution)/shard_map/ppermute | solution.py:331
  27.0 5.5 %copy-start.10 = (bf16[8,11,256]{2,1,0:T(8,128)(2,1)}, bf16[8,11,256]{2,1,0:T(8,128)(2,1)S(1)}, u32[]{:S(2)}) copy-start(bf16[8,11,256]{2,1,0:T(8,128)(2,1)S(1)} %collective-permute-done.14.refs_6_) | copy-start | bytes 135172
  27.0 16.7 %collective-permute-start.5 = (f32[32,2,256]{2,1,0:T(2,128)S(1)}, f32[32,2,256]{2,1,0:T(2,128)S(1)}, u32[]{:S(2)}, u32[]{:S(2)}) collective-permute-start(f32[32,2,256]{2,1,0:T(2,128)S(1)} %collective-permute-done.1.refs_1_), channel_id=1, source_target_pairs={{0,8},{4,12},{8,0},{12,4},{1,9},{5,13},{9,1},{13,5},{2,10},{6,14},... | collective-permute-start | bytes 196616 | tf_op jit(solution)/shard_map/ppermute | solution.py:331
  28.1 4.4 %copy-start.12 = (bf16[8,11,256]{2,1,0:T(8,128)(2,1)}, bf16[8,11,256]{2,1,0:T(8,128)(2,1)S(1)}, u32[]{:S(2)}) copy-start(bf16[8,11,256]{2,1,0:T(8,128)(2,1)S(1)} %collective-permute-done.12.refs_4_) | copy-start | bytes 135172
  28.1 15.6 %collective-permute-start.3 = (f32[32,2,256]{2,1,0:T(2,128)S(1)}, f32[32,2,256]{2,1,0:T(2,128)S(1)}, u32[]{:S(2)}, u32[]{:S(2)}) collective-permute-start(f32[32,2,256]{2,1,0:T(2,128)S(1)} %collective-permute-done.1.refs_1_), channel_id=1, source_target_pairs={{0,4},{4,8},{8,12},{12,0},{1,5},{5,9},{9,13},{13,1},{2,6},{6,10},{... | collective-permute-start | bytes 196616 | tf_op jit(solution)/shard_map/ppermute | solution.py:331
  30.0 2.5 %copy-start.13 = (bf16[8,11,256]{2,1,0:T(8,128)(2,1)}, bf16[8,11,256]{2,1,0:T(8,128)(2,1)S(1)}, u32[]{:S(2)}) copy-start(bf16[8,11,256]{2,1,0:T(8,128)(2,1)S(1)} %collective-permute-done.10.refs_2_) | copy-start | bytes 135172
  30.0 13.7 %collective-permute-start.4 = (f32[32,2,256]{2,1,0:T(2,128)S(1)}, f32[32,2,256]{2,1,0:T(2,128)S(1)}, u32[]{:S(2)}, u32[]{:S(2)}) collective-permute-start(f32[32,2,256]{2,1,0:T(2,128)S(1)} %broadcast_select_fusion.1.refs_0_), channel_id=1, source_target_pairs={{0,8},{4,12},{8,0},{12,4},{1,9},{5,13},{9,1},{13,5},{2,10},{6,14},... | collective-permute-start | bytes 196616 | tf_op jit(solution)/shard_map/ppermute | solution.py:331
  30.7 13.2 %copy-start.11 = (f32[32,2,256]{2,1,0:T(2,128)}, f32[32,2,256]{2,1,0:T(2,128)S(1)}, u32[]{:S(2)}) copy-start(f32[32,2,256]{2,1,0:T(2,128)S(1)} %collective-permute-done.7.refs_7_) | copy-start | bytes 196612
  30.7 13.1 %collective-permute-start.2 = (f32[32,2,256]{2,1,0:T(2,128)S(1)}, f32[32,2,256]{2,1,0:T(2,128)S(1)}, u32[]{:S(2)}, u32[]{:S(2)}) collective-permute-start(f32[32,2,256]{2,1,0:T(2,128)S(1)} %broadcast_select_fusion.1.refs_0_), channel_id=1, source_target_pairs={{0,4},{4,8},{8,12},{12,0},{1,5},{5,9},{9,13},{13,1},{2,6},{6,10},{... | collective-permute-start | bytes 196616 | tf_op jit(solution)/shard_map/ppermute | solution.py:331
  43.7 0.6 copy-start.16
  43.7 0.6 copy-start.17
  43.7 0.6 copy-start.14
  43.8 0.6 copy-start.18
  43.8 0.6 copy-start.19
  47.1 2.1 %collective-permute-start.16 = (f32[2,256,256]{2,1,0:T(8,128)}, f32[2,256,256]{2,1,0:T(8,128)S(1)}, u32[]{:S(2)}, u32[]{:S(2)}) collective-permute-start(f32[2,256,256]{2,1,0:T(8,128)} %get-tuple-element.18.refs_2_), channel_id=1, source_target_pairs={{0,1},{1,0},{2,3},{3,2},{4,5},{5,4},{6,7},{7,6},{8,9},{9,8},{10,11... | collective-permute-start | bytes 1572872 | tf_op jit(solution)/shard_map/ppermute | solution.py:344
  49.2 1.0 copy-start.1
  66.1 2.2 %collective-permute-start.17 = (f32[2,256,256]{2,1,0:T(8,128)}, f32[2,256,256]{2,1,0:T(8,128)S(1)}, u32[]{:S(2)}, u32[]{:S(2)}) collective-permute-start(f32[2,256,256]{2,1,0:T(8,128)} %get-tuple-element.24.refs_2_), channel_id=1, source_target_pairs={{0,1},{1,0},{2,3},{3,2},{4,5},{5,4},{6,7},{7,6},{8,9},{9,8},{10,11... | collective-permute-start | bytes 1572872 | tf_op jit(solution)/shard_map/ppermute | solution.py:344
  68.3 0.8 copy-start.2
  85.1 2.2 %collective-permute-start.18 = (f32[2,256,256]{2,1,0:T(8,128)}, f32[2,256,256]{2,1,0:T(8,128)S(1)}, u32[]{:S(2)}, u32[]{:S(2)}) collective-permute-start(f32[2,256,256]{2,1,0:T(8,128)} %get-tuple-element.26.refs_2_), channel_id=1, source_target_pairs={{0,1},{1,0},{2,3},{3,2},{4,5},{5,4},{6,7},{7,6},{8,9},{9,8},{10,11... | collective-permute-start | bytes 1572872 | tf_op jit(solution)/shard_map/ppermute | solution.py:344
  87.3 0.8 copy-start
  103.9 2.2 %collective-permute-start.19 = (f32[2,256,256]{2,1,0:T(8,128)}, f32[2,256,256]{2,1,0:T(8,128)S(1)}, u32[]{:S(2)}, u32[]{:S(2)}) collective-permute-start(f32[2,256,256]{2,1,0:T(8,128)} %get-tuple-element.28.refs_0_), channel_id=1, source_target_pairs={{0,1},{1,0},{2,3},{3,2},{4,5},{5,4},{6,7},{7,6},{8,9},{9,8},{10,11... | collective-permute-start | bytes 1572872 | tf_op jit(solution)/shard_map/ppermute | solution.py:344
  106.1 0.8 copy-start.3

commit v2 on v1

--- a/solution.py
+++ b/solution.py
@@ -13,6 +13,7 @@
 ITERS = 4
 STEP_SIZE = 0.5
 GROUP = 4
+PARAMS = pltpu.CompilerParams(vmem_limit_bytes=26 * 2**20)
 F32 = jnp.float32
 BF16 = jnp.bfloat16
 
@@ -161,16 +162,18 @@
     return right_dft(half[:n], half[n:], dft, -1)
 
 
-def first_kernel(share, first_of, places_of, live_total, pieces, n, *refs):
+def first_kernel(share, first_of, places_of, live_total, pieces, spk_dev, fields, n, *refs):
     piece_refs, refs = refs[:pieces], refs[pieces:]
-    dft_ref, row_out, col_out, data_out, back_out = refs[:5]
-    slots, rows_s, cols_s, grid_s, list_s, row_sem, col_sem = refs[5:]
-    spk_dev, fields, ro = piece_refs[0].shape
+    dft_ref, rows_s, cols_s, data_out, back_out, slots, grid_s, list_s = refs
+    blocks, ro = slots.shape[0] // spk_dev, slots.shape[-1]
     groups = share // GROUP
-    for piece, place in zip(piece_refs, places_of(), strict=True):
-        slots[pl.ds(place * spk_dev, spk_dev), 0:fields, :] = piece[...].astype(F32)
+    for piece, at in zip(piece_refs, places_of(), strict=True):
+        for i, place in enumerate(at):
+            block = piece[i].astype(F32)
+            for depth in range(spk_dev):
+                slots[place * spk_dev + depth, 0:fields, :] = block[depth * fields : (depth + 1) * fields]
     taken = jnp.int32(0)
-    for block in range(pieces):
+    for block in range(blocks):
         count = jnp.max(slots[block * spk_dev, fields - 1 : fields, :]).astype(jnp.int32)
         for depth in range(spk_dev):
             list_s[taken] = block * spk_dev + depth
@@ -198,42 +201,29 @@
             data_out[group * GROUP + j] = data
             smeared.append(smear(col_table, -density * data))
         grid_s[...] += grid_dot(jnp.concatenate(smeared, axis=1), rows_s[group])
-        pltpu.make_async_copy(rows_s.at[group], row_out.at[group], row_sem.at[group]).start()
-        pltpu.make_async_copy(cols_s.at[group], col_out.at[group], col_sem.at[group]).start()
         return carry
 
     lax.fori_loop(0, groups, group_step, 0)
     back_out[...] = adjoint(grid_s[...], dft_ref)
 
-    def drain(group, carry):
-        pltpu.make_async_copy(rows_s.at[group], row_out.at[group], row_sem.at[group]).wait()
-        pltpu.make_async_copy(cols_s.at[group], col_out.at[group], col_sem.at[group]).wait()
-        return carry
-
-    lax.fori_loop(0, groups, drain, 0)
-
-
-def step_kernel(share, live_total, n_parts, *refs):
-    thr_ref, est_ref, part_refs, refs = refs[0], refs[1], refs[2 : 2 + n_parts], refs[2 + n_parts :]
-    map_ref, data_ref, dft_ref, haar_ref, row_hbm, col_hbm, est_out, part_out = refs[:8]
-    rows_s, cols_s, weighted_s, grid_s, row_sem, col_sem = refs[8:]
+
+def target_of(est_ref, part_refs):
+    out = []
+    for p in range(2):
+        gradient = sum(part[p] for part in part_refs)
+        out.append((0.0 if est_ref is None else est_ref[p]) - STEP_SIZE * gradient)
+    return out
+
+
+def step_kernel(share, live_total, n_est, n_parts, *refs):
+    thr_ref, refs = refs[0], refs[1:]
+    est_ref, refs = refs[0] if n_est else None, refs[n_est:]
+    part_refs, refs = refs[:n_parts], refs[n_parts:]
+    map_ref, data_ref, dft_ref, haar_ref, rows_s, cols_s, est_out, part_out, weighted_s, grid_s = refs
     groups = share // GROUP
     n = map_ref.shape[1]
     ro = data_ref.shape[-1]
-
-    def copies(group):
-        return (
-            pltpu.make_async_copy(row_hbm.at[group], rows_s.at[group], row_sem.at[group]),
-            pltpu.make_async_copy(col_hbm.at[group], cols_s.at[group], col_sem.at[group]),
-        )
-
-    for group in range(groups):
-        for copy in copies(group):
-            copy.start()
-    target = []
-    for p in range(2):
-        gradient = sum(part[p] for part in part_refs)
-        target.append(est_ref[p] - STEP_SIZE * gradient)
+    target = target_of(est_ref, part_refs)
     re, im = shrink(target[0], target[1], thr_ref, haar_ref)
     est_out[0] = re
     est_out[1] = im
@@ -244,8 +234,6 @@
     grid_s[...] = jnp.zeros_like(grid_s)
 
     def sample_group(group, carry):
-        for copy in copies(group):
-            copy.wait()
         for j in range(GROUP):
             inner = mm(kspace, rows_s[group, :, j * ro : (j + 1) * ro])
             col = cols_s[group, :, j * ro : (j + 1) * ro].astype(F32)
@@ -277,10 +265,11 @@
 
 def map_kernel(places_of, pieces, *refs):
     piece_refs, (back_ref, map_out, part_out, full) = refs[:pieces], refs[pieces:]
-    rows = piece_refs[0].shape[0]
-    for piece, place in zip(piece_refs, places_of(), strict=True):
-        for p in range(2):
-            full[p, pl.ds(place * rows, rows), :] = piece[:, p, :]
+    rows = piece_refs[0].shape[1]
+    for piece, at in zip(piece_refs, places_of(), strict=True):
+        for i, place in enumerate(at):
+            for p in range(2):
+                full[p, pl.ds(place * rows, rows), :] = piece[i, :, p, :]
     for p in range(2):
         map_out[p] = full[p].T
     conj_map(map_out[0], map_out[1], back_ref[...], part_out)
@@ -289,10 +278,7 @@
 def last_kernel(n_parts, rows, mine_of, thr_ref, est_ref, *refs):
     part_refs, (haar_ref, out_ref) = refs[:n_parts], refs[n_parts:]
     n = est_ref.shape[1]
-    target = []
-    for p in range(2):
-        gradient = sum(part[p] for part in part_refs)
-        target.append(est_ref[p] - STEP_SIZE * gradient)
+    target = target_of(est_ref, part_refs)
     mine = mine_of()
     pick = lax.broadcasted_iota(jnp.int32, (rows, n), 1) == (
         lax.broadcasted_iota(jnp.int32, (rows, n), 0) + mine * rows
@@ -314,6 +300,8 @@
     cells = jnp.stack([sample_bins // n, sample_bins % n], axis=1).astype(BF16)
     count = jnp.broadcast_to(spoke_count.astype(BF16)[:, None, None], (spk_dev, 1, ro))
     bundle = jnp.concatenate([interp_weights, cells, kspace_data[0], count], axis=1)
+    fields = bundle.shape[1]
+    bundle = bundle.reshape(spk_dev * fields, ro)
 
     if by_core:
         onto = [(0, 2), (3, 1), (1, 0), (2, 3)]
@@ -323,29 +311,31 @@
         def collect(value):
             near = lax.ppermute(value, ("coil", "spk"), onto)
             far = lax.ppermute(value, ("coil", "spk"), across)
-            return [jnp.where(is_own, value, far), near]
-
-        def spread(values):
-            out = list(values)
+            return jnp.stack([jnp.where(is_own, value, far), near])
+
+        def spread(value):
+            out = [value]
             for shift in range(1, n_tile):
-                out += [lax.ppermute(v, "tile", [(i, (i + shift) % n_tile) for i in range(n_tile)]) for v in values]
+                out.append(lax.ppermute(value, "tile", [(i, (i + shift) % n_tile) for i in range(n_tile)]))
             return out
 
         def places_of():
             tile, coil = lax.axis_index("tile"), lax.axis_index("coil")
             sent = [(tile - shift + n_tile) % n_tile for shift in range(n_tile)]
-            return [at * 2 + block for at in sent for block in (coil, 1 - coil)]
-
-        spokes = spread(collect(bundle))
-        maps = spread(collect(own_map))
+            return [[at * 2 + coil, at * 2 + 1 - coil] for at in sent]
+
+        pair, map_pair = collect(bundle), collect(own_map)
+        spokes = spread(pair)
+        spokes, map_pair = lax.optimization_barrier((spokes, map_pair))
+        maps = spread(map_pair)
         share, first_of = live_total, lambda: jnp.int32(0)
 
         def parts_of(part):
             return [part, lax.ppermute(part, "spk", [(0, 1), (1, 0)])]
     else:
-        spokes = list(lax.all_gather(bundle, ("tile", "spk"), axis=0, tiled=False))
-        maps = list(lax.all_gather(own_map, ("tile", "spk"), axis=0, tiled=False))
-        places_of = lambda: list(range(blocks))
+        spokes = [lax.all_gather(bundle, ("tile", "spk"), axis=0, tiled=False)]
+        maps = [lax.all_gather(own_map, ("tile", "spk"), axis=0, tiled=False)]
+        places_of = lambda: [list(range(blocks))]
         share = live_total // blocks
         first_of = lambda: (lax.axis_index("tile") * n_spk + lax.axis_index("spk")) * share
 
@@ -359,44 +349,38 @@
     image = jax.ShapeDtypeStruct((2, n, n), F32)
     vmem = pl.BlockSpec(memory_space=pltpu.VMEM)
     smem = pl.BlockSpec(memory_space=pltpu.SMEM)
-    hbm = pl.BlockSpec(memory_space=pl.ANY)
-    table_scratch = [pltpu.VMEM(tables.shape, BF16)] * 2
-    sems = [pltpu.SemaphoreType.DMA((groups,))] * 2
     row_tab, col_tab, data, back = pl.pallas_call(
-        functools.partial(first_kernel, share, first_of, places_of, live_total, blocks, n),
+        functools.partial(first_kernel, share, first_of, places_of, live_total, len(spokes), spk_dev, fields, n),
         out_shape=[tables, tables, jax.ShapeDtypeStruct((share, 2, ro), F32), jax.ShapeDtypeStruct((2 * n, n), F32)],
-        in_specs=[vmem] * (blocks + 1),
-        out_specs=[hbm, hbm, vmem, vmem],
+        in_specs=[vmem] * (len(spokes) + 1),
+        out_specs=[vmem] * 4,
         scratch_shapes=[
             pltpu.VMEM((blocks * spk_dev, 16, ro), F32),
-            *table_scratch,
             pltpu.VMEM((2 * n, n), F32),
             pltpu.SMEM((blocks * spk_dev + 1,), jnp.int32),
-            *sems,
         ],
+        compiler_params=PARAMS,
     )(*spokes, dft)
     map_t, part = pl.pallas_call(
-        functools.partial(map_kernel, places_of, blocks),
+        functools.partial(map_kernel, places_of, len(maps)),
         out_shape=[image, image],
-        in_specs=[vmem] * (blocks + 1),
+        in_specs=[vmem] * (len(maps) + 1),
         out_specs=[vmem, vmem],
         scratch_shapes=[pltpu.VMEM((2, n, n), F32)],
+        compiler_params=PARAMS,
     )(*maps, back)
-    estimate = jnp.zeros((2, n, n), F32)
+    estimate = []
     parts = parts_of(part)
     for _ in range(1, ITERS):
-        estimate, part = pl.pallas_call(
-            functools.partial(step_kernel, share, live_total, len(parts)),
+        inputs = (*estimate, *parts, map_t, data, dft, haar, row_tab, col_tab)
+        *estimate, part = pl.pallas_call(
+            functools.partial(step_kernel, share, live_total, len(estimate), len(parts)),
             out_shape=[image, image],
-            in_specs=[smem] + [vmem] * (len(parts) + 5) + [hbm, hbm],
+            in_specs=[smem] + [vmem] * len(inputs),
             out_specs=[vmem, vmem],
-            scratch_shapes=[
-                *table_scratch,
-                pltpu.VMEM((share, 2, ro), F32),
-                pltpu.VMEM((2 * n, n), F32),
-                *sems,
-            ],
-        )(thresholds, estimate, *parts, map_t, data, dft, haar, row_tab, col_tab)
+            scratch_shapes=[pltpu.VMEM((share, 2, ro), F32), pltpu.VMEM((2 * n, n), F32)],
+            compiler_params=PARAMS,
+        )(thresholds, *inputs)
         parts = parts_of(part)
     mine_of = lambda: lax.axis_index("tile") * n_spk + lax.axis_index("spk")
     return pl.pallas_call(
@@ -404,7 +388,8 @@
         out_shape=jax.ShapeDtypeStruct((rows, 2, n), F32),
         in_specs=[smem] + [vmem] * (len(parts) + 2),
         out_specs=vmem,
-    )(thresholds, estimate, *parts, haar)
+        compiler_params=PARAMS,
+    )(thresholds, *estimate, *parts, haar)
 
 
 def solution(mesh):

time: 112 us -> 93.2 us (0.83)
  starting transfers between devices: 27.9 us -> 15.2 us
  Pallas kernels: 65.8 us -> 53.1 us
  waiting for transfers between devices: 9.33 us -> 15.8 us
    ppermute x12 -> x6, starting transfers between devices: 21.8 us -> 8.86 us  [spread(): lax.ppermute(value, 'tile', [(i, (i + shift) % n_tile) for i in range(n_t...]
    pallas_call x4, Pallas kernels: 50.4 us -> 41.1 us  [the longest x3 40.7 us: local(): pl.pallas_call(functools.partial(step_kernel, share, live_total, len(esti...]
    ppermute x12 -> x6, waiting for transfers between devices: 1.21 us -> 7.65 us  [spread(): lax.ppermute(value, 'tile', [(i, (i + shift) % n_tile) for i in range(n_t...]
    pallas_call x1, Pallas kernels: 11.2 us -> 8.69 us  [local(): pl.pallas_call(functools.partial(first_kernel, share, first_of, places_of...]
    unnamed x41 -> x12, local copies, waits for them, and re-layouts: 3.91 us -> 5.41 us
    unnamed x0 -> x2, other arithmetic: none -> 1.41 us
  transfers between devices with their start and end apart: 20 -> 14, of which waited for: 5 -> 8; matrix products, arithmetic and copies ran while one was open for 1% -> 1% of each run, Pallas kernels for 10% -> 9%
where the time goes in v2:
time: 93.2 us; the launch traced here: 92.7 us
  Pallas kernels  53.1 us (57%)
  waiting for transfers between devices  15.8 us (17%)
  starting transfers between devices  15.2 us (16%)
  local copies, waits for them, and re-layouts  5.46 us (6%)
  other arithmetic  2.37 us (3%)
    pallas_call x3, Pallas kernels, local(): pl.pallas_call(functools.partial(step_kernel, share, live_total, len(esti...  40.7 us
    ppermute x6, starting transfers between devices, spread(): lax.ppermute(value, 'tile', [(i, (i + shift) % n_tile) for i in range(n_t...  8.86 us
    pallas_call x1, Pallas kernels, local(): pl.pallas_call(functools.partial(first_kernel, share, first_of, places_of...  8.69 us
    ppermute x6, waiting for transfers between devices, spread(): lax.ppermute(value, 'tile', [(i, (i + shift) % n_tile) for i in range(n_t...  7.65 us
    ppermute x4, waiting for transfers between devices, parts_of(): return [part, lax.ppermute(part, 'spk', [(0, 1), (1, 0)])]  7.18 us
    unnamed x12, local copies, waits for them, and re-layouts  5.41 us
    ppermute x2, starting transfers between devices, collect(): near = lax.ppermute(value, ('coil', 'spk'), onto)  4.27 us
    pallas_call x1, Pallas kernels, local(): pl.pallas_call(functools.partial(last_kernel, len(parts), rows, mine_of),...  3.28 us
  transfers between devices with their start and end apart: 14, of which 8 were waited for; matrix products, arithmetic and copies ran while one was open for 1% of the time, Pallas kernels for 9%

profile of v2, /device:TPU:0, one launch (start us, length us, event | category | flops | bytes accessed | tf_op | source)
XLA Modules:
  0.0 92.7 jit_solution(8373214798792196109)
XLA Ops:
  0.7 0.7 constant_dynamic-update-slice_fusion.4
  1.4 0.7 constant_dynamic-update-slice_fusion.3
  2.1 0.7 constant_dynamic-update-slice_fusion.2
  2.8 0.7 constant_dynamic-update-slice_fusion.1
  3.6 0.7 collective-permute-start
  4.2 4.2 %collective-permute-start.1 = (bf16[88,256]{1,0:T(8,128)(2,1)S(1)}, bf16[88,256]{1,0:T(8,128)(2,1)S(1)}, u32[]{:S(2)}, u32[]{:S(2)}) collective-permute-start(bf16[88,256]{1,0:T(8,128)(2,1)S(1)} %reshape.6), channel_id=1, source_target_pairs={{0,2},{3,1},{1,0},{2,3},{4,6},{7,5},{5,4},{6,7},{8,10},{11,9},{9,8... | collective-permute-start | bytes 135176 | tf_op jit(solution)/shard_map/ppermute | solution.py:312
  8.5 0.0 collective-permute-start.6
  8.5 0.7 collective-permute-start.5
  9.2 0.0 collective-permute-done
  9.2 1.0 %collective-permute-done.1 = bf16[88,256]{1,0:T(8,128)(2,1)S(1)} collective-permute-done((bf16[88,256]{1,0:T(8,128)(2,1)S(1)}, bf16[88,256]{1,0:T(8,128)(2,1)S(1)}, u32[]{:S(2)}, u32[]{:S(2)}) %collective-permute-start.1) | collective-permute-done | bytes 45088 | tf_op jit(solution)/shard_map/ppermute | solution.py:312
  10.2 3.7 %collective-permute-start.4 = (bf16[2,88,256]{2,1,0:T(8,128)(2,1)S(1)}, bf16[2,88,256]{2,1,0:T(8,128)(2,1)S(1)}, u32[]{:S(2)}, u32[]{:S(2)}) collective-permute-start(bf16[2,88,256]{2,1,0:T(8,128)(2,1)S(1)} %pad_maximum_fusion.1.refs_0_), channel_id=1, source_target_pairs={{0,12},{4,0},{8,4},{12,8},{1,13},{5,1},{9,5},{13,9},{2,14},{6,2},{... | collective-permute-start | bytes 270344 | tf_op jit(solution)/shard_map/ppermute | solution.py:319
  13.9 0.0 collective-permute-start.3
  13.9 1.0 %collective-permute-start.2 = (bf16[2,88,256]{2,1,0:T(8,128)(2,1)S(1)}, bf16[2,88,256]{2,1,0:T(8,128)(2,1)S(1)}, u32[]{:S(2)}, u32[]{:S(2)}) collective-permute-start(bf16[2,88,256]{2,1,0:T(8,128)(2,1)S(1)} %pad_maximum_fusion.1.refs_0_), channel_id=1, source_target_pairs={{0,4},{4,8},{8,12},{12,0},{1,5},{5,9},{9,13},{13,1},{2,6},{6,10},{... | collective-permute-start | bytes 270344 | tf_op jit(solution)/shard_map/ppermute | solution.py:319
  14.9 0.0 collective-permute-done.5
  14.9 0.9 select_bitcast_fusion
  15.8 0.0 collective-permute-done.6
  15.8 0.1 pad_maximum_fusion.refs_0_
  15.8 0.2 collective-permute-done.4.refs_3_
  16.0 6.9 %collective-permute-done.3.refs_2_ = bf16[2,88,256]{2,1,0:T(8,128)(2,1)S(1)} collective-permute-done((bf16[2,88,256]{2,1,0:T(8,128)(2,1)S(1)}, bf16[2,88,256]{2,1,0:T(8,128)(2,1)S(1)}, u32[]{:S(2)}, u32[]{:S(2)}) %collective-permute-start.3) | collective-permute-done | bytes 90144 | tf_op jit(solution)/shard_map/ppermute | solution.py:319
  22.9 0.0 collective-permute-done.2.refs_1_
  22.9 0.8 collective-permute-start.9
  23.7 1.3 %collective-permute-start.8 = (f32[2,32,2,256]{3,2,1,0:T(2,128)S(1)}, f32[2,32,2,256]{3,2,1,0:T(2,128)S(1)}, u32[]{:S(2)}, u32[]{:S(2)}) collective-permute-start(f32[2,32,2,256]{3,2,1,0:T(2,128)S(1)} %pad_maximum_fusion.refs_0_), channel_id=1, source_target_pairs={{0,8},{4,12},{8,0},{12,4},{1,9},{5,13},{9,1},{13,5},{2,10},{6,14},... | collective-permute-start | bytes 393224 | tf_op jit(solution)/shard_map/ppermute | solution.py:319
  25.1 2.0 %collective-permute-start.7 = (f32[2,32,2,256]{3,2,1,0:T(2,128)S(1)}, f32[2,32,2,256]{3,2,1,0:T(2,128)S(1)}, u32[]{:S(2)}, u32[]{:S(2)}) collective-permute-start(f32[2,32,2,256]{3,2,1,0:T(2,128)S(1)} %pad_maximum_fusion.refs_0_), channel_id=1, source_target_pairs={{0,4},{4,8},{8,12},{12,0},{1,5},{5,9},{9,13},{13,1},{2,6},{6,10},{... | collective-permute-start | bytes 393224 | tf_op jit(solution)/shard_map/ppermute | solution.py:319
  27.1 0.0 copy-start
  27.1 1.1 %copy-done = bf16[6,256,256]{2,1,0:T(8,128)(2,1)S(1)} copy-done((bf16[6,256,256]{2,1,0:T(8,128)(2,1)S(1)}, bf16[6,256,256]{2,1,0:T(8,128)(2,1)}, u32[]{:S(2)}) %copy-start) | copy-done | bytes 786456
  28.2 8.7 %shard_map.82 = (bf16[8,256,1024]{2,1,0:T(8,128)(2,1)S(1)}, bf16[8,256,1024]{2,1,0:T(8,128)(2,1)S(1)}, f32[32,2,256]{2,1,0:T(2,128)S(1)}, f32[512,256]{1,0:T(8,128)S(1)}) custom-call(bf16[2,88,256]{2,1,0:T(8,128)(2,1)S(1)} %pad_maximum_fusion.1.refs_0_, bf16[2,88,256]{2,1,0:T(8,128)(2,1)S(1)} %collective-permute-done.2.refs_1_, ...), custom_call_target="tpu_custom_call" | custom-call | tf_op jit(solution)/shard_map/pallas_call | solution.py:352
  36.9 0.0 collective-permute-done.9.refs_3_
  36.9 0.6 collective-permute-done.8.refs_2_
  37.5 0.0 collective-permute-done.7.refs_1_
  37.5 0.4 shard_map.83
  37.9 0.1 collective-permute-start.10
  38.0 1.9 %collective-permute-done.10.refs_2_ = f32[2,256,256]{2,1,0:T(8,128)S(1)} collective-permute-done((f32[2,256,256]{2,1,0:T(8,128)S(1)}, f32[2,256,256]{2,1,0:T(8,128)S(1)}, u32[]{:S(2)}, u32[]{:S(2)}) %collective-permute-start.10) | collective-permute-done | bytes 524320 | tf_op jit(solution)/shard_map/ppermute | solution.py:334
  39.9 0.0 copy-start.1
  39.9 1.1 %copy-done.1 = bf16[6,256,256]{2,1,0:T(8,128)(2,1)S(1)} copy-done((bf16[6,256,256]{2,1,0:T(8,128)(2,1)S(1)}, bf16[6,256,256]{2,1,0:T(8,128)(2,1)}, u32[]{:S(2)}) %copy-start.1) | copy-done | bytes 786456
  41.0 0.0 copy-start.2
  41.0 1.0 %copy-done.2 = bf16[4,256,256]{2,1,0:T(8,128)(2,1)S(1)} copy-done((bf16[4,256,256]{2,1,0:T(8,128)(2,1)S(1)}, bf16[4,256,256]{2,1,0:T(8,128)(2,1)}, u32[]{:S(2)}) %copy-start.2) | copy-done | bytes 524312
  42.0 0.7 copy-done.4
  42.7 13.5 %shard_map.84 = (f32[2,256,256]{2,1,0:T(8,128)S(1)}, f32[2,256,256]{2,1,0:T(8,128)S(1)}) custom-call(f32[3]{0:T(128)S(1)} %copy-done.4, f32[2,256,256]{2,1,0:T(8,128)S(1)} %get-tuple-element.28.refs_1_, f32[2,256,256]{2,1,0:T(8,128)S(1)} %collective-permute-done.10.refs_2_, f32[2,256,256]{2,1,0:T(8,128)S(1)} %get-tuple-element.29.refs_3_.refs_4_, ...), custom_call_target="tpu_custom_call" | custom-call | tf_op jit(solution)/shard_map/pallas_call | solution.py:376
  56.2 0.2 collective-permute-start.11
  56.4 1.8 %collective-permute-done.11.refs_3_ = f32[2,256,256]{2,1,0:T(8,128)S(1)} collective-permute-done((f32[2,256,256]{2,1,0:T(8,128)S(1)}, f32[2,256,256]{2,1,0:T(8,128)S(1)}, u32[]{:S(2)}, u32[]{:S(2)}) %collective-permute-start.11) | collective-permute-done | bytes 524320 | tf_op jit(solution)/shard_map/ppermute | solution.py:334
  58.2 0.0 copy-done.3
  58.2 13.7 %shard_map.85 = (f32[2,256,256]{2,1,0:T(8,128)S(1)}, f32[2,256,256]{2,1,0:T(8,128)S(1)}) custom-call(f32[3]{0:T(128)S(1)} %copy-done.4, f32[2,256,256]{2,1,0:T(8,128)S(1)} %get-tuple-element.33.refs_1_, f32[2,256,256]{2,1,0:T(8,128)S(1)} %get-tuple-element.34.refs_2_, f32[2,256,256]{2,1,0:T(8,128)S(1)} %collective-permute-done.11.refs_3_, ...), custom_call_target="tpu_custom_call" | custom-call | tf_op jit(solution)/shard_map/pallas_call | solution.py:376
  71.9 0.2 collective-permute-start.12
  72.1 1.8 %collective-permute-done.12.refs_3_ = f32[2,256,256]{2,1,0:T(8,128)S(1)} collective-permute-done((f32[2,256,256]{2,1,0:T(8,128)S(1)}, f32[2,256,256]{2,1,0:T(8,128)S(1)}, u32[]{:S(2)}, u32[]{:S(2)}) %collective-permute-start.12) | collective-permute-done | bytes 524320 | tf_op jit(solution)/shard_map/ppermute | solution.py:334
  73.9 13.5 %shard_map.86 = (f32[2,256,256]{2,1,0:T(8,128)S(1)}, f32[2,256,256]{2,1,0:T(8,128)S(1)}) custom-call(f32[3]{0:T(128)S(1)} %copy-done.4, f32[2,256,256]{2,1,0:T(8,128)S(1)} %get-tuple-element.35.refs_1_, f32[2,256,256]{2,1,0:T(8,128)S(1)} %get-tuple-element.36.refs_2_, f32[2,256,256]{2,1,0:T(8,128)S(1)} %collective-permute-done.12.refs_3_, ...), custom_call_target="tpu_custom_call" | custom-call | tf_op jit(solution)/shard_map/pallas_call | solution.py:376
  87.4 0.2 collective-permute-start.13
  87.6 1.8 %collective-permute-done.13.refs_1_ = f32[2,256,256]{2,1,0:T(8,128)S(1)} collective-permute-done((f32[2,256,256]{2,1,0:T(8,128)S(1)}, f32[2,256,256]{2,1,0:T(8,128)S(1)}, u32[]{:S(2)}, u32[]{:S(2)}) %collective-permute-start.13) | collective-permute-done | bytes 524320 | tf_op jit(solution)/shard_map/ppermute | solution.py:334
  89.4 3.3 %shard_map.87 = f32[32,2,256]{2,1,0:T(2,128)} custom-call(f32[3]{0:T(128)S(1)} %copy-done.4, f32[2,256,256]{2,1,0:T(8,128)S(1)} %get-tuple-element.37.est_ref, f32[2,256,256]{2,1,0:T(8,128)S(1)} %get-tuple-element.38.refs_0_, f32[2,256,256]{2,1,0:T(8,128)S(1)} %collective-permute-done.13.refs_1_, bf16[4,256,256]{2,1,0:T(8,128)(2,1)S(1)} %copy-done.3), custom_call_target="tpu_custom_call" | custom-call | tf_op jit(solution)/shard_map/pallas_call | solution.py:386
  (7 shorter events, 0.1 us)
Async XLA Ops:
  3.6 5.6 %collective-permute-start = (bf16[88,256]{1,0:T(8,128)(2,1)S(1)}, bf16[88,256]{1,0:T(8,128)(2,1)S(1)}, u32[]{:S(2)}, u32[]{:S(2)}) collective-permute-start(bf16[88,256]{1,0:T(8,128)(2,1)S(1)} %reshape.6), channel_id=1, source_target_pairs={{1,2},{2,1},{5,6},{6,5},{9,10},{10,9},{13,14},{14,13},{17,18},{18,... | collective-permute-start | bytes 135176 | tf_op jit(solution)/shard_map/ppermute | solution.py:313
  4.2 6.0 %collective-permute-start.1 = (bf16[88,256]{1,0:T(8,128)(2,1)S(1)}, bf16[88,256]{1,0:T(8,128)(2,1)S(1)}, u32[]{:S(2)}, u32[]{:S(2)}) collective-permute-start(bf16[88,256]{1,0:T(8,128)(2,1)S(1)} %reshape.6), channel_id=1, source_target_pairs={{0,2},{3,1},{1,0},{2,3},{4,6},{7,5},{5,4},{6,7},{8,10},{11,9},{9,8... | collective-permute-start | bytes 135176 | tf_op jit(solution)/shard_map/ppermute | solution.py:312
  8.5 7.3 %collective-permute-start.6 = (f32[32,2,256]{2,1,0:T(2,128)}, f32[32,2,256]{2,1,0:T(2,128)S(1)}, u32[]{:S(2)}, u32[]{:S(2)}) collective-permute-start(f32[32,2,256]{2,1,0:T(2,128)} %bitcast.15), channel_id=1, source_target_pairs={{0,2},{3,1},{1,0},{2,3},{4,6},{7,5},{5,4},{6,7},{8,10},{11,9},{9,8... | collective-permute-start | bytes 196616 | tf_op jit(solution)/shard_map/ppermute | solution.py:312
  8.5 6.4 %collective-permute-start.5 = (f32[32,2,256]{2,1,0:T(2,128)}, f32[32,2,256]{2,1,0:T(2,128)S(1)}, u32[]{:S(2)}, u32[]{:S(2)}) collective-permute-start(f32[32,2,256]{2,1,0:T(2,128)} %bitcast.16), channel_id=1, source_target_pairs={{1,2},{2,1},{5,6},{6,5},{9,10},{10,9},{13,14},{14,13},{17,18},{18,... | collective-permute-start | bytes 196616 | tf_op jit(solution)/shard_map/ppermute | solution.py:313
  10.2 5.8 %collective-permute-start.4 = (bf16[2,88,256]{2,1,0:T(8,128)(2,1)S(1)}, bf16[2,88,256]{2,1,0:T(8,128)(2,1)S(1)}, u32[]{:S(2)}, u32[]{:S(2)}) collective-permute-start(bf16[2,88,256]{2,1,0:T(8,128)(2,1)S(1)} %pad_maximum_fusion.1.refs_0_), channel_id=1, source_target_pairs={{0,12},{4,0},{8,4},{12,8},{1,13},{5,1},{9,5},{13,9},{2,14},{6,2},{... | collective-permute-start | bytes 270344 | tf_op jit(solution)/shard_map/ppermute | solution.py:319
  13.9 9.0 %collective-permute-start.3 = (bf16[2,88,256]{2,1,0:T(8,128)(2,1)S(1)}, bf16[2,88,256]{2,1,0:T(8,128)(2,1)S(1)}, u32[]{:S(2)}, u32[]{:S(2)}) collective-permute-start(bf16[2,88,256]{2,1,0:T(8,128)(2,1)S(1)} %pad_maximum_fusion.1.refs_0_), channel_id=1, source_target_pairs={{0,8},{4,12},{8,0},{12,4},{1,9},{5,13},{9,1},{13,5},{2,10},{6,14},... | collective-permute-start | bytes 270344 | tf_op jit(solution)/shard_map/ppermute | solution.py:319
  13.9 9.0 %collective-permute-start.2 = (bf16[2,88,256]{2,1,0:T(8,128)(2,1)S(1)}, bf16[2,88,256]{2,1,0:T(8,128)(2,1)S(1)}, u32[]{:S(2)}, u32[]{:S(2)}) collective-permute-start(bf16[2,88,256]{2,1,0:T(8,128)(2,1)S(1)} %pad_maximum_fusion.1.refs_0_), channel_id=1, source_target_pairs={{0,4},{4,8},{8,12},{12,0},{1,5},{5,9},{9,13},{13,1},{2,6},{6,10},{... | collective-permute-start | bytes 270344 | tf_op jit(solution)/shard_map/ppermute | solution.py:319
  22.9 14.0 %collective-permute-start.9 = (f32[2,32,2,256]{3,2,1,0:T(2,128)S(1)}, f32[2,32,2,256]{3,2,1,0:T(2,128)S(1)}, u32[]{:S(2)}, u32[]{:S(2)}) collective-permute-start(f32[2,32,2,256]{3,2,1,0:T(2,128)S(1)} %pad_maximum_fusion.refs_0_), channel_id=1, source_target_pairs={{0,12},{4,0},{8,4},{12,8},{1,13},{5,1},{9,5},{13,9},{2,14},{6,2},{... | collective-permute-start | bytes 393224 | tf_op jit(solution)/shard_map/ppermute | solution.py:319
  23.7 13.8 %collective-permute-start.8 = (f32[2,32,2,256]{3,2,1,0:T(2,128)S(1)}, f32[2,32,2,256]{3,2,1,0:T(2,128)S(1)}, u32[]{:S(2)}, u32[]{:S(2)}) collective-permute-start(f32[2,32,2,256]{3,2,1,0:T(2,128)S(1)} %pad_maximum_fusion.refs_0_), channel_id=1, source_target_pairs={{0,8},{4,12},{8,0},{12,4},{1,9},{5,13},{9,1},{13,5},{2,10},{6,14},... | collective-permute-start | bytes 393224 | tf_op jit(solution)/shard_map/ppermute | solution.py:319
  25.1 12.5 %collective-permute-start.7 = (f32[2,32,2,256]{3,2,1,0:T(2,128)S(1)}, f32[2,32,2,256]{3,2,1,0:T(2,128)S(1)}, u32[]{:S(2)}, u32[]{:S(2)}) collective-permute-start(f32[2,32,2,256]{3,2,1,0:T(2,128)S(1)} %pad_maximum_fusion.refs_0_), channel_id=1, source_target_pairs={{0,4},{4,8},{8,12},{12,0},{1,5},{5,9},{9,13},{13,1},{2,6},{6,10},{... | collective-permute-start | bytes 393224 | tf_op jit(solution)/shard_map/ppermute | solution.py:319
  27.1 1.1 %copy-start = (bf16[6,256,256]{2,1,0:T(8,128)(2,1)S(1)}, bf16[6,256,256]{2,1,0:T(8,128)(2,1)}, u32[]{:S(2)}) copy-start(bf16[6,256,256]{2,1,0:T(8,128)(2,1)} %constant.38.clone.refs_4_.refs_5_.refs_6_) | copy-start | bytes 2359300
  37.9 2.0 %collective-permute-start.10 = (f32[2,256,256]{2,1,0:T(8,128)S(1)}, f32[2,256,256]{2,1,0:T(8,128)S(1)}, u32[]{:S(2)}, u32[]{:S(2)}) collective-permute-start(f32[2,256,256]{2,1,0:T(8,128)S(1)} %get-tuple-element.28.refs_1_), channel_id=1, source_target_pairs={{0,1},{1,0},{2,3},{3,2},{4,5},{5,4},{6,7},{7,6},{8,9},{9,8},{10,11... | collective-permute-start | bytes 1572872 | tf_op jit(solution)/shard_map/ppermute | solution.py:334
  39.9 1.1 %copy-start.1 = (bf16[6,256,256]{2,1,0:T(8,128)(2,1)S(1)}, bf16[6,256,256]{2,1,0:T(8,128)(2,1)}, u32[]{:S(2)}) copy-start(bf16[6,256,256]{2,1,0:T(8,128)(2,1)} %constant.38.clone.refs_4_.refs_5_.refs_6_) | copy-start | bytes 2359300
  41.0 1.0 %copy-start.2 = (bf16[4,256,256]{2,1,0:T(8,128)(2,1)S(1)}, bf16[4,256,256]{2,1,0:T(8,128)(2,1)}, u32[]{:S(2)}) copy-start(bf16[4,256,256]{2,1,0:T(8,128)(2,1)} %constant.39.clone.refs_6_.refs_7_.refs_2_) | copy-start | bytes 1572868
  42.0 0.7 copy-start.4
  42.7 15.5 %copy-start.3 = (bf16[4,256,256]{2,1,0:T(8,128)(2,1)S(1)}, bf16[4,256,256]{2,1,0:T(8,128)(2,1)}, u32[]{:S(2)}) copy-start(bf16[4,256,256]{2,1,0:T(8,128)(2,1)} %constant.39.clone.refs_6_.refs_7_.refs_2_) | copy-start | bytes 1572868
  56.2 2.0 %collective-permute-start.11 = (f32[2,256,256]{2,1,0:T(8,128)S(1)}, f32[2,256,256]{2,1,0:T(8,128)S(1)}, u32[]{:S(2)}, u32[]{:S(2)}) collective-permute-start(f32[2,256,256]{2,1,0:T(8,128)S(1)} %get-tuple-element.34.refs_2_), channel_id=1, source_target_pairs={{0,1},{1,0},{2,3},{3,2},{4,5},{5,4},{6,7},{7,6},{8,9},{9,8},{10,11... | collective-permute-start | bytes 1572872 | tf_op jit(solution)/shard_map/ppermute | solution.py:334
  71.9 2.0 %collective-permute-start.12 = (f32[2,256,256]{2,1,0:T(8,128)S(1)}, f32[2,256,256]{2,1,0:T(8,128)S(1)}, u32[]{:S(2)}, u32[]{:S(2)}) collective-permute-start(f32[2,256,256]{2,1,0:T(8,128)S(1)} %get-tuple-element.36.refs_2_), channel_id=1, source_target_pairs={{0,1},{1,0},{2,3},{3,2},{4,5},{5,4},{6,7},{7,6},{8,9},{9,8},{10,11... | collective-permute-start | bytes 1572872 | tf_op jit(solution)/shard_map/ppermute | solution.py:334
  87.4 2.0 %collective-permute-start.13 = (f32[2,256,256]{2,1,0:T(8,128)S(1)}, f32[2,256,256]{2,1,0:T(8,128)S(1)}, u32[]{:S(2)}, u32[]{:S(2)}) collective-permute-start(f32[2,256,256]{2,1,0:T(8,128)S(1)} %get-tuple-element.38.refs_0_), channel_id=1, source_target_pairs={{0,1},{1,0},{2,3},{3,2},{4,5},{5,4},{6,7},{7,6},{8,9},{9,8},{10,11... | collective-permute-start | bytes 1572872 | tf_op jit(solution)/shard_map/ppermute | solution.py:334

commit v3 on v2

--- a/solution.py
+++ b/solution.py
@@ -12,7 +12,8 @@
 LEVELS = 3
 ITERS = 4
 STEP_SIZE = 0.5
-GROUP = 4
+GROUP = 8
+MARGIN = 8
 PARAMS = pltpu.CompilerParams(vmem_limit_bytes=26 * 2**20)
 F32 = jnp.float32
 BF16 = jnp.bfloat16
@@ -57,24 +58,27 @@
     return high, (x - high.astype(F32)).astype(BF16)
 
 
-def split3(x):
-    high = x.astype(BF16)
-    rest = x - high.astype(F32)
-    mid = rest.astype(BF16)
-    return high, mid, (rest - mid.astype(F32)).astype(BF16)
-
-
 def mm(a, b):
     return jnp.dot(a, b, preferred_element_type=F32)
 
 
+def mm_t(a, b):
+    return lax.dot_general(a, b, (((1,), (1,)), ((), ())), preferred_element_type=F32)
+
+
+def joined(parts, axis):
+    return jnp.concatenate(parts, axis=axis)
+
+
 def right_dft(re, im, dft, sign):
-    top = jnp.concatenate([re, sign * im], axis=1)
-    bottom = jnp.concatenate([im, -sign * re], axis=1)
-    high, low = split2(jnp.concatenate([top, bottom], axis=0))
-    t_high = jnp.concatenate([dft[0], dft[1]], axis=0)
-    t_low = jnp.concatenate([dft[3], dft[4]], axis=0)
-    return mm(high, t_high) + mm(low, t_high) + mm(high, t_low)
+    re_h, re_l = split2(re)
+    im_h, im_l = split2(im)
+    if sign > 0:
+        top, bottom = (re_h, im_h, re_l, im_l, re_h, im_h), (im_h, -re_h, im_l, -re_l, im_h, -re_h)
+    else:
+        top, bottom = (re_h, -im_h, re_l, -im_l, re_h, -im_h), (im_h, re_h, im_l, re_l, im_h, re_h)
+    values = joined([joined(top, 1), joined(bottom, 1)], 0)
+    return mm(values, joined([dft[0], dft[1], dft[0], dft[1], dft[3], dft[4]], 0))
 
 
 def left_dft(stacked, dft, sign):
@@ -82,12 +86,11 @@
     high, low = split2(stacked)
 
     def table(base):
-        top = jnp.concatenate([dft[base], dft[base + plus]], axis=1)
-        bottom = jnp.concatenate([dft[base + minus], dft[base]], axis=1)
-        return jnp.concatenate([top, bottom], axis=0)
-
-    t_high, t_low = table(0), table(3)
-    return mm(t_high, high) + mm(t_high, low) + mm(t_low, high)
+        top = joined([dft[base], dft[base + plus]], 1)
+        bottom = joined([dft[base + minus], dft[base]], 1)
+        return joined([top, bottom], 0)
+
+    return mm(joined([table(0), table(0), table(3)], 1), joined([high, low, high], 0))
 
 
 def labels(positions, length):
@@ -95,14 +98,6 @@
     for level in range(1, LEVELS + 1):
         out = out + jnp.where(positions < length >> level, 1.0, 0.0)
     return out
-
-
-def exact_left(signs, parts):
-    return sum(mm(signs, part) for part in parts)
-
-
-def exact_right(parts, signs):
-    return sum(mm(part, signs) for part in parts)
 
 
 def shrink(re, im, thr_ref, haar, last_rows=None):
@@ -118,26 +113,21 @@
     for level in range(LEVELS):
         limits = jnp.where(band == level + 1, thr_ref[level], limits)
     scale = col_scale * row_scale
-    coeffs = []
-    for part in (re, im):
-        half = exact_left(haar[0], split3(part))
-        coeffs.append(exact_right(split3(half), haar[2]) * scale)
+    half = mm(joined([haar[0]] * 2, 1), joined(split2(joined([re, im], 1)), 0))
+    half = joined([half[:, :n], half[:, n:]], 0)
+    full = mm(joined(split2(half), 1), joined([haar[2]] * 2, 0))
+    coeffs = [full[:n] * scale, full[n:] * scale]
     magnitude = jnp.sqrt(coeffs[0] * coeffs[0] + coeffs[1] * coeffs[1])
     factor = jnp.maximum(magnitude - limits, 0.0) / jnp.maximum(magnitude, limits)
     factor = jnp.where(band <= LEVELS, factor, 1.0) * scale
-    out = []
-    for part in coeffs:
-        half = exact_left(haar[1], split3(part * factor))
-        if last_rows is None:
-            out.append(exact_right(split3(half), haar[3]))
-        else:
-            out.append(
-                sum(
-                    lax.dot_general(last_rows, p, (((1,), (1,)), ((), ())), preferred_element_type=F32)
-                    for p in split3(half)
-                )
-            )
-    return out
+    kept = joined([coeffs[0] * factor, coeffs[1] * factor], 1)
+    half = mm(joined([haar[1]] * 2, 1), joined(split2(kept), 0))
+    half = joined([half[:, :n], half[:, n:]], 0)
+    if last_rows is None:
+        full = mm(joined(split2(half), 1), joined([haar[3]] * 2, 0))
+        return full[:n], full[n:]
+    full = mm_t(joined([last_rows] * 2, 1), joined(split2(half), 1))
+    return full[:, :n], full[:, n:]
 
 
 def density_of(ro, n, live_total):
@@ -148,12 +138,40 @@
 
 def smear(col_table, weighted):
     col = col_table.astype(F32)
-    both = [(col * weighted[p : p + 1]).astype(BF16) for p in range(2)]
-    return jnp.concatenate(both, axis=0)
-
-
-def grid_dot(smeared, row_table):
-    return lax.dot_general(smeared, row_table, (((1,), (1,)), ((), ())), preferred_element_type=F32)
+    return joined([(col * weighted[p : p + 1]).astype(BF16) for p in range(2)], 0)
+
+
+def grid_group(group, rows_s, cols_s, weighted_s, grid_s):
+    span = cols_s.shape[-1]
+    for side in range(2):
+        smeared = smear(cols_s[group, side], weighted_s[group, side])
+        grid_s[side] += mm_t(smeared, rows_s[group, :, side * span : (side + 1) * span])
+
+
+def to_sides(kspace):
+    n = kspace.shape[0] // 2
+    mid = n // 2
+    low, high = [], []
+    for part in (kspace[:n], kspace[n:]):
+        low += [part[n - MARGIN :], part[: mid + MARGIN]]
+        high += [part[mid - MARGIN :], part[:MARGIN]]
+    return joined(low, 0), joined(high, 0)
+
+
+def from_sides(grid_s):
+    span = grid_s.shape[1] // 2
+    mid, m = span - 2 * MARGIN, MARGIN
+    out = []
+    for p in range(2):
+        low, high = grid_s[0, p * span : (p + 1) * span], grid_s[1, p * span : (p + 1) * span]
+        out += [
+            low[m : 2 * m] + high[mid + m :],
+            low[2 * m : mid],
+            low[mid:] + high[: 2 * m],
+            high[2 * m : mid],
+            high[mid : mid + m] + low[:m],
+        ]
+    return joined(out, 0)
 
 
 def adjoint(gridded, dft):
@@ -164,47 +182,63 @@
 
 def first_kernel(share, first_of, places_of, live_total, pieces, spk_dev, fields, n, *refs):
     piece_refs, refs = refs[:pieces], refs[pieces:]
-    dft_ref, rows_s, cols_s, data_out, back_out, slots, grid_s, list_s = refs
-    blocks, ro = slots.shape[0] // spk_dev, slots.shape[-1]
-    groups = share // GROUP
+    dft_ref, rows_s, cols_s, data_out, back_out, slots, weighted_s, grid_s, list_s = refs
+    blocks, ro = slots.shape[0], slots.shape[-1]
+    groups, _, _, span = weighted_s.shape
+    per_group, half = 2 * span // ro, ro // 2
     for piece, at in zip(piece_refs, places_of(), strict=True):
         for i, place in enumerate(at):
-            block = piece[i].astype(F32)
-            for depth in range(spk_dev):
-                slots[place * spk_dev + depth, 0:fields, :] = block[depth * fields : (depth + 1) * fields]
+            slots[place] = piece[i].astype(F32)
     taken = jnp.int32(0)
     for block in range(blocks):
-        count = jnp.max(slots[block * spk_dev, fields - 1 : fields, :]).astype(jnp.int32)
+        count = jnp.max(slots[block, spk_dev * (fields - 1) :, :]).astype(jnp.int32)
         for depth in range(spk_dev):
-            list_s[taken] = block * spk_dev + depth
+            list_s[0, taken] = block
+            list_s[1, taken] = depth
             taken = taken + (depth < count).astype(jnp.int32)
     start = first_of()
     density = density_of(ro, n, live_total)
-    cells = lax.broadcasted_iota(jnp.int32, (n, ro), 0).astype(F32)
+    row_cells = lax.broadcasted_iota(jnp.int32, (n, ro), 0).astype(F32)
+    side_rows = n // 2 + 2 * MARGIN
+    low_cells = lax.broadcasted_iota(jnp.int32, (side_rows, half), 0) + (n - MARGIN)
+    side_cells = [((low_cells + side * (n // 2)) % n).astype(F32) for side in range(2)]
     grid_s[...] = jnp.zeros_like(grid_s)
 
-    def table(at, weights):
+    def table(cells, at, weights):
         before = jnp.where(at == 0, n - 1.0, at - 1)
         after = jnp.where(at == n - 1, 0.0, at + 1)
-        out = jnp.where(cells == after, weights[2:3], 0.0)
-        out = jnp.where(cells == at, weights[1:2], out)
-        return jnp.where(cells == before, weights[0:1], out).astype(BF16)
+        out = jnp.where(cells == after, weights[2], 0.0)
+        out = jnp.where(cells == at, weights[1], out)
+        return jnp.where(cells == before, weights[0], out).astype(BF16)
+
+    def build(group):
+        for j in range(per_group):
+            which = start + group * per_group + j
+            block, depth = list_s[0, which], list_s[1, which]
+            slot = [slots[block, pl.ds(f * spk_dev + depth, 1), :] for f in range(fields - 1)]
+            low_first = slot[7][:, 1:2] <= n // 2
+            slot = [jnp.where(low_first, f, joined([f[:, half:], f[:, :half]], 1)) for f in slot + [density]]
+            rows = table(row_cells, slot[6], slot[0:3])
+            for side in range(2):
+                lanes = slice(side * half, (side + 1) * half)
+                to = slice(j * half, (j + 1) * half)
+                rows_s[group, :, side * span + j * half : side * span + (j + 1) * half] = rows[:, lanes]
+                cols_s[group, side, :, to] = table(side_cells[side], slot[7][:, lanes], [w[:, lanes] for w in slot[3:6]])
+                data = joined([slot[8][:, lanes], slot[9][:, lanes]], 0)
+                data_out[group, side, 0:2, to] = data
+                data_out[group, side, 2:3, to] = slot[10][:, lanes]
+                weighted_s[group, side, :, to] = -slot[10][:, lanes] * data
+
+    build(0)
 
     def group_step(group, carry):
-        smeared = []
-        for j in range(GROUP):
-            slot = slots[list_s[start + group * GROUP + j]]
-            rows_s[group, :, j * ro : (j + 1) * ro] = table(slot[6:7], slot[0:3])
-            col_table = table(slot[7:8], slot[3:6])
-            cols_s[group, :, j * ro : (j + 1) * ro] = col_table
-            data = slot[8:10]
-            data_out[group * GROUP + j] = data
-            smeared.append(smear(col_table, -density * data))
-        grid_s[...] += grid_dot(jnp.concatenate(smeared, axis=1), rows_s[group])
+        grid_group(group - 1, rows_s, cols_s, weighted_s, grid_s)
+        build(group)
         return carry
 
-    lax.fori_loop(0, groups, group_step, 0)
-    back_out[...] = adjoint(grid_s[...], dft_ref)
+    lax.fori_loop(1, groups, group_step, 0)
+    grid_group(groups - 1, rows_s, cols_s, weighted_s, grid_s)
+    back_out[...] = adjoint(from_sides(grid_s), dft_ref)
 
 
 def target_of(est_ref, part_refs):
@@ -215,44 +249,44 @@
     return out
 
 
-def step_kernel(share, live_total, n_est, n_parts, *refs):
+def step_kernel(n_est, n_parts, *refs):
     thr_ref, refs = refs[0], refs[1:]
     est_ref, refs = refs[0] if n_est else None, refs[n_est:]
     part_refs, refs = refs[:n_parts], refs[n_parts:]
-    map_ref, data_ref, dft_ref, haar_ref, rows_s, cols_s, est_out, part_out, weighted_s, grid_s = refs
-    groups = share // GROUP
-    n = map_ref.shape[1]
-    ro = data_ref.shape[-1]
+    map_ref, data_ref, dft_ref, haar_ref, rows_s, cols_s, est_out, part_out, sides_s, weighted_s, grid_s = refs
+    groups, _, _, span = weighted_s.shape
+    n, rows = map_ref.shape[1], cols_s.shape[2]
     target = target_of(est_ref, part_refs)
     re, im = shrink(target[0], target[1], thr_ref, haar_ref)
     est_out[0] = re
     est_out[1] = im
     mre, mim = map_ref[0], map_ref[1]
     half = right_dft(mre * re - mim * im, mre * im + mim * re, dft_ref, 1)
-    kspace = left_dft(half, dft_ref, 1).astype(BF16)
-    density = density_of(ro, n, live_total)
+    for side, values in enumerate(to_sides(left_dft(half, dft_ref, 1))):
+        sides_s[side] = values.astype(BF16)
     grid_s[...] = jnp.zeros_like(grid_s)
 
-    def sample_group(group, carry):
-        for j in range(GROUP):
-            inner = mm(kspace, rows_s[group, :, j * ro : (j + 1) * ro])
-            col = cols_s[group, :, j * ro : (j + 1) * ro].astype(F32)
-            data = data_ref[group * GROUP + j]
-            model = [jnp.sum(inner[p * n : (p + 1) * n] * col, axis=0, keepdims=True) for p in range(2)]
-            weighted_s[group * GROUP + j] = density * (jnp.concatenate(model, axis=0) - data)
+    def sample_group(group):
+        width = min(n, span)
+        for side in range(2):
+            for at in range(0, span, width):
+                lanes = slice(at, at + width)
+                inner = mm(sides_s[side], rows_s[group, :, side * span + at : side * span + at + width])
+                col = cols_s[group, side, :, lanes].astype(F32)
+                model = [jnp.sum(inner[p * rows : (p + 1) * rows] * col, axis=0, keepdims=True) for p in range(2)]
+                data = data_ref[group, side, :, lanes]
+                weighted_s[group, side, :, lanes] = data[2:3] * (joined(model, 0) - data[0:2])
+
+    sample_group(0)
+
+    def group_step(group, carry):
+        grid_group(group - 1, rows_s, cols_s, weighted_s, grid_s)
+        sample_group(group)
         return carry
 
-    lax.fori_loop(0, groups, sample_group, 0)
-
-    def grid_group(group, carry):
-        smeared = [
-            smear(cols_s[group, :, j * ro : (j + 1) * ro], weighted_s[group * GROUP + j]) for j in range(GROUP)
-        ]
-        grid_s[...] += grid_dot(jnp.concatenate(smeared, axis=1), rows_s[group])
-        return carry
-
-    lax.fori_loop(0, groups, grid_group, 0)
-    back = adjoint(grid_s[...], dft_ref)
+    lax.fori_loop(1, groups, group_step, 0)
+    grid_group(groups - 1, rows_s, cols_s, weighted_s, grid_s)
+    back = adjoint(from_sides(grid_s), dft_ref)
     conj_map(map_ref[0], map_ref[1], back, part_out)
 
 
@@ -297,11 +331,12 @@
     live_total = blocks * spk_dev // 2
     own_map = coil_maps[0]
     by_core = n_coil == n_spk == 2
-    cells = jnp.stack([sample_bins // n, sample_bins % n], axis=1).astype(BF16)
-    count = jnp.broadcast_to(spoke_count.astype(BF16)[:, None, None], (spk_dev, 1, ro))
-    bundle = jnp.concatenate([interp_weights, cells, kspace_data[0], count], axis=1)
-    fields = bundle.shape[1]
-    bundle = bundle.reshape(spk_dev * fields, ro)
+    count = jnp.broadcast_to(spoke_count.astype(BF16)[:, None, None], (1, spk_dev, ro))
+    cells = jnp.stack([sample_bins // n, sample_bins % n]).astype(BF16)
+    by_field = [jnp.swapaxes(interp_weights, 0, 1), cells, jnp.swapaxes(kspace_data[0], 0, 1), count]
+    bundle = jnp.concatenate(by_field, axis=0)
+    fields = bundle.shape[0]
+    bundle = bundle.reshape(fields * spk_dev, ro)
 
     if by_core:
         onto = [(0, 2), (3, 1), (1, 0), (2, 3)]
@@ -342,22 +377,30 @@
         def parts_of(part):
             return [lax.psum(part, ("tile", "coil", "spk"))]
 
-    groups = share // GROUP
+    per_group = min(GROUP, share)
+    groups, span, side_rows = share // per_group, per_group * ro // 2, n // 2 + 2 * MARGIN
     dft = jnp.asarray(dft_tables(n))
     haar = jnp.asarray(haar_tables(n))
-    tables = jax.ShapeDtypeStruct((groups, n, GROUP * ro), BF16)
     image = jax.ShapeDtypeStruct((2, n, n), F32)
+    weighted = pltpu.VMEM((groups, 2, 2, span), F32)
+    gridded = pltpu.VMEM((2, 2 * side_rows, n), F32)
     vmem = pl.BlockSpec(memory_space=pltpu.VMEM)
     smem = pl.BlockSpec(memory_space=pltpu.SMEM)
     row_tab, col_tab, data, back = pl.pallas_call(
         functools.partial(first_kernel, share, first_of, places_of, live_total, len(spokes), spk_dev, fields, n),
-        out_shape=[tables, tables, jax.ShapeDtypeStruct((share, 2, ro), F32), jax.ShapeDtypeStruct((2 * n, n), F32)],
+        out_shape=[
+            jax.ShapeDtypeStruct((groups, n, 2 * span), BF16),
+            jax.ShapeDtypeStruct((groups, 2, side_rows, span), BF16),
+            jax.ShapeDtypeStruct((groups, 2, 3, span), F32),
+            jax.ShapeDtypeStruct((2 * n, n), F32),
+        ],
         in_specs=[vmem] * (len(spokes) + 1),
         out_specs=[vmem] * 4,
         scratch_shapes=[
-            pltpu.VMEM((blocks * spk_dev, 16, ro), F32),
-            pltpu.VMEM((2 * n, n), F32),
-            pltpu.SMEM((blocks * spk_dev + 1,), jnp.int32),
+            pltpu.VMEM((blocks, fields * spk_dev, ro), F32),
+            weighted,
+            gridded,
+            pltpu.SMEM((2, blocks * spk_dev + 1), jnp.int32),
         ],
         compiler_params=PARAMS,
     )(*spokes, dft)
@@ -374,11 +417,11 @@
     for _ in range(1, ITERS):
         inputs = (*estimate, *parts, map_t, data, dft, haar, row_tab, col_tab)
         *estimate, part = pl.pallas_call(
-            functools.partial(step_kernel, share, live_total, len(estimate), len(parts)),
+            functools.partial(step_kernel, len(estimate), len(parts)),
             out_shape=[image, image],
             in_specs=[smem] + [vmem] * len(inputs),
             out_specs=[vmem, vmem],
-            scratch_shapes=[pltpu.VMEM((share, 2, ro), F32), pltpu.VMEM((2 * n, n), F32)],
+            scratch_shapes=[pltpu.VMEM((2, 2 * side_rows, n), BF16), weighted, gridded],
             compiler_params=PARAMS,
         )(thresholds, *inputs)
         parts = parts_of(part)

time: 93.2 us -> 79.1 us (0.85)
  Pallas kernels: 53.1 us -> 39.4 us
    pallas_call x3, Pallas kernels: 40.7 us -> 27.4 us  [local(): pl.pallas_call(functools.partial(step_kernel, len(estimate), len(parts)),...]
  transfers between devices with their start and end apart: 14 -> 14, of which waited for: 8 -> 8; matrix products, arithmetic and copies ran while one was open for 1% -> 1% of each run, Pallas kernels for 9% -> 11%
where the time goes in v3:
time: 79.1 us; the launch traced here: 78.6 us
  Pallas kernels  39.4 us (50%)
  waiting for transfers between devices  15.5 us (20%)
  starting transfers between devices  15.1 us (19%)
  local copies, waits for them, and re-layouts  5.41 us (7%)
  other arithmetic  2.37 us (3%)
    pallas_call x3, Pallas kernels, local(): pl.pallas_call(functools.partial(step_kernel, len(estimate), len(parts)),...  27.4 us
    pallas_call x1, Pallas kernels, local(): pl.pallas_call(functools.partial(first_kernel, share, first_of, places_of...  8.99 us
    ppermute x6, starting transfers between devices, spread(): lax.ppermute(value, 'tile', [(i, (i + shift) % n_tile) for i in range(n_t...  8.86 us
    ppermute x6, waiting for transfers between devices, spread(): lax.ppermute(value, 'tile', [(i, (i + shift) % n_tile) for i in range(n_t...  7.34 us
    ppermute x4, waiting for transfers between devices, parts_of(): return [part, lax.ppermute(part, 'spk', [(0, 1), (1, 0)])]  7.19 us
    unnamed x12, local copies, waits for them, and re-layouts  5.41 us
    ppermute x2, starting transfers between devices, collect(): near = lax.ppermute(value, ('coil', 'spk'), onto)  4.27 us
    pallas_call x1, Pallas kernels, local(): pl.pallas_call(functools.partial(last_kernel, len(parts), rows, mine_of),...  2.56 us
  transfers between devices with their start and end apart: 14, of which 8 were waited for; matrix products, arithmetic and copies ran while one was open for 1% of the time, Pallas kernels for 11%

profile of v3, /device:TPU:0, one launch (start us, length us, event | category | flops | bytes accessed | tf_op | source)
XLA Modules:
  0.0 78.6 jit_solution(9290883915171781196)
XLA Ops:
  0.7 0.7 bitcast_dynamic-update-slice_fusion
  1.4 0.7 constant_dynamic-update-slice_fusion.3
  2.1 0.7 constant_dynamic-update-slice_fusion.2
  2.8 0.7 constant_dynamic-update-slice_fusion.1
  3.5 0.7 collective-permute-start
  4.2 4.2 %collective-permute-start.1 = (bf16[88,256]{1,0:T(8,128)(2,1)S(1)}, bf16[88,256]{1,0:T(8,128)(2,1)S(1)}, u32[]{:S(2)}, u32[]{:S(2)}) collective-permute-start(bf16[88,256]{1,0:T(8,128)(2,1)S(1)} %bitcast.22), channel_id=1, source_target_pairs={{0,2},{3,1},{1,0},{2,3},{4,6},{7,5},{5,4},{6,7},{8,10},{11,9},{9,8... | collective-permute-start | bytes 135176 | tf_op jit(solution)/shard_map/ppermute | solution.py:347
  8.4 0.0 collective-permute-start.6
  8.4 0.7 collective-permute-start.5
  9.1 0.0 collective-permute-done
  9.1 1.0 %collective-permute-done.1 = bf16[88,256]{1,0:T(8,128)(2,1)S(1)} collective-permute-done((bf16[88,256]{1,0:T(8,128)(2,1)S(1)}, bf16[88,256]{1,0:T(8,128)(2,1)S(1)}, u32[]{:S(2)}, u32[]{:S(2)}) %collective-permute-start.1) | collective-permute-done | bytes 45088 | tf_op jit(solution)/shard_map/ppermute | solution.py:347
  10.1 3.7 %collective-permute-start.4 = (bf16[2,88,256]{2,1,0:T(8,128)(2,1)S(1)}, bf16[2,88,256]{2,1,0:T(8,128)(2,1)S(1)}, u32[]{:S(2)}, u32[]{:S(2)}) collective-permute-start(bf16[2,88,256]{2,1,0:T(8,128)(2,1)S(1)} %pad_maximum_fusion.1.refs_0_), channel_id=1, source_target_pairs={{0,12},{4,0},{8,4},{12,8},{1,13},{5,1},{9,5},{13,9},{2,14},{6,2},{... | collective-permute-start | bytes 270344 | tf_op jit(solution)/shard_map/ppermute | solution.py:354
  13.8 0.0 collective-permute-start.3
  13.8 1.0 %collective-permute-start.2 = (bf16[2,88,256]{2,1,0:T(8,128)(2,1)S(1)}, bf16[2,88,256]{2,1,0:T(8,128)(2,1)S(1)}, u32[]{:S(2)}, u32[]{:S(2)}) collective-permute-start(bf16[2,88,256]{2,1,0:T(8,128)(2,1)S(1)} %pad_maximum_fusion.1.refs_0_), channel_id=1, source_target_pairs={{0,4},{4,8},{8,12},{12,0},{1,5},{5,9},{9,13},{13,1},{2,6},{6,10},{... | collective-permute-start | bytes 270344 | tf_op jit(solution)/shard_map/ppermute | solution.py:354
  14.8 0.0 collective-permute-done.5
  14.8 0.9 %select_bitcast_fusion = f32[1,32,2,256]{3,2,1,0:T(2,128)S(1)} fusion(f32[32,2,256]{2,1,0:T(2,128)S(1)} %collective-permute-done.5, pred[]{:T(512)S(6)} %eq.5, f32[1,32,2,256]{3,2,1,0:T(2,128)} %param.8), kind=kLoop, calls=%fused_computation.2 | loop fusion | flops 16384 | bytes 196609 | tf_op jit(solution)/shard_map/stack | solution.py:349
  15.7 0.0 collective-permute-done.6
  15.7 0.1 pad_maximum_fusion.refs_0_
  15.8 0.2 collective-permute-done.4.refs_3_
  15.9 6.9 %collective-permute-done.3.refs_2_ = bf16[2,88,256]{2,1,0:T(8,128)(2,1)S(1)} collective-permute-done((bf16[2,88,256]{2,1,0:T(8,128)(2,1)S(1)}, bf16[2,88,256]{2,1,0:T(8,128)(2,1)S(1)}, u32[]{:S(2)}, u32[]{:S(2)}) %collective-permute-start.3) | collective-permute-done | bytes 90144 | tf_op jit(solution)/shard_map/ppermute | solution.py:354
  22.8 0.0 collective-permute-done.2.refs_1_
  22.8 0.8 %collective-permute-start.9 = (f32[2,32,2,256]{3,2,1,0:T(2,128)S(1)}, f32[2,32,2,256]{3,2,1,0:T(2,128)S(1)}, u32[]{:S(2)}, u32[]{:S(2)}) collective-permute-start(f32[2,32,2,256]{3,2,1,0:T(2,128)S(1)} %pad_maximum_fusion.refs_0_), channel_id=1, source_target_pairs={{0,12},{4,0},{8,4},{12,8},{1,13},{5,1},{9,5},{13,9},{2,14},{6,2},{... | collective-permute-start | bytes 393224 | tf_op jit(solution)/shard_map/ppermute | solution.py:354
  23.7 1.3 %collective-permute-start.8 = (f32[2,32,2,256]{3,2,1,0:T(2,128)S(1)}, f32[2,32,2,256]{3,2,1,0:T(2,128)S(1)}, u32[]{:S(2)}, u32[]{:S(2)}) collective-permute-start(f32[2,32,2,256]{3,2,1,0:T(2,128)S(1)} %pad_maximum_fusion.refs_0_), channel_id=1, source_target_pairs={{0,8},{4,12},{8,0},{12,4},{1,9},{5,13},{9,1},{13,5},{2,10},{6,14},... | collective-permute-start | bytes 393224 | tf_op jit(solution)/shard_map/ppermute | solution.py:354
  25.0 2.0 %collective-permute-start.7 = (f32[2,32,2,256]{3,2,1,0:T(2,128)S(1)}, f32[2,32,2,256]{3,2,1,0:T(2,128)S(1)}, u32[]{:S(2)}, u32[]{:S(2)}) collective-permute-start(f32[2,32,2,256]{3,2,1,0:T(2,128)S(1)} %pad_maximum_fusion.refs_0_), channel_id=1, source_target_pairs={{0,4},{4,8},{8,12},{12,0},{1,5},{5,9},{9,13},{13,1},{2,6},{6,10},{... | collective-permute-start | bytes 393224 | tf_op jit(solution)/shard_map/ppermute | solution.py:354
  27.0 0.0 copy-start
  27.0 1.1 %copy-done = bf16[6,256,256]{2,1,0:T(8,128)(2,1)S(1)} copy-done((bf16[6,256,256]{2,1,0:T(8,128)(2,1)S(1)}, bf16[6,256,256]{2,1,0:T(8,128)(2,1)}, u32[]{:S(2)}) %copy-start) | copy-done | bytes 786456
  28.1 9.0 %shard_map.82 = (bf16[4,256,2048]{2,1,0:T(8,128)(2,1)S(1)}, bf16[4,2,144,1024]{3,2,1,0:T(8,128)(2,1)S(1)}, f32[4,2,3,1024]{3,2,1,0:T(4,128)S(1)}, f32[512,256]{1,0:T(8,128)S(1)}) custom-call(bf16[2,88,256]{2,1,0:T(8,128)(2,1)S(1)} %pad_maximum_fusion.1.refs_0_, bf16[2,88,256]{2,1,0:T(8,128)(2,1)S(1)} %collective-permute-done.2.refs_1_, ...), custom_call_target="tpu_custom_call" | custom-call | tf_op jit(solution)/shard_map/pallas_call | solution.py:389
  37.1 0.0 collective-permute-done.9.refs_3_
  37.2 0.3 collective-permute-done.8.refs_2_
  37.4 0.0 collective-permute-done.7.refs_1_
  37.4 0.4 shard_map.83
  37.8 0.1 collective-permute-start.10
  37.9 1.9 %collective-permute-done.10.refs_2_ = f32[2,256,256]{2,1,0:T(8,128)S(1)} collective-permute-done((f32[2,256,256]{2,1,0:T(8,128)S(1)}, f32[2,256,256]{2,1,0:T(8,128)S(1)}, u32[]{:S(2)}, u32[]{:S(2)}) %collective-permute-start.10) | collective-permute-done | bytes 524320 | tf_op jit(solution)/shard_map/ppermute | solution.py:369
  39.8 0.0 copy-start.1
  39.8 1.1 %copy-done.1 = bf16[6,256,256]{2,1,0:T(8,128)(2,1)S(1)} copy-done((bf16[6,256,256]{2,1,0:T(8,128)(2,1)S(1)}, bf16[6,256,256]{2,1,0:T(8,128)(2,1)}, u32[]{:S(2)}) %copy-start.1) | copy-done | bytes 786456
  40.9 0.0 copy-start.2
  40.9 1.0 %copy-done.2 = bf16[4,256,256]{2,1,0:T(8,128)(2,1)S(1)} copy-done((bf16[4,256,256]{2,1,0:T(8,128)(2,1)S(1)}, bf16[4,256,256]{2,1,0:T(8,128)(2,1)}, u32[]{:S(2)}) %copy-start.2) | copy-done | bytes 524312
  42.0 0.7 copy-done.4
  42.6 9.1 %shard_map.84 = (f32[2,256,256]{2,1,0:T(8,128)S(1)}, f32[2,256,256]{2,1,0:T(8,128)S(1)}) custom-call(f32[3]{0:T(128)S(1)} %copy-done.4, f32[2,256,256]{2,1,0:T(8,128)S(1)} %get-tuple-element.28.refs_1_, f32[2,256,256]{2,1,0:T(8,128)S(1)} %collective-permute-done.10.refs_2_, f32[2,256,256]{2,1,0:T(8,128)S(1)} %get-tuple-element.29.refs_3_.refs_4_, ...), custom_call_target="tpu_custom_call" | custom-call | tf_op jit(solution)/shard_map/pallas_call | solution.py:419
  51.7 0.2 collective-permute-start.11
  51.9 1.8 %collective-permute-done.11.refs_3_ = f32[2,256,256]{2,1,0:T(8,128)S(1)} collective-permute-done((f32[2,256,256]{2,1,0:T(8,128)S(1)}, f32[2,256,256]{2,1,0:T(8,128)S(1)}, u32[]{:S(2)}, u32[]{:S(2)}) %collective-permute-start.11) | collective-permute-done | bytes 524320 | tf_op jit(solution)/shard_map/ppermute | solution.py:369
  53.7 0.0 copy-done.3
  53.7 9.3 %shard_map.85 = (f32[2,256,256]{2,1,0:T(8,128)S(1)}, f32[2,256,256]{2,1,0:T(8,128)S(1)}) custom-call(f32[3]{0:T(128)S(1)} %copy-done.4, f32[2,256,256]{2,1,0:T(8,128)S(1)} %get-tuple-element.33.refs_1_, f32[2,256,256]{2,1,0:T(8,128)S(1)} %get-tuple-element.34.refs_2_, f32[2,256,256]{2,1,0:T(8,128)S(1)} %collective-permute-done.11.refs_3_, ...), custom_call_target="tpu_custom_call" | custom-call | tf_op jit(solution)/shard_map/pallas_call | solution.py:419
  63.0 0.2 collective-permute-start.12
  63.2 1.8 %collective-permute-done.12.refs_3_ = f32[2,256,256]{2,1,0:T(8,128)S(1)} collective-permute-done((f32[2,256,256]{2,1,0:T(8,128)S(1)}, f32[2,256,256]{2,1,0:T(8,128)S(1)}, u32[]{:S(2)}, u32[]{:S(2)}) %collective-permute-start.12) | collective-permute-done | bytes 524320 | tf_op jit(solution)/shard_map/ppermute | solution.py:369
  65.0 9.1 %shard_map.86 = (f32[2,256,256]{2,1,0:T(8,128)S(1)}, f32[2,256,256]{2,1,0:T(8,128)S(1)}) custom-call(f32[3]{0:T(128)S(1)} %copy-done.4, f32[2,256,256]{2,1,0:T(8,128)S(1)} %get-tuple-element.35.refs_1_, f32[2,256,256]{2,1,0:T(8,128)S(1)} %get-tuple-element.36.refs_2_, f32[2,256,256]{2,1,0:T(8,128)S(1)} %collective-permute-done.12.refs_3_, ...), custom_call_target="tpu_custom_call" | custom-call | tf_op jit(solution)/shard_map/pallas_call | solution.py:419
  74.0 0.2 collective-permute-start.13
  74.3 1.8 %collective-permute-done.13.refs_1_ = f32[2,256,256]{2,1,0:T(8,128)S(1)} collective-permute-done((f32[2,256,256]{2,1,0:T(8,128)S(1)}, f32[2,256,256]{2,1,0:T(8,128)S(1)}, u32[]{:S(2)}, u32[]{:S(2)}) %collective-permute-start.13) | collective-permute-done | bytes 524320 | tf_op jit(solution)/shard_map/ppermute | solution.py:369
  76.0 2.6 %shard_map.87 = f32[32,2,256]{2,1,0:T(2,128)} custom-call(f32[3]{0:T(128)S(1)} %copy-done.4, f32[2,256,256]{2,1,0:T(8,128)S(1)} %get-tuple-element.37.est_ref, f32[2,256,256]{2,1,0:T(8,128)S(1)} %get-tuple-element.38.refs_0_, f32[2,256,256]{2,1,0:T(8,128)S(1)} %collective-permute-done.13.refs_1_, bf16[4,256,256]{2,1,0:T(8,128)(2,1)S(1)} %copy-done.3), custom_call_target="tpu_custom_call" | custom-call | tf_op jit(solution)/shard_map/pallas_call | solution.py:429
  (5 shorter events, 0.0 us)
Async XLA Ops:
  3.5 5.6 %collective-permute-start = (bf16[88,256]{1,0:T(8,128)(2,1)S(1)}, bf16[88,256]{1,0:T(8,128)(2,1)S(1)}, u32[]{:S(2)}, u32[]{:S(2)}) collective-permute-start(bf16[88,256]{1,0:T(8,128)(2,1)S(1)} %bitcast.21), channel_id=1, source_target_pairs={{1,2},{2,1},{5,6},{6,5},{9,10},{10,9},{13,14},{14,13},{17,18},{18,... | collective-permute-start | bytes 135176 | tf_op jit(solution)/shard_map/ppermute | solution.py:348
  4.2 6.0 %collective-permute-start.1 = (bf16[88,256]{1,0:T(8,128)(2,1)S(1)}, bf16[88,256]{1,0:T(8,128)(2,1)S(1)}, u32[]{:S(2)}, u32[]{:S(2)}) collective-permute-start(bf16[88,256]{1,0:T(8,128)(2,1)S(1)} %bitcast.22), channel_id=1, source_target_pairs={{0,2},{3,1},{1,0},{2,3},{4,6},{7,5},{5,4},{6,7},{8,10},{11,9},{9,8... | collective-permute-start | bytes 135176 | tf_op jit(solution)/shard_map/ppermute | solution.py:347
  8.4 7.3 %collective-permute-start.6 = (f32[32,2,256]{2,1,0:T(2,128)}, f32[32,2,256]{2,1,0:T(2,128)S(1)}, u32[]{:S(2)}, u32[]{:S(2)}) collective-permute-start(f32[32,2,256]{2,1,0:T(2,128)} %bitcast.23), channel_id=1, source_target_pairs={{0,2},{3,1},{1,0},{2,3},{4,6},{7,5},{5,4},{6,7},{8,10},{11,9},{9,8... | collective-permute-start | bytes 196616 | tf_op jit(solution)/shard_map/ppermute | solution.py:347
  8.4 6.4 %collective-permute-start.5 = (f32[32,2,256]{2,1,0:T(2,128)}, f32[32,2,256]{2,1,0:T(2,128)S(1)}, u32[]{:S(2)}, u32[]{:S(2)}) collective-permute-start(f32[32,2,256]{2,1,0:T(2,128)} %bitcast.24), channel_id=1, source_target_pairs={{1,2},{2,1},{5,6},{6,5},{9,10},{10,9},{13,14},{14,13},{17,18},{18,... | collective-permute-start | bytes 196616 | tf_op jit(solution)/shard_map/ppermute | solution.py:348
  10.1 5.8 %collective-permute-start.4 = (bf16[2,88,256]{2,1,0:T(8,128)(2,1)S(1)}, bf16[2,88,256]{2,1,0:T(8,128)(2,1)S(1)}, u32[]{:S(2)}, u32[]{:S(2)}) collective-permute-start(bf16[2,88,256]{2,1,0:T(8,128)(2,1)S(1)} %pad_maximum_fusion.1.refs_0_), channel_id=1, source_target_pairs={{0,12},{4,0},{8,4},{12,8},{1,13},{5,1},{9,5},{13,9},{2,14},{6,2},{... | collective-permute-start | bytes 270344 | tf_op jit(solution)/shard_map/ppermute | solution.py:354
  13.8 9.0 %collective-permute-start.3 = (bf16[2,88,256]{2,1,0:T(8,128)(2,1)S(1)}, bf16[2,88,256]{2,1,0:T(8,128)(2,1)S(1)}, u32[]{:S(2)}, u32[]{:S(2)}) collective-permute-start(bf16[2,88,256]{2,1,0:T(8,128)(2,1)S(1)} %pad_maximum_fusion.1.refs_0_), channel_id=1, source_target_pairs={{0,8},{4,12},{8,0},{12,4},{1,9},{5,13},{9,1},{13,5},{2,10},{6,14},... | collective-permute-start | bytes 270344 | tf_op jit(solution)/shard_map/ppermute | solution.py:354
  13.8 9.0 %collective-permute-start.2 = (bf16[2,88,256]{2,1,0:T(8,128)(2,1)S(1)}, bf16[2,88,256]{2,1,0:T(8,128)(2,1)S(1)}, u32[]{:S(2)}, u32[]{:S(2)}) collective-permute-start(bf16[2,88,256]{2,1,0:T(8,128)(2,1)S(1)} %pad_maximum_fusion.1.refs_0_), channel_id=1, source_target_pairs={{0,4},{4,8},{8,12},{12,0},{1,5},{5,9},{9,13},{13,1},{2,6},{6,10},{... | collective-permute-start | bytes 270344 | tf_op jit(solution)/shard_map/ppermute | solution.py:354
  22.8 14.3 %collective-permute-start.9 = (f32[2,32,2,256]{3,2,1,0:T(2,128)S(1)}, f32[2,32,2,256]{3,2,1,0:T(2,128)S(1)}, u32[]{:S(2)}, u32[]{:S(2)}) collective-permute-start(f32[2,32,2,256]{3,2,1,0:T(2,128)S(1)} %pad_maximum_fusion.refs_0_), channel_id=1, source_target_pairs={{0,12},{4,0},{8,4},{12,8},{1,13},{5,1},{9,5},{13,9},{2,14},{6,2},{... | collective-permute-start | bytes 393224 | tf_op jit(solution)/shard_map/ppermute | solution.py:354
  23.7 13.8 %collective-permute-start.8 = (f32[2,32,2,256]{3,2,1,0:T(2,128)S(1)}, f32[2,32,2,256]{3,2,1,0:T(2,128)S(1)}, u32[]{:S(2)}, u32[]{:S(2)}) collective-permute-start(f32[2,32,2,256]{3,2,1,0:T(2,128)S(1)} %pad_maximum_fusion.refs_0_), channel_id=1, source_target_pairs={{0,8},{4,12},{8,0},{12,4},{1,9},{5,13},{9,1},{13,5},{2,10},{6,14},... | collective-permute-start | bytes 393224 | tf_op jit(solution)/shard_map/ppermute | solution.py:354
  25.0 12.5 %collective-permute-start.7 = (f32[2,32,2,256]{3,2,1,0:T(2,128)S(1)}, f32[2,32,2,256]{3,2,1,0:T(2,128)S(1)}, u32[]{:S(2)}, u32[]{:S(2)}) collective-permute-start(f32[2,32,2,256]{3,2,1,0:T(2,128)S(1)} %pad_maximum_fusion.refs_0_), channel_id=1, source_target_pairs={{0,4},{4,8},{8,12},{12,0},{1,5},{5,9},{9,13},{13,1},{2,6},{6,10},{... | collective-permute-start | bytes 393224 | tf_op jit(solution)/shard_map/ppermute | solution.py:354
  27.0 1.1 %copy-start = (bf16[6,256,256]{2,1,0:T(8,128)(2,1)S(1)}, bf16[6,256,256]{2,1,0:T(8,128)(2,1)}, u32[]{:S(2)}) copy-start(bf16[6,256,256]{2,1,0:T(8,128)(2,1)} %constant.38.clone.refs_4_.refs_5_.refs_6_) | copy-start | bytes 2359300
  37.8 2.0 %collective-permute-start.10 = (f32[2,256,256]{2,1,0:T(8,128)S(1)}, f32[2,256,256]{2,1,0:T(8,128)S(1)}, u32[]{:S(2)}, u32[]{:S(2)}) collective-permute-start(f32[2,256,256]{2,1,0:T(8,128)S(1)} %get-tuple-element.28.refs_1_), channel_id=1, source_target_pairs={{0,1},{1,0},{2,3},{3,2},{4,5},{5,4},{6,7},{7,6},{8,9},{9,8},{10,11... | collective-permute-start | bytes 1572872 | tf_op jit(solution)/shard_map/ppermute | solution.py:369
  39.8 1.1 %copy-start.1 = (bf16[6,256,256]{2,1,0:T(8,128)(2,1)S(1)}, bf16[6,256,256]{2,1,0:T(8,128)(2,1)}, u32[]{:S(2)}) copy-start(bf16[6,256,256]{2,1,0:T(8,128)(2,1)} %constant.38.clone.refs_4_.refs_5_.refs_6_) | copy-start | bytes 2359300
  40.9 1.0 %copy-start.2 = (bf16[4,256,256]{2,1,0:T(8,128)(2,1)S(1)}, bf16[4,256,256]{2,1,0:T(8,128)(2,1)}, u32[]{:S(2)}) copy-start(bf16[4,256,256]{2,1,0:T(8,128)(2,1)} %constant.39.clone.refs_6_.refs_7_.refs_2_) | copy-start | bytes 1572868
  42.0 0.7 copy-start.4
  42.6 11.1 %copy-start.3 = (bf16[4,256,256]{2,1,0:T(8,128)(2,1)S(1)}, bf16[4,256,256]{2,1,0:T(8,128)(2,1)}, u32[]{:S(2)}) copy-start(bf16[4,256,256]{2,1,0:T(8,128)(2,1)} %constant.39.clone.refs_6_.refs_7_.refs_2_) | copy-start | bytes 1572868
  51.7 2.0 %collective-permute-start.11 = (f32[2,256,256]{2,1,0:T(8,128)S(1)}, f32[2,256,256]{2,1,0:T(8,128)S(1)}, u32[]{:S(2)}, u32[]{:S(2)}) collective-permute-start(f32[2,256,256]{2,1,0:T(8,128)S(1)} %get-tuple-element.34.refs_2_), channel_id=1, source_target_pairs={{0,1},{1,0},{2,3},{3,2},{4,5},{5,4},{6,7},{7,6},{8,9},{9,8},{10,11... | collective-permute-start | bytes 1572872 | tf_op jit(solution)/shard_map/ppermute | solution.py:369
  63.0 2.0 %collective-permute-start.12 = (f32[2,256,256]{2,1,0:T(8,128)S(1)}, f32[2,256,256]{2,1,0:T(8,128)S(1)}, u32[]{:S(2)}, u32[]{:S(2)}) collective-permute-start(f32[2,256,256]{2,1,0:T(8,128)S(1)} %get-tuple-element.36.refs_2_), channel_id=1, source_target_pairs={{0,1},{1,0},{2,3},{3,2},{4,5},{5,4},{6,7},{7,6},{8,9},{9,8},{10,11... | collective-permute-start | bytes 1572872 | tf_op jit(solution)/shard_map/ppermute | solution.py:369
  74.0 2.0 %collective-permute-start.13 = (f32[2,256,256]{2,1,0:T(8,128)S(1)}, f32[2,256,256]{2,1,0:T(8,128)S(1)}, u32[]{:S(2)}, u32[]{:S(2)}) collective-permute-start(f32[2,256,256]{2,1,0:T(8,128)S(1)} %get-tuple-element.38.refs_0_), channel_id=1, source_target_pairs={{0,1},{1,0},{2,3},{3,2},{4,5},{5,4},{6,7},{7,6},{8,9},{9,8},{10,11... | collective-permute-start | bytes 1572872 | tf_op jit(solution)/shard_map/ppermute | solution.py:369

commit v4 on v3

--- a/solution.py
+++ b/solution.py
@@ -111,7 +111,7 @@
     band = jnp.minimum(col_label, row_label)
     limits = jnp.full((n, n), 1.0, F32)
     for level in range(LEVELS):
-        limits = jnp.where(band == level + 1, thr_ref[level], limits)
+        limits = jnp.where(band == level + 1, thr_ref[level : level + 1, :], limits)
     scale = col_scale * row_scale
     half = mm(joined([haar[0]] * 2, 1), joined(split2(joined([re, im], 1)), 0))
     half = joined([half[:, :n], half[:, n:]], 0)
@@ -180,29 +180,61 @@
     return right_dft(half[:n], half[n:], dft, -1)
 
 
-def first_kernel(share, first_of, places_of, live_total, pieces, spk_dev, fields, n, *refs):
-    piece_refs, refs = refs[:pieces], refs[pieces:]
-    dft_ref, rows_s, cols_s, data_out, back_out, slots, weighted_s, grid_s, list_s = refs
-    blocks, ro = slots.shape[0], slots.shape[-1]
-    groups, _, _, span = weighted_s.shape
-    per_group, half = 2 * span // ro, ro // 2
-    for piece, at in zip(piece_refs, places_of(), strict=True):
-        for i, place in enumerate(at):
-            slots[place] = piece[i].astype(F32)
+def pack_kernel(data_ref, weight_ref, bins_ref, count_ref, out_ref):
+    slots, ro = bins_ref.shape
+    n = ro
+    bins = bins_ref[...]
+    fields = [data_ref[:, p, :].astype(F32) for p in range(2)]
+    fields += [weight_ref[i].astype(F32) for i in range(weight_ref.shape[0])]
+    fields += [(bins // n).astype(F32), (bins % n).astype(F32)]
+    fields.append(jnp.full((slots, ro), count_ref[0].astype(F32)))
+    out_ref[...] = joined(fields, 0).astype(BF16)
+
+
+def join_kernel(data_rows, *refs):
+    pieces, (data_out, spoke_out) = refs[:-2], refs[-2:]
+    for i, piece in enumerate(pieces):
+        data_out[i] = piece[:data_rows]
+        spoke_out[i] = piece[data_rows:]
+
+
+def stack_kernel(*refs):
+    for i, piece in enumerate(refs[:-1]):
+        refs[-1][i] = piece[...]
+
+
+def constants_kernel(thr_ref, dft_ref, haar_ref, thr_out, dft_out, haar_out):
+    for level in range(LEVELS):
+        thr_out[level : level + 1, :] = jnp.full((1, thr_out.shape[1]), thr_ref[level])
+    dft_out[...] = dft_ref[...]
+    haar_out[...] = haar_ref[...]
+
+
+def live_list(slots, spk_dev, list_s):
     taken = jnp.int32(0)
-    for block in range(blocks):
-        count = jnp.max(slots[block, spk_dev * (fields - 1) :, :]).astype(jnp.int32)
+    for block in range(slots.shape[0]):
+        count = jnp.max(slots[block, slots.shape[1] - spk_dev :, :]).astype(jnp.int32)
         for depth in range(spk_dev):
             list_s[0, taken] = block
             list_s[1, taken] = depth
             taken = taken + (depth < count).astype(jnp.int32)
+
+
+def table_kernel(first_of, blocks_of, live_total, pieces, spk_dev, n, *refs):
+    spoke_refs, refs = refs[:pieces], refs[pieces:]
+    rows_s, cols_s, flags_out, list_out, slots = refs
+    ro = slots.shape[-1]
+    groups, _, _, span = flags_out.shape
+    per_group, half = 2 * span // ro, ro // 2
+    for place, value in blocks_of(spoke_refs):
+        slots[place] = value.astype(F32)
+    live_list(slots, spk_dev, list_out)
     start = first_of()
     density = density_of(ro, n, live_total)
     row_cells = lax.broadcasted_iota(jnp.int32, (n, ro), 0).astype(F32)
     side_rows = n // 2 + 2 * MARGIN
     low_cells = lax.broadcasted_iota(jnp.int32, (side_rows, half), 0) + (n - MARGIN)
     side_cells = [((low_cells + side * (n // 2)) % n).astype(F32) for side in range(2)]
-    grid_s[...] = jnp.zeros_like(grid_s)
 
     def table(cells, at, weights):
         before = jnp.where(at == 0, n - 1.0, at - 1)
@@ -211,29 +243,57 @@
         out = jnp.where(cells == at, weights[1], out)
         return jnp.where(cells == before, weights[0], out).astype(BF16)
 
-    def build(group):
+    def build(group, carry):
         for j in range(per_group):
             which = start + group * per_group + j
-            block, depth = list_s[0, which], list_s[1, which]
-            slot = [slots[block, pl.ds(f * spk_dev + depth, 1), :] for f in range(fields - 1)]
+            block, depth = list_out[0, which], list_out[1, which]
+            slot = [slots[block, pl.ds(f * spk_dev + depth, 1), :] for f in range(8)]
             low_first = slot[7][:, 1:2] <= n // 2
-            slot = [jnp.where(low_first, f, joined([f[:, half:], f[:, :half]], 1)) for f in slot + [density]]
+            slot = slot + [density, jnp.where(low_first, jnp.ones_like(density), 0.0)]
+            slot = [jnp.where(low_first, f, joined([f[:, half:], f[:, :half]], 1)) for f in slot]
             rows = table(row_cells, slot[6], slot[0:3])
             for side in range(2):
                 lanes = slice(side * half, (side + 1) * half)
                 to = slice(j * half, (j + 1) * half)
                 rows_s[group, :, side * span + j * half : side * span + (j + 1) * half] = rows[:, lanes]
                 cols_s[group, side, :, to] = table(side_cells[side], slot[7][:, lanes], [w[:, lanes] for w in slot[3:6]])
-                data = joined([slot[8][:, lanes], slot[9][:, lanes]], 0)
-                data_out[group, side, 0:2, to] = data
-                data_out[group, side, 2:3, to] = slot[10][:, lanes]
-                weighted_s[group, side, :, to] = -slot[10][:, lanes] * data
-
-    build(0)
+                flags_out[group, side, :, to] = joined([f[:, lanes] for f in slot[8:10]], 0)
+        return carry
+
+    lax.fori_loop(0, groups, build, 0)
+
+
+def first_kernel(first_of, blocks_of, pieces, spk_dev, *refs):
+    data_refs, refs = refs[:pieces], refs[pieces:]
+    list_ref, flags_ref, rows_s, cols_s, dft_ref, data_out, back_out, slots, weighted_s, grid_s = refs
+    ro = slots.shape[-1]
+    groups, _, _, span = weighted_s.shape
+    per_group, half = 2 * span // ro, ro // 2
+    for place, value in blocks_of(data_refs):
+        slots[place] = value.astype(F32)
+    start = first_of()
+    grid_s[...] = jnp.zeros_like(grid_s)
+
+    def pick(group):
+        for j in range(per_group):
+            which = start + group * per_group + j
+            block, depth = list_ref[0, which], list_ref[1, which]
+            data = joined([slots[block, pl.ds(p * spk_dev + depth, 1), :] for p in range(2)], 0)
+            to = slice(j * half, (j + 1) * half)
+            low_first = flags_ref[group, 0, 1:2, to] > 0.5
+            halves = [data[:, :half], data[:, half:]]
+            for side in range(2):
+                mine = jnp.where(low_first, halves[side], halves[1 - side])
+                density = flags_ref[group, side, 0:1, to]
+                data_out[group, side, 0:2, to] = mine
+                data_out[group, side, 2:3, to] = density
+                weighted_s[group, side, :, to] = -density * mine
+
+    pick(0)
 
     def group_step(group, carry):
         grid_group(group - 1, rows_s, cols_s, weighted_s, grid_s)
-        build(group)
+        pick(group)
         return carry
 
     lax.fori_loop(1, groups, group_step, 0)
@@ -297,13 +357,12 @@
     part_out[1] = mre * bim - mim * bre
 
 
-def map_kernel(places_of, pieces, *refs):
+def map_kernel(blocks_of, pieces, *refs):
     piece_refs, (back_ref, map_out, part_out, full) = refs[:pieces], refs[pieces:]
     rows = piece_refs[0].shape[1]
-    for piece, at in zip(piece_refs, places_of(), strict=True):
-        for i, place in enumerate(at):
-            for p in range(2):
-                full[p, pl.ds(place * rows, rows), :] = piece[i, :, p, :]
+    for place, value in blocks_of(piece_refs):
+        for p in range(2):
+            full[p, pl.ds(place * rows, rows), :] = value[:, p, :]
     for p in range(2):
         map_out[p] = full[p].T
     conj_map(map_out[0], map_out[1], back_ref[...], part_out)
@@ -331,22 +390,34 @@
     live_total = blocks * spk_dev // 2
     own_map = coil_maps[0]
     by_core = n_coil == n_spk == 2
-    count = jnp.broadcast_to(spoke_count.astype(BF16)[:, None, None], (1, spk_dev, ro))
-    cells = jnp.stack([sample_bins // n, sample_bins % n]).astype(BF16)
-    by_field = [jnp.swapaxes(interp_weights, 0, 1), cells, jnp.swapaxes(kspace_data[0], 0, 1), count]
-    bundle = jnp.concatenate(by_field, axis=0)
-    fields = bundle.shape[0]
-    bundle = bundle.reshape(fields * spk_dev, ro)
+    vmem = pl.BlockSpec(memory_space=pltpu.VMEM)
+    smem = pl.BlockSpec(memory_space=pltpu.SMEM)
+    data_rows, fields = 2 * spk_dev, 11
+    spoke_rows = fields * spk_dev - data_rows
+    bundle = pl.pallas_call(
+        pack_kernel,
+        out_shape=jax.ShapeDtypeStruct((fields * spk_dev, ro), BF16),
+        in_specs=[vmem, vmem, vmem, smem],
+        out_specs=vmem,
+        compiler_params=PARAMS,
+    )(kspace_data[0], jnp.swapaxes(interp_weights, 0, 1), sample_bins, spoke_count)
+
+    dft, haar = dft_tables(n), haar_tables(n)
+    limits, dft, haar = pl.pallas_call(
+        constants_kernel,
+        out_shape=[
+            jax.ShapeDtypeStruct((LEVELS, n), F32),
+            jax.ShapeDtypeStruct(dft.shape, BF16),
+            jax.ShapeDtypeStruct(haar.shape, BF16),
+        ],
+        in_specs=[smem, vmem, vmem],
+        out_specs=[vmem] * 3,
+        compiler_params=PARAMS,
+    )(thresholds, jnp.asarray(dft), jnp.asarray(haar))
 
     if by_core:
         onto = [(0, 2), (3, 1), (1, 0), (2, 3)]
         across = [(1, 2), (2, 1)]
-        is_own = lax.axis_index("coil") == lax.axis_index("spk")
-
-        def collect(value):
-            near = lax.ppermute(value, ("coil", "spk"), onto)
-            far = lax.ppermute(value, ("coil", "spk"), across)
-            return jnp.stack([jnp.where(is_own, value, far), near])
 
         def spread(value):
             out = [value]
@@ -354,23 +425,68 @@
                 out.append(lax.ppermute(value, "tile", [(i, (i + shift) % n_tile) for i in range(n_tile)]))
             return out
 
-        def places_of():
-            tile, coil = lax.axis_index("tile"), lax.axis_index("coil")
-            sent = [(tile - shift + n_tile) % n_tile for shift in range(n_tile)]
-            return [[at * 2 + coil, at * 2 + 1 - coil] for at in sent]
-
-        pair, map_pair = collect(bundle), collect(own_map)
-        spokes = spread(pair)
-        spokes, map_pair = lax.optimization_barrier((spokes, map_pair))
-        maps = spread(map_pair)
+        def to_coil(value):
+            return [value, lax.ppermute(value, ("coil", "spk"), across), lax.ppermute(value, ("coil", "spk"), onto)]
+
+        def senders():
+            tile = lax.axis_index("tile")
+            return [(tile - shift + n_tile) % n_tile for shift in range(n_tile)]
+
+        def spoke_blocks(refs):
+            own, other = refs
+            spk = lax.axis_index("spk")
+            for i, at in enumerate(senders()):
+                yield at * 2 + spk, own[i]
+                yield at * 2 + 1 - spk, other[i]
+
+        def coil_blocks(refs):
+            own, far, near = refs
+            coil = lax.axis_index("coil")
+            is_own = coil == lax.axis_index("spk")
+            for i, at in enumerate(senders()):
+                yield at * 2 + coil, jnp.where(is_own, own[i], far[i])
+                yield at * 2 + 1 - coil, near[i]
+
+        swap = [(0, 1), (1, 0)]
+        pieces = spread(bundle)
+        own_map, bundle = lax.optimization_barrier((own_map, bundle))
+        map_pieces = spread(own_map)
+        pieces, limits, dft, haar = lax.optimization_barrier((pieces, limits, dft, haar))
+        own_data, own_spokes = pl.pallas_call(
+            functools.partial(join_kernel, data_rows),
+            out_shape=[
+                jax.ShapeDtypeStruct((n_tile, data_rows, ro), BF16),
+                jax.ShapeDtypeStruct((n_tile, spoke_rows, ro), BF16),
+            ],
+            in_specs=[vmem] * n_tile,
+            out_specs=[vmem] * 2,
+            compiler_params=PARAMS,
+        )(*pieces)
+        other_spokes = lax.ppermute(own_spokes, "spk", swap)
+        coil_data = to_coil(own_data)
+        map_pieces, own_spokes, own_data = lax.optimization_barrier((map_pieces, own_spokes, own_data))
+        own_maps = pl.pallas_call(
+            stack_kernel,
+            out_shape=jax.ShapeDtypeStruct((n_tile, *own_map.shape), F32),
+            in_specs=[vmem] * n_tile,
+            out_specs=vmem,
+            compiler_params=PARAMS,
+        )(*map_pieces)
+        maps = to_coil(own_maps)
+        spokes = [own_spokes, other_spokes]
         share, first_of = live_total, lambda: jnp.int32(0)
 
         def parts_of(part):
-            return [part, lax.ppermute(part, "spk", [(0, 1), (1, 0)])]
+            return [part, lax.ppermute(part, "spk", swap)]
     else:
-        spokes = [lax.all_gather(bundle, ("tile", "spk"), axis=0, tiled=False)]
-        maps = [lax.all_gather(own_map, ("tile", "spk"), axis=0, tiled=False)]
-        places_of = lambda: [list(range(blocks))]
+        def gather(value):
+            return [lax.all_gather(value, ("tile", "spk"), axis=0, tiled=False)]
+
+        def spoke_blocks(refs):
+            return ((i, refs[0][i]) for i in range(blocks))
+
+        coil_blocks = spoke_blocks
+        spokes, coil_data, maps = gather(bundle[data_rows:]), gather(bundle[:data_rows]), gather(own_map)
         share = live_total // blocks
         first_of = lambda: (lax.axis_index("tile") * n_spk + lax.axis_index("spk")) * share
 
@@ -379,33 +495,35 @@
 
     per_group = min(GROUP, share)
     groups, span, side_rows = share // per_group, per_group * ro // 2, n // 2 + 2 * MARGIN
-    dft = jnp.asarray(dft_tables(n))
-    haar = jnp.asarray(haar_tables(n))
     image = jax.ShapeDtypeStruct((2, n, n), F32)
     weighted = pltpu.VMEM((groups, 2, 2, span), F32)
     gridded = pltpu.VMEM((2, 2 * side_rows, n), F32)
-    vmem = pl.BlockSpec(memory_space=pltpu.VMEM)
-    smem = pl.BlockSpec(memory_space=pltpu.SMEM)
-    row_tab, col_tab, data, back = pl.pallas_call(
-        functools.partial(first_kernel, share, first_of, places_of, live_total, len(spokes), spk_dev, fields, n),
+    row_tab, col_tab, flags, live = pl.pallas_call(
+        functools.partial(table_kernel, first_of, spoke_blocks, live_total, len(spokes), spk_dev, n),
         out_shape=[
             jax.ShapeDtypeStruct((groups, n, 2 * span), BF16),
             jax.ShapeDtypeStruct((groups, 2, side_rows, span), BF16),
+            jax.ShapeDtypeStruct((groups, 2, 2, span), F32),
+            jax.ShapeDtypeStruct((2, blocks * spk_dev + 1), jnp.int32),
+        ],
+        in_specs=[vmem] * len(spokes),
+        out_specs=[vmem, vmem, vmem, smem],
+        scratch_shapes=[pltpu.VMEM((blocks, spoke_rows, ro), F32)],
+        compiler_params=PARAMS,
+    )(*spokes)
+    data, back = pl.pallas_call(
+        functools.partial(first_kernel, first_of, coil_blocks, len(coil_data), spk_dev),
+        out_shape=[
             jax.ShapeDtypeStruct((groups, 2, 3, span), F32),
             jax.ShapeDtypeStruct((2 * n, n), F32),
         ],
-        in_specs=[vmem] * (len(spokes) + 1),
-        out_specs=[vmem] * 4,
-        scratch_shapes=[
-            pltpu.VMEM((blocks, fields * spk_dev, ro), F32),
-            weighted,
-            gridded,
-            pltpu.SMEM((2, blocks * spk_dev + 1), jnp.int32),
-        ],
+        in_specs=[vmem] * len(coil_data) + [smem] + [vmem] * 4,
+        out_specs=[vmem] * 2,
+        scratch_shapes=[pltpu.VMEM((blocks, data_rows, ro), F32), weighted, gridded],
         compiler_params=PARAMS,
-    )(*spokes, dft)
+    )(*coil_data, live, flags, row_tab, col_tab, dft)
     map_t, part = pl.pallas_call(
-        functools.partial(map_kernel, places_of, len(maps)),
+        functools.partial(map_kernel, coil_blocks, len(maps)),
         out_shape=[image, image],
         in_specs=[vmem] * (len(maps) + 1),
         out_specs=[vmem, vmem],
@@ -419,20 +537,20 @@
         *estimate, part = pl.pallas_call(
             functools.partial(step_kernel, len(estimate), len(parts)),
             out_shape=[image, image],
-            in_specs=[smem] + [vmem] * len(inputs),
+            in_specs=[vmem] * (len(inputs) + 1),
             out_specs=[vmem, vmem],
             scratch_shapes=[pltpu.VMEM((2, 2 * side_rows, n), BF16), weighted, gridded],
             compiler_params=PARAMS,
-        )(thresholds, *inputs)
+        )(limits, *inputs)
         parts = parts_of(part)
     mine_of = lambda: lax.axis_index("tile") * n_spk + lax.axis_index("spk")
     return pl.pallas_call(
         functools.partial(last_kernel, len(parts), rows, mine_of),
         out_shape=jax.ShapeDtypeStruct((rows, 2, n), F32),
-        in_specs=[smem] + [vmem] * (len(parts) + 2),
+        in_specs=[vmem] * (len(parts) + 3),
         out_specs=vmem,
         compiler_params=PARAMS,
-    )(thresholds, *estimate, *parts, haar)
+    )(limits, *estimate, *parts, haar)
 
 
 def solution(mesh):
@@ -444,6 +562,7 @@
         P(("grp", "tile", "spk")),
         P(),
     )
+
     return jax.shard_map(
         local,
         mesh=mesh,

time: 79.1 us -> 72.6 us (0.918)
  waiting for transfers between devices: 15.5 us -> 8.59 us
  starting transfers between devices: 15.1 us -> 18.1 us
  other arithmetic: 2.37 us -> 0 us
    ppermute x6, waiting for transfers between devices: 7.34 us -> 2.43 us  [spread(): lax.ppermute(value, 'tile', [(i, (i + shift) % n_tile) for i in range(n_t...]
    ppermute x8 -> x9, waiting for transfers between devices: 8.18 us -> 6.16 us  [the longest x4 6.15 us: parts_of(): return [part, lax.ppermute(part, 'spk', swap)]]
    ppermute x8 -> x9, starting transfers between devices: 6.28 us -> 8.02 us  [the longest x4 3.22 us: parts_of(): return [part, lax.ppermute(part, 'spk', swap)]]
    pallas_call x2 -> x7, Pallas kernels: 9.37 us -> 11.1 us  [the longest x1 5.46 us: local(): pl.pallas_call(functools.partial(table_kernel, first_of, spoke_blocks, li...]
    pallas_call x3, Pallas kernels: 27.4 us -> 25.7 us  [local(): pl.pallas_call(functools.partial(step_kernel, len(estimate), len(parts)),...]
    unnamed x2 -> x0, other arithmetic: 1.41 us -> none
    ppermute x6, starting transfers between devices: 8.86 us -> 10.1 us  [spread(): lax.ppermute(value, 'tile', [(i, (i + shift) % n_tile) for i in range(n_t...]
    another operation x4 -> x0, other arithmetic: 0.96 us -> none  [collect(): return jnp.stack([jnp.where(is_own, value, far), near])]
  transfers between devices with their start and end apart: 14 -> 15, of which waited for: 8 -> 6; matrix products, arithmetic and copies ran while one was open for 1% -> 0% of each run, Pallas kernels for 11% -> 15%
where the time goes in v4:
time: 72.6 us; the launch traced here: 72.2 us
  Pallas kernels  38.9 us (54%)
  starting transfers between devices  18.1 us (25%)
  waiting for transfers between devices  8.59 us (12%)
  local copies, waits for them, and re-layouts  5.79 us (8%)
  between operations  0.83 us (1%)
    pallas_call x3, Pallas kernels, local(): pl.pallas_call(functools.partial(step_kernel, len(estimate), len(parts)),...  25.7 us
    ppermute x6, starting transfers between devices, spread(): lax.ppermute(value, 'tile', [(i, (i + shift) % n_tile) for i in range(n_t...  10.1 us
    ppermute x4, waiting for transfers between devices, parts_of(): return [part, lax.ppermute(part, 'spk', swap)]  6.15 us
    unnamed x14, local copies, waits for them, and re-layouts  5.79 us
    pallas_call x1, Pallas kernels, local(): pl.pallas_call(functools.partial(table_kernel, first_of, spoke_blocks, li...  5.46 us
    pallas_call x1, Pallas kernels, local(): pl.pallas_call(functools.partial(first_kernel, first_of, coil_blocks, len...  4.5 us
    ppermute x4, starting transfers between devices, parts_of(): return [part, lax.ppermute(part, 'spk', swap)]  3.22 us
    ppermute x6, waiting for transfers between devices, spread(): lax.ppermute(value, 'tile', [(i, (i + shift) % n_tile) for i in range(n_t...  2.43 us
  transfers between devices with their start and end apart: 15, of which 6 were waited for; matrix products, arithmetic and copies ran while one was open for 0% of the time, Pallas kernels for 15%

profile of v4, /device:TPU:0, one launch (start us, length us, event | category | flops | bytes accessed | tf_op | source)
XLA Modules:
  0.0 72.2 jit_solution(11200224877614819066)
XLA Ops:
  0.7 0.0 copy-start.3
  0.7 0.7 %copy-done.3 = bf16[8,6,256]{2,0,1:T(8,128)(2,1)S(1)} copy-done((bf16[8,6,256]{2,0,1:T(8,128)(2,1)S(1)}, bf16[8,6,256]{2,0,1:T(8,128)(2,1)}, u32[]{:S(2)}) %copy-start.3) | copy-done | bytes 24600
  1.4 0.0 copy-start.4
  1.4 0.7 copy-done.4
  2.1 0.7 copy-done.5
  2.8 5.1 %collective-permute-start.2 = (bf16[88,256]{1,0:T(8,128)(2,1)S(1)}, bf16[88,256]{1,0:T(8,128)(2,1)S(1)}, u32[]{:S(2)}, u32[]{:S(2)}) collective-permute-start(bf16[88,256]{1,0:T(8,128)(2,1)S(1)} %shard_map.82.refs_0_), channel_id=1, source_target_pairs={{0,12},{4,0},{8,4},{12,8},{1,13},{5,1},{9,5},{13,9},{2,14},{6,2},{... | collective-permute-start | bytes 135176 | tf_op jit(solution)/shard_map/ppermute | solution.py:425
  7.9 0.4 collective-permute-start.5
  8.4 0.0 collective-permute-start.4
  8.4 1.6 %collective-permute-start.3 = (f32[32,2,256]{2,1,0:T(2,128)}, f32[32,2,256]{2,1,0:T(2,128)S(1)}, u32[]{:S(2)}, u32[]{:S(2)}) collective-permute-start(f32[32,2,256]{2,1,0:T(2,128)} %bitcast.5), channel_id=1, source_target_pairs={{0,4},{4,8},{8,12},{12,0},{1,5},{5,9},{9,13},{13,1},{2,6},{6,10},{... | collective-permute-start | bytes 196616 | tf_op jit(solution)/shard_map/ppermute | solution.py:425
  10.0 2.9 %collective-permute-start.1 = (bf16[88,256]{1,0:T(8,128)(2,1)S(1)}, bf16[88,256]{1,0:T(8,128)(2,1)S(1)}, u32[]{:S(2)}, u32[]{:S(2)}) collective-permute-start(bf16[88,256]{1,0:T(8,128)(2,1)S(1)} %shard_map.82.refs_0_), channel_id=1, source_target_pairs={{0,8},{4,12},{8,0},{12,4},{1,9},{5,13},{9,1},{13,5},{2,10},{6,14},... | collective-permute-start | bytes 135176 | tf_op jit(solution)/shard_map/ppermute | solution.py:425
  12.9 0.0 collective-permute-done.2.refs_3_
  12.9 0.0 collective-permute-start
  12.9 1.1 %copy-done = bf16[6,256,256]{2,1,0:T(8,128)(2,1)S(1)} copy-done((bf16[6,256,256]{2,1,0:T(8,128)(2,1)S(1)}, bf16[6,256,256]{2,1,0:T(8,128)(2,1)}, u32[]{:S(2)}) %copy-start) | copy-done | bytes 786456
  14.0 1.0 %copy-done.1 = bf16[4,256,256]{2,1,0:T(8,128)(2,1)S(1)} copy-done((bf16[4,256,256]{2,1,0:T(8,128)(2,1)S(1)}, bf16[4,256,256]{2,1,0:T(8,128)(2,1)}, u32[]{:S(2)}) %copy-start.1) | copy-done | bytes 524312
  15.1 0.7 copy-done.6
  15.7 0.6 shard_map.83
  16.4 2.0 %collective-permute-done.1.refs_2_ = bf16[88,256]{1,0:T(8,128)(2,1)S(1)} collective-permute-done((bf16[88,256]{1,0:T(8,128)(2,1)S(1)}, bf16[88,256]{1,0:T(8,128)(2,1)S(1)}, u32[]{:S(2)}, u32[]{:S(2)}) %collective-permute-start.1) | collective-permute-done | bytes 45088 | tf_op jit(solution)/shard_map/ppermute | solution.py:425
  18.3 0.5 collective-permute-done.refs_1_
  18.8 0.0 collective-permute-done.5.refs_3_
  18.8 0.0 collective-permute-done.4.refs_2_
  18.8 0.0 collective-permute-done.3.refs_1_
  18.8 0.0 copy-start.2
  18.8 0.8 %copy-done.2 = f32[1,32,2,256]{3,2,1,0:T(2,128)S(1)} copy-done((f32[1,32,2,256]{3,2,1,0:T(2,128)S(1)}, f32[1,32,2,256]{3,2,1,0:T(2,128)}, u32[]{:S(2)}) %copy-start.2) | copy-done | bytes 65560
  19.7 1.5 %collective-permute-start.7 = (f32[4,32,2,256]{3,2,1,0:T(2,128)S(1)}, f32[4,32,2,256]{3,2,1,0:T(2,128)S(1)}, u32[]{:S(2)}, u32[]{:S(2)}) collective-permute-start(f32[4,32,2,256]{3,2,1,0:T(2,128)S(1)} %shard_map.85.refs_0_), channel_id=1, source_target_pairs={{0,2},{3,1},{1,0},{2,3},{4,6},{7,5},{5,4},{6,7},{8,10},{11,9},{9,8... | collective-permute-start | bytes 786440 | tf_op jit(solution)/shard_map/ppermute | solution.py:429
  21.2 0.7 collective-permute-start.6
  21.9 1.4 %collective-permute-start.10 = (bf16[4,72,256]{2,1,0:T(8,128)(2,1)S(1)}, bf16[4,72,256]{2,1,0:T(8,128)(2,1)S(1)}, u32[]{:S(2)}, u32[]{:S(2)}) collective-permute-start(bf16[4,72,256]{2,1,0:T(8,128)(2,1)S(1)} %get-tuple-element.52.refs_0_), channel_id=1, source_target_pairs={{0,1},{1,0},{2,3},{3,2},{4,5},{5,4},{6,7},{7,6},{8,9},{9,8},{10,11... | collective-permute-start | bytes 442376 | tf_op jit(solution)/shard_map/ppermute | solution.py:465
  23.3 0.5 collective-permute-start.9
  23.9 0.7 collective-permute-start.8
  24.5 0.0 collective-permute-done.10.refs_1_
  24.5 5.5 %shard_map.86 = (bf16[4,256,2048]{2,1,0:T(8,128)(2,1)S(1)}, bf16[4,2,144,1024]{3,2,1,0:T(8,128)(2,1)S(1)}, f32[4,2,2,1024]{3,2,1,0:T(2,128)S(1)}, s32[2,65]{1,0:T(2,128)S(1)}) custom-call(bf16[4,72,256]{2,1,0:T(8,128)(2,1)S(1)} %get-tuple-element.52.refs_0_, bf16[4,72,256]{2,1,0:T(8,128)(2,1)S(1)} %collective-permute-done.10.refs_1_), custom_call_target="tpu_custom_call" | custom-call | tf_op jit(solution)/shard_map/pallas_call | solution.py:501
  30.0 0.0 collective-permute-done.9.refs_2_
  30.0 0.0 collective-permute-done.8.refs_1_
  30.0 4.5 %shard_map.87 = (f32[4,2,3,1024]{3,2,1,0:T(4,128)S(1)}, f32[512,256]{1,0:T(8,128)S(1)}) custom-call(bf16[4,16,256]{2,1,0:T(8,128)(2,1)S(1)} %get-tuple-element.47.refs_0_, bf16[4,16,256]{2,1,0:T(8,128)(2,1)S(1)} %collective-permute-done.8.refs_1_, bf16[4,16,256]{2,1,0:T(8,128)(2,1)S(1)} %collective-permute-done.9.refs_2_, ...), custom_call_target="tpu_custom_call" | custom-call | tf_op jit(solution)/shard_map/pallas_call | solution.py:514
  34.5 0.0 collective-permute-done.7.refs_2_
  34.5 0.0 collective-permute-done.6.refs_1_
  34.5 0.5 shard_map.88
  35.0 1.9 %collective-permute-start.11 = (f32[2,256,256]{2,1,0:T(8,128)S(1)}, f32[2,256,256]{2,1,0:T(8,128)S(1)}, u32[]{:S(2)}, u32[]{:S(2)}) collective-permute-start(f32[2,256,256]{2,1,0:T(8,128)S(1)} %get-tuple-element.59.refs_1_), channel_id=1, source_target_pairs={{0,1},{1,0},{2,3},{3,2},{4,5},{5,4},{6,7},{7,6},{8,9},{9,8},{10,11... | collective-permute-start | bytes 1572872 | tf_op jit(solution)/shard_map/ppermute | solution.py:480
  36.9 1.5 %collective-permute-done.11.refs_2_ = f32[2,256,256]{2,1,0:T(8,128)S(1)} collective-permute-done((f32[2,256,256]{2,1,0:T(8,128)S(1)}, f32[2,256,256]{2,1,0:T(8,128)S(1)}, u32[]{:S(2)}, u32[]{:S(2)}) %collective-permute-start.11) | collective-permute-done | bytes 524320 | tf_op jit(solution)/shard_map/ppermute | solution.py:480
  38.4 8.5 %shard_map.89 = (f32[2,256,256]{2,1,0:T(8,128)S(1)}, f32[2,256,256]{2,1,0:T(8,128)S(1)}) custom-call(f32[3,256]{1,0:T(4,128)S(1)} %get-tuple-element.40.refs_0_.thr_ref, f32[2,256,256]{2,1,0:T(8,128)S(1)} %get-tuple-element.59.refs_1_, f32[2,256,256]{2,1,0:T(8,128)S(1)} %collective-permute-done.11.refs_2_, ...), custom_call_target="tpu_custom_call" | custom-call | tf_op jit(solution)/shard_map/pallas_call | solution.py:537
  47.0 0.4 collective-permute-start.12
  47.4 1.5 %collective-permute-done.12.refs_3_ = f32[2,256,256]{2,1,0:T(8,128)S(1)} collective-permute-done((f32[2,256,256]{2,1,0:T(8,128)S(1)}, f32[2,256,256]{2,1,0:T(8,128)S(1)}, u32[]{:S(2)}, u32[]{:S(2)}) %collective-permute-start.12) | collective-permute-done | bytes 524320 | tf_op jit(solution)/shard_map/ppermute | solution.py:480
  49.0 8.7 %shard_map.90 = (f32[2,256,256]{2,1,0:T(8,128)S(1)}, f32[2,256,256]{2,1,0:T(8,128)S(1)}) custom-call(f32[3,256]{1,0:T(4,128)S(1)} %get-tuple-element.40.refs_0_.thr_ref, f32[2,256,256]{2,1,0:T(8,128)S(1)} %get-tuple-element.63.refs_1_, f32[2,256,256]{2,1,0:T(8,128)S(1)} %get-tuple-element.64.refs_2_, f32[2,256,256]{2,1,0:T(8,128)S(1)} %collective-permute-done.12.refs_3_, ...), custom_call_target="tpu_custom_call" | custom-call | tf_op jit(solution)/shard_map/pallas_call | solution.py:537
  57.6 0.4 collective-permute-start.13
  58.1 1.5 %collective-permute-done.13.refs_3_ = f32[2,256,256]{2,1,0:T(8,128)S(1)} collective-permute-done((f32[2,256,256]{2,1,0:T(8,128)S(1)}, f32[2,256,256]{2,1,0:T(8,128)S(1)}, u32[]{:S(2)}, u32[]{:S(2)}) %collective-permute-start.13) | collective-permute-done | bytes 524320 | tf_op jit(solution)/shard_map/ppermute | solution.py:480
  59.6 8.5 %shard_map.91 = (f32[2,256,256]{2,1,0:T(8,128)S(1)}, f32[2,256,256]{2,1,0:T(8,128)S(1)}) custom-call(f32[3,256]{1,0:T(4,128)S(1)} %get-tuple-element.40.refs_0_.thr_ref, f32[2,256,256]{2,1,0:T(8,128)S(1)} %get-tuple-element.65.refs_1_, f32[2,256,256]{2,1,0:T(8,128)S(1)} %get-tuple-element.66.refs_2_, f32[2,256,256]{2,1,0:T(8,128)S(1)} %collective-permute-done.13.refs_3_, ...), custom_call_target="tpu_custom_call" | custom-call | tf_op jit(solution)/shard_map/pallas_call | solution.py:537
  68.2 0.4 collective-permute-start.14
  68.6 1.5 %collective-permute-done.14.refs_1_ = f32[2,256,256]{2,1,0:T(8,128)S(1)} collective-permute-done((f32[2,256,256]{2,1,0:T(8,128)S(1)}, f32[2,256,256]{2,1,0:T(8,128)S(1)}, u32[]{:S(2)}, u32[]{:S(2)}) %collective-permute-start.14) | collective-permute-done | bytes 524320 | tf_op jit(solution)/shard_map/ppermute | solution.py:480
  70.1 2.0 %shard_map.92 = f32[32,2,256]{2,1,0:T(2,128)} custom-call(f32[3,256]{1,0:T(4,128)S(1)} %get-tuple-element.40.refs_0_.thr_ref, f32[2,256,256]{2,1,0:T(8,128)S(1)} %get-tuple-element.67.est_ref, f32[2,256,256]{2,1,0:T(8,128)S(1)} %get-tuple-element.68.refs_0_, f32[2,256,256]{2,1,0:T(8,128)S(1)} %collective-permute-done.14.refs_1_, ...), custom_call_target="tpu_custom_call" | custom-call | tf_op jit(solution)/shard_map/pallas_call | solution.py:547
  (7 shorter events, 0.1 us)
Async XLA Ops:
  0.7 0.7 %copy-start.3 = (bf16[8,6,256]{2,0,1:T(8,128)(2,1)S(1)}, bf16[8,6,256]{2,0,1:T(8,128)(2,1)}, u32[]{:S(2)}) copy-start(bf16[8,6,256]{2,0,1:T(8,128)(2,1)} %param.10) | copy-start | bytes 73732
  1.4 0.7 copy-start.4
  2.1 0.7 copy-start.5
  2.8 10.1 %collective-permute-start.2 = (bf16[88,256]{1,0:T(8,128)(2,1)S(1)}, bf16[88,256]{1,0:T(8,128)(2,1)S(1)}, u32[]{:S(2)}, u32[]{:S(2)}) collective-permute-start(bf16[88,256]{1,0:T(8,128)(2,1)S(1)} %shard_map.82.refs_0_), channel_id=1, source_target_pairs={{0,12},{4,0},{8,4},{12,8},{1,13},{5,1},{9,5},{13,9},{2,14},{6,2},{... | collective-permute-start | bytes 135176 | tf_op jit(solution)/shard_map/ppermute | solution.py:425
  7.9 10.9 %collective-permute-start.5 = (f32[32,2,256]{2,1,0:T(2,128)}, f32[32,2,256]{2,1,0:T(2,128)S(1)}, u32[]{:S(2)}, u32[]{:S(2)}) collective-permute-start(f32[32,2,256]{2,1,0:T(2,128)} %bitcast.3), channel_id=1, source_target_pairs={{0,12},{4,0},{8,4},{12,8},{1,13},{5,1},{9,5},{13,9},{2,14},{6,2},{... | collective-permute-start | bytes 196616 | tf_op jit(solution)/shard_map/ppermute | solution.py:425
  8.4 10.4 %collective-permute-start.4 = (f32[32,2,256]{2,1,0:T(2,128)}, f32[32,2,256]{2,1,0:T(2,128)S(1)}, u32[]{:S(2)}, u32[]{:S(2)}) collective-permute-start(f32[32,2,256]{2,1,0:T(2,128)} %bitcast.4), channel_id=1, source_target_pairs={{0,8},{4,12},{8,0},{12,4},{1,9},{5,13},{9,1},{13,5},{2,10},{6,14},... | collective-permute-start | bytes 196616 | tf_op jit(solution)/shard_map/ppermute | solution.py:425
  8.4 10.4 %collective-permute-start.3 = (f32[32,2,256]{2,1,0:T(2,128)}, f32[32,2,256]{2,1,0:T(2,128)S(1)}, u32[]{:S(2)}, u32[]{:S(2)}) collective-permute-start(f32[32,2,256]{2,1,0:T(2,128)} %bitcast.5), channel_id=1, source_target_pairs={{0,4},{4,8},{8,12},{12,0},{1,5},{5,9},{9,13},{13,1},{2,6},{6,10},{... | collective-permute-start | bytes 196616 | tf_op jit(solution)/shard_map/ppermute | solution.py:425
  10.0 8.3 %collective-permute-start.1 = (bf16[88,256]{1,0:T(8,128)(2,1)S(1)}, bf16[88,256]{1,0:T(8,128)(2,1)S(1)}, u32[]{:S(2)}, u32[]{:S(2)}) collective-permute-start(bf16[88,256]{1,0:T(8,128)(2,1)S(1)} %shard_map.82.refs_0_), channel_id=1, source_target_pairs={{0,8},{4,12},{8,0},{12,4},{1,9},{5,13},{9,1},{13,5},{2,10},{6,14},... | collective-permute-start | bytes 135176 | tf_op jit(solution)/shard_map/ppermute | solution.py:425
  12.9 5.9 %collective-permute-start = (bf16[88,256]{1,0:T(8,128)(2,1)S(1)}, bf16[88,256]{1,0:T(8,128)(2,1)S(1)}, u32[]{:S(2)}, u32[]{:S(2)}) collective-permute-start(bf16[88,256]{1,0:T(8,128)(2,1)S(1)} %shard_map.82.refs_0_), channel_id=1, source_target_pairs={{0,4},{4,8},{8,12},{12,0},{1,5},{5,9},{9,13},{13,1},{2,6},{6,10},{... | collective-permute-start | bytes 135176 | tf_op jit(solution)/shard_map/ppermute | solution.py:425
  12.9 1.1 %copy-start = (bf16[6,256,256]{2,1,0:T(8,128)(2,1)S(1)}, bf16[6,256,256]{2,1,0:T(8,128)(2,1)}, u32[]{:S(2)}) copy-start(bf16[6,256,256]{2,1,0:T(8,128)(2,1)} %constant.4.clone.dft_ref) | copy-start | bytes 2359300
  14.0 1.0 %copy-start.1 = (bf16[4,256,256]{2,1,0:T(8,128)(2,1)S(1)}, bf16[4,256,256]{2,1,0:T(8,128)(2,1)}, u32[]{:S(2)}) copy-start(bf16[4,256,256]{2,1,0:T(8,128)(2,1)} %constant.5.clone.haar_ref) | copy-start | bytes 1572868
  15.1 0.7 copy-start.6
  18.8 0.8 %copy-start.2 = (f32[1,32,2,256]{3,2,1,0:T(2,128)S(1)}, f32[1,32,2,256]{3,2,1,0:T(2,128)}, u32[]{:S(2)}) copy-start(f32[1,32,2,256]{3,2,1,0:T(2,128)} %param.8) | copy-start | bytes 196612
  19.7 14.8 %collective-permute-start.7 = (f32[4,32,2,256]{3,2,1,0:T(2,128)S(1)}, f32[4,32,2,256]{3,2,1,0:T(2,128)S(1)}, u32[]{:S(2)}, u32[]{:S(2)}) collective-permute-start(f32[4,32,2,256]{3,2,1,0:T(2,128)S(1)} %shard_map.85.refs_0_), channel_id=1, source_target_pairs={{0,2},{3,1},{1,0},{2,3},{4,6},{7,5},{5,4},{6,7},{8,10},{11,9},{9,8... | collective-permute-start | bytes 786440 | tf_op jit(solution)/shard_map/ppermute | solution.py:429
  21.2 13.3 %collective-permute-start.6 = (f32[4,32,2,256]{3,2,1,0:T(2,128)S(1)}, f32[4,32,2,256]{3,2,1,0:T(2,128)S(1)}, u32[]{:S(2)}, u32[]{:S(2)}) collective-permute-start(f32[4,32,2,256]{3,2,1,0:T(2,128)S(1)} %shard_map.85.refs_0_), channel_id=1, source_target_pairs={{1,2},{2,1},{5,6},{6,5},{9,10},{10,9},{13,14},{14,13},{17,18},{18,... | collective-permute-start | bytes 786440 | tf_op jit(solution)/shard_map/ppermute | solution.py:429
  21.9 2.6 %collective-permute-start.10 = (bf16[4,72,256]{2,1,0:T(8,128)(2,1)S(1)}, bf16[4,72,256]{2,1,0:T(8,128)(2,1)S(1)}, u32[]{:S(2)}, u32[]{:S(2)}) collective-permute-start(bf16[4,72,256]{2,1,0:T(8,128)(2,1)S(1)} %get-tuple-element.52.refs_0_), channel_id=1, source_target_pairs={{0,1},{1,0},{2,3},{3,2},{4,5},{5,4},{6,7},{7,6},{8,9},{9,8},{10,11... | collective-permute-start | bytes 442376 | tf_op jit(solution)/shard_map/ppermute | solution.py:465
  23.3 6.7 %collective-permute-start.9 = (bf16[4,16,256]{2,1,0:T(8,128)(2,1)S(1)}, bf16[4,16,256]{2,1,0:T(8,128)(2,1)S(1)}, u32[]{:S(2)}, u32[]{:S(2)}) collective-permute-start(bf16[4,16,256]{2,1,0:T(8,128)(2,1)S(1)} %get-tuple-element.47.refs_0_), channel_id=1, source_target_pairs={{0,2},{3,1},{1,0},{2,3},{4,6},{7,5},{5,4},{6,7},{8,10},{11,9},{9,8... | collective-permute-start | bytes 98312 | tf_op jit(solution)/shard_map/ppermute | solution.py:429
  23.9 6.1 %collective-permute-start.8 = (bf16[4,16,256]{2,1,0:T(8,128)(2,1)S(1)}, bf16[4,16,256]{2,1,0:T(8,128)(2,1)S(1)}, u32[]{:S(2)}, u32[]{:S(2)}) collective-permute-start(bf16[4,16,256]{2,1,0:T(8,128)(2,1)S(1)} %get-tuple-element.47.refs_0_), channel_id=1, source_target_pairs={{1,2},{2,1},{5,6},{6,5},{9,10},{10,9},{13,14},{14,13},{17,18},{18,... | collective-permute-start | bytes 98312 | tf_op jit(solution)/shard_map/ppermute | solution.py:429
  35.0 3.4 %collective-permute-start.11 = (f32[2,256,256]{2,1,0:T(8,128)S(1)}, f32[2,256,256]{2,1,0:T(8,128)S(1)}, u32[]{:S(2)}, u32[]{:S(2)}) collective-permute-start(f32[2,256,256]{2,1,0:T(8,128)S(1)} %get-tuple-element.59.refs_1_), channel_id=1, source_target_pairs={{0,1},{1,0},{2,3},{3,2},{4,5},{5,4},{6,7},{7,6},{8,9},{9,8},{10,11... | collective-permute-start | bytes 1572872 | tf_op jit(solution)/shard_map/ppermute | solution.py:480
  47.0 2.0 %collective-permute-start.12 = (f32[2,256,256]{2,1,0:T(8,128)S(1)}, f32[2,256,256]{2,1,0:T(8,128)S(1)}, u32[]{:S(2)}, u32[]{:S(2)}) collective-permute-start(f32[2,256,256]{2,1,0:T(8,128)S(1)} %get-tuple-element.64.refs_2_), channel_id=1, source_target_pairs={{0,1},{1,0},{2,3},{3,2},{4,5},{5,4},{6,7},{7,6},{8,9},{9,8},{10,11... | collective-permute-start | bytes 1572872 | tf_op jit(solution)/shard_map/ppermute | solution.py:480
  57.6 2.0 %collective-permute-start.13 = (f32[2,256,256]{2,1,0:T(8,128)S(1)}, f32[2,256,256]{2,1,0:T(8,128)S(1)}, u32[]{:S(2)}, u32[]{:S(2)}) collective-permute-start(f32[2,256,256]{2,1,0:T(8,128)S(1)} %get-tuple-element.66.refs_2_), channel_id=1, source_target_pairs={{0,1},{1,0},{2,3},{3,2},{4,5},{5,4},{6,7},{7,6},{8,9},{9,8},{10,11... | collective-permute-start | bytes 1572872 | tf_op jit(solution)/shard_map/ppermute | solution.py:480
  68.2 2.0 %collective-permute-start.14 = (f32[2,256,256]{2,1,0:T(8,128)S(1)}, f32[2,256,256]{2,1,0:T(8,128)S(1)}, u32[]{:S(2)}, u32[]{:S(2)}) collective-permute-start(f32[2,256,256]{2,1,0:T(8,128)S(1)} %get-tuple-element.68.refs_0_), channel_id=1, source_target_pairs={{0,1},{1,0},{2,3},{3,2},{4,5},{5,4},{6,7},{7,6},{8,9},{9,8},{10,11... | collective-permute-start | bytes 1572872 | tf_op jit(solution)/shard_map/ppermute | solution.py:480

commit v5 on v4

--- a/solution.py
+++ b/solution.py
@@ -100,7 +100,7 @@
     return out
 
 
-def shrink(re, im, thr_ref, haar, last_rows=None):
+def shrink(re, im, thr_ref, const, last_rows=None):
     n = re.shape[0]
     block = 2**LEVELS
     col_pos = lax.broadcasted_iota(jnp.int32, (n, 1), 0)
@@ -113,18 +113,18 @@
     for level in range(LEVELS):
         limits = jnp.where(band == level + 1, thr_ref[level : level + 1, :], limits)
     scale = col_scale * row_scale
-    half = mm(joined([haar[0]] * 2, 1), joined(split2(joined([re, im], 1)), 0))
+    half = mm(joined([const[6]] * 2, 1), joined(split2(joined([re, im], 1)), 0))
     half = joined([half[:, :n], half[:, n:]], 0)
-    full = mm(joined(split2(half), 1), joined([haar[2]] * 2, 0))
+    full = mm(joined(split2(half), 1), joined([const[8]] * 2, 0))
     coeffs = [full[:n] * scale, full[n:] * scale]
     magnitude = jnp.sqrt(coeffs[0] * coeffs[0] + coeffs[1] * coeffs[1])
     factor = jnp.maximum(magnitude - limits, 0.0) / jnp.maximum(magnitude, limits)
     factor = jnp.where(band <= LEVELS, factor, 1.0) * scale
     kept = joined([coeffs[0] * factor, coeffs[1] * factor], 1)
-    half = mm(joined([haar[1]] * 2, 1), joined(split2(kept), 0))
+    half = mm(joined([const[7]] * 2, 1), joined(split2(kept), 0))
     half = joined([half[:, :n], half[:, n:]], 0)
     if last_rows is None:
-        full = mm(joined(split2(half), 1), joined([haar[3]] * 2, 0))
+        full = mm(joined(split2(half), 1), joined([const[9]] * 2, 0))
         return full[:n], full[n:]
     full = mm_t(joined([last_rows] * 2, 1), joined(split2(half), 1))
     return full[:, :n], full[:, n:]
@@ -203,102 +203,75 @@
         refs[-1][i] = piece[...]
 
 
-def constants_kernel(thr_ref, dft_ref, haar_ref, thr_out, dft_out, haar_out):
+def constants_kernel(thr_ref, const_ref, thr_out, const_out):
     for level in range(LEVELS):
         thr_out[level : level + 1, :] = jnp.full((1, thr_out.shape[1]), thr_ref[level])
-    dft_out[...] = dft_ref[...]
-    haar_out[...] = haar_ref[...]
-
-
-def live_list(slots, spk_dev, list_s):
+    const_out[...] = const_ref[...]
+
+
+def first_kernel(first_of, spoke_blocks, coil_blocks, live_total, counts, spk_dev, n, *refs):
+    spoke_refs, data_refs, refs = refs[: counts[0]], refs[counts[0] : sum(counts)], refs[sum(counts) :]
+    const_ref, rows_s, cols_s, data_out, back_out, slots, weighted_s, grid_s, list_s = refs
+    spoke_rows = slots.shape[1] - 2 * spk_dev
+    ro = slots.shape[-1]
+    groups, _, _, span = weighted_s.shape
+    per_group, half = 2 * span // ro, ro // 2
+    for place, value in spoke_blocks(spoke_refs):
+        slots[place, 0:spoke_rows] = value.astype(F32)
+    for place, value in coil_blocks(data_refs):
+        slots[place, spoke_rows:] = value.astype(F32)
     taken = jnp.int32(0)
     for block in range(slots.shape[0]):
-        count = jnp.max(slots[block, slots.shape[1] - spk_dev :, :]).astype(jnp.int32)
+        count = jnp.max(slots[block, spoke_rows - spk_dev : spoke_rows, :]).astype(jnp.int32)
         for depth in range(spk_dev):
             list_s[0, taken] = block
             list_s[1, taken] = depth
             taken = taken + (depth < count).astype(jnp.int32)
-
-
-def table_kernel(first_of, blocks_of, live_total, pieces, spk_dev, n, *refs):
-    spoke_refs, refs = refs[:pieces], refs[pieces:]
-    rows_s, cols_s, flags_out, list_out, slots = refs
-    ro = slots.shape[-1]
-    groups, _, _, span = flags_out.shape
-    per_group, half = 2 * span // ro, ro // 2
-    for place, value in blocks_of(spoke_refs):
-        slots[place] = value.astype(F32)
-    live_list(slots, spk_dev, list_out)
     start = first_of()
     density = density_of(ro, n, live_total)
-    row_cells = lax.broadcasted_iota(jnp.int32, (n, ro), 0).astype(F32)
+    row_cells = lax.broadcasted_iota(jnp.int32, (n, ro), 0).astype(F32).astype(BF16)
     side_rows = n // 2 + 2 * MARGIN
     low_cells = lax.broadcasted_iota(jnp.int32, (side_rows, half), 0) + (n - MARGIN)
-    side_cells = [((low_cells + side * (n // 2)) % n).astype(F32) for side in range(2)]
+    side_cells = [((low_cells + side * (n // 2)) % n).astype(F32).astype(BF16) for side in range(2)]
+    grid_s[...] = jnp.zeros_like(grid_s)
 
     def table(cells, at, weights):
         before = jnp.where(at == 0, n - 1.0, at - 1)
         after = jnp.where(at == n - 1, 0.0, at + 1)
-        out = jnp.where(cells == after, weights[2], 0.0)
+        before, at, after = (t.astype(BF16) for t in (before, at, after))
+        weights = [w.astype(BF16) for w in weights]
+        out = jnp.where(cells == after, weights[2], jnp.zeros((), BF16))
         out = jnp.where(cells == at, weights[1], out)
-        return jnp.where(cells == before, weights[0], out).astype(BF16)
-
-    def build(group, carry):
+        return jnp.where(cells == before, weights[0], out)
+
+    def build(group):
         for j in range(per_group):
             which = start + group * per_group + j
-            block, depth = list_out[0, which], list_out[1, which]
-            slot = [slots[block, pl.ds(f * spk_dev + depth, 1), :] for f in range(8)]
+            block, depth = list_s[0, which], list_s[1, which]
+            slot = [slots[block, pl.ds(f * spk_dev + depth, 1), :] for f in (0, 1, 2, 3, 4, 5, 6, 7, 9, 10)]
             low_first = slot[7][:, 1:2] <= n // 2
-            slot = slot + [density, jnp.where(low_first, jnp.ones_like(density), 0.0)]
-            slot = [jnp.where(low_first, f, joined([f[:, half:], f[:, :half]], 1)) for f in slot]
+            slot = [jnp.where(low_first, f, joined([f[:, half:], f[:, :half]], 1)) for f in slot + [density]]
             rows = table(row_cells, slot[6], slot[0:3])
             for side in range(2):
                 lanes = slice(side * half, (side + 1) * half)
                 to = slice(j * half, (j + 1) * half)
                 rows_s[group, :, side * span + j * half : side * span + (j + 1) * half] = rows[:, lanes]
                 cols_s[group, side, :, to] = table(side_cells[side], slot[7][:, lanes], [w[:, lanes] for w in slot[3:6]])
-                flags_out[group, side, :, to] = joined([f[:, lanes] for f in slot[8:10]], 0)
-        return carry
-
-    lax.fori_loop(0, groups, build, 0)
-
-
-def first_kernel(first_of, blocks_of, pieces, spk_dev, *refs):
-    data_refs, refs = refs[:pieces], refs[pieces:]
-    list_ref, flags_ref, rows_s, cols_s, dft_ref, data_out, back_out, slots, weighted_s, grid_s = refs
-    ro = slots.shape[-1]
-    groups, _, _, span = weighted_s.shape
-    per_group, half = 2 * span // ro, ro // 2
-    for place, value in blocks_of(data_refs):
-        slots[place] = value.astype(F32)
-    start = first_of()
-    grid_s[...] = jnp.zeros_like(grid_s)
-
-    def pick(group):
-        for j in range(per_group):
-            which = start + group * per_group + j
-            block, depth = list_ref[0, which], list_ref[1, which]
-            data = joined([slots[block, pl.ds(p * spk_dev + depth, 1), :] for p in range(2)], 0)
-            to = slice(j * half, (j + 1) * half)
-            low_first = flags_ref[group, 0, 1:2, to] > 0.5
-            halves = [data[:, :half], data[:, half:]]
-            for side in range(2):
-                mine = jnp.where(low_first, halves[side], halves[1 - side])
-                density = flags_ref[group, side, 0:1, to]
-                data_out[group, side, 0:2, to] = mine
-                data_out[group, side, 2:3, to] = density
-                weighted_s[group, side, :, to] = -density * mine
-
-    pick(0)
+                data = joined([slot[8][:, lanes], slot[9][:, lanes]], 0)
+                data_out[group, side, 0:2, to] = data
+                data_out[group, side, 2:3, to] = slot[10][:, lanes]
+                weighted_s[group, side, :, to] = -slot[10][:, lanes] * data
+
+    build(0)
 
     def group_step(group, carry):
         grid_group(group - 1, rows_s, cols_s, weighted_s, grid_s)
-        pick(group)
+        build(group)
         return carry
 
     lax.fori_loop(1, groups, group_step, 0)
     grid_group(groups - 1, rows_s, cols_s, weighted_s, grid_s)
-    back_out[...] = adjoint(from_sides(grid_s), dft_ref)
+    back_out[...] = adjoint(from_sides(grid_s), const_ref)
 
 
 def target_of(est_ref, part_refs):
@@ -313,16 +286,16 @@
     thr_ref, refs = refs[0], refs[1:]
     est_ref, refs = refs[0] if n_est else None, refs[n_est:]
     part_refs, refs = refs[:n_parts], refs[n_parts:]
-    map_ref, data_ref, dft_ref, haar_ref, rows_s, cols_s, est_out, part_out, sides_s, weighted_s, grid_s = refs
+    map_ref, data_ref, const_ref, rows_s, cols_s, est_out, part_out, sides_s, weighted_s, grid_s = refs
     groups, _, _, span = weighted_s.shape
     n, rows = map_ref.shape[1], cols_s.shape[2]
     target = target_of(est_ref, part_refs)
-    re, im = shrink(target[0], target[1], thr_ref, haar_ref)
+    re, im = shrink(target[0], target[1], thr_ref, const_ref)
     est_out[0] = re
     est_out[1] = im
     mre, mim = map_ref[0], map_ref[1]
-    half = right_dft(mre * re - mim * im, mre * im + mim * re, dft_ref, 1)
-    for side, values in enumerate(to_sides(left_dft(half, dft_ref, 1))):
+    half = right_dft(mre * re - mim * im, mre * im + mim * re, const_ref, 1)
+    for side, values in enumerate(to_sides(left_dft(half, const_ref, 1))):
         sides_s[side] = values.astype(BF16)
     grid_s[...] = jnp.zeros_like(grid_s)
 
@@ -346,7 +319,7 @@
 
     lax.fori_loop(1, groups, group_step, 0)
     grid_group(groups - 1, rows_s, cols_s, weighted_s, grid_s)
-    back = adjoint(from_sides(grid_s), dft_ref)
+    back = adjoint(from_sides(grid_s), const_ref)
     conj_map(map_ref[0], map_ref[1], back, part_out)
 
 
@@ -369,15 +342,15 @@
 
 
 def last_kernel(n_parts, rows, mine_of, thr_ref, est_ref, *refs):
-    part_refs, (haar_ref, out_ref) = refs[:n_parts], refs[n_parts:]
+    part_refs, (const_ref, out_ref) = refs[:n_parts], refs[n_parts:]
     n = est_ref.shape[1]
     target = target_of(est_ref, part_refs)
     mine = mine_of()
     pick = lax.broadcasted_iota(jnp.int32, (rows, n), 1) == (
         lax.broadcasted_iota(jnp.int32, (rows, n), 0) + mine * rows
     )
-    own = mm(jnp.where(pick, 1.0, 0.0).astype(BF16), haar_ref[2]).astype(BF16)
-    re, im = shrink(target[0], target[1], thr_ref, haar_ref, own)
+    own = mm(jnp.where(pick, 1.0, 0.0).astype(BF16), const_ref[8]).astype(BF16)
+    re, im = shrink(target[0], target[1], thr_ref, const_ref, own)
     out_ref[:, 0, :] = re
     out_ref[:, 1, :] = im
 
@@ -389,7 +362,7 @@
     spk_dev, ro = sample_bins.shape
     live_total = blocks * spk_dev // 2
     own_map = coil_maps[0]
-    by_core = n_coil == n_spk == 2
+    by_core = n_coil == n_spk == 2 and n_tile & (n_tile - 1) == 0
     vmem = pl.BlockSpec(memory_space=pltpu.VMEM)
     smem = pl.BlockSpec(memory_space=pltpu.SMEM)
     data_rows, fields = 2 * spk_dev, 11
@@ -402,18 +375,14 @@
         compiler_params=PARAMS,
     )(kspace_data[0], jnp.swapaxes(interp_weights, 0, 1), sample_bins, spoke_count)
 
-    dft, haar = dft_tables(n), haar_tables(n)
-    limits, dft, haar = pl.pallas_call(
+    const = np.concatenate([dft_tables(n), haar_tables(n)])
+    limits, const = pl.pallas_call(
         constants_kernel,
-        out_shape=[
-            jax.ShapeDtypeStruct((LEVELS, n), F32),
-            jax.ShapeDtypeStruct(dft.shape, BF16),
-            jax.ShapeDtypeStruct(haar.shape, BF16),
-        ],
-        in_specs=[smem, vmem, vmem],
-        out_specs=[vmem] * 3,
+        out_shape=[jax.ShapeDtypeStruct((LEVELS, n), F32), jax.ShapeDtypeStruct(const.shape, BF16)],
+        in_specs=[smem, vmem],
+        out_specs=[vmem] * 2,
         compiler_params=PARAMS,
-    )(thresholds, jnp.asarray(dft), jnp.asarray(haar))
+    )(thresholds, jnp.asarray(const))
 
     if by_core:
         onto = [(0, 2), (3, 1), (1, 0), (2, 3)]
@@ -422,7 +391,7 @@
         def spread(value):
             out = [value]
             for shift in range(1, n_tile):
-                out.append(lax.ppermute(value, "tile", [(i, (i + shift) % n_tile) for i in range(n_tile)]))
+                out.append(lax.ppermute(value, "tile", [(i, i ^ shift) for i in range(n_tile)]))
             return out
 
         def to_coil(value):
@@ -430,7 +399,7 @@
 
         def senders():
             tile = lax.axis_index("tile")
-            return [(tile - shift + n_tile) % n_tile for shift in range(n_tile)]
+            return [tile ^ shift for shift in range(n_tile)]
 
         def spoke_blocks(refs):
             own, other = refs
@@ -451,7 +420,7 @@
         pieces = spread(bundle)
         own_map, bundle = lax.optimization_barrier((own_map, bundle))
         map_pieces = spread(own_map)
-        pieces, limits, dft, haar = lax.optimization_barrier((pieces, limits, dft, haar))
+        pieces, limits, const = lax.optimization_barrier((pieces, limits, const))
         own_data, own_spokes = pl.pallas_call(
             functools.partial(join_kernel, data_rows),
             out_shape=[
@@ -498,30 +467,25 @@
     image = jax.ShapeDtypeStruct((2, n, n), F32)
     weighted = pltpu.VMEM((groups, 2, 2, span), F32)
     gridded = pltpu.VMEM((2, 2 * side_rows, n), F32)
-    row_tab, col_tab, flags, live = pl.pallas_call(
-        functools.partial(table_kernel, first_of, spoke_blocks, live_total, len(spokes), spk_dev, n),
+    counts = (len(spokes), len(coil_data))
+    row_tab, col_tab, data, back = pl.pallas_call(
+        functools.partial(first_kernel, first_of, spoke_blocks, coil_blocks, live_total, counts, spk_dev, n),
         out_shape=[
             jax.ShapeDtypeStruct((groups, n, 2 * span), BF16),
             jax.ShapeDtypeStruct((groups, 2, side_rows, span), BF16),
-            jax.ShapeDtypeStruct((groups, 2, 2, span), F32),
-            jax.ShapeDtypeStruct((2, blocks * spk_dev + 1), jnp.int32),
-        ],
-        in_specs=[vmem] * len(spokes),
-        out_specs=[vmem, vmem, vmem, smem],
-        scratch_shapes=[pltpu.VMEM((blocks, spoke_rows, ro), F32)],
-        compiler_params=PARAMS,
-    )(*spokes)
-    data, back = pl.pallas_call(
-        functools.partial(first_kernel, first_of, coil_blocks, len(coil_data), spk_dev),
-        out_shape=[
             jax.ShapeDtypeStruct((groups, 2, 3, span), F32),
             jax.ShapeDtypeStruct((2 * n, n), F32),
         ],
-        in_specs=[vmem] * len(coil_data) + [smem] + [vmem] * 4,
-        out_specs=[vmem] * 2,
-        scratch_shapes=[pltpu.VMEM((blocks, data_rows, ro), F32), weighted, gridded],
+        in_specs=[vmem] * (sum(counts) + 1),
+        out_specs=[vmem] * 4,
+        scratch_shapes=[
+            pltpu.VMEM((blocks, fields * spk_dev, ro), F32),
+            weighted,
+            gridded,
+            pltpu.SMEM((2, blocks * spk_dev + 1), jnp.int32),
+        ],
         compiler_params=PARAMS,
-    )(*coil_data, live, flags, row_tab, col_tab, dft)
+    )(*spokes, *coil_data, const)
     map_t, part = pl.pallas_call(
         functools.partial(map_kernel, coil_blocks, len(maps)),
         out_shape=[image, image],
@@ -533,7 +497,7 @@
     estimate = []
     parts = parts_of(part)
     for _ in range(1, ITERS):
-        inputs = (*estimate, *parts, map_t, data, dft, haar, row_tab, col_tab)
+        inputs = (*estimate, *parts, map_t, data, const, row_tab, col_tab)
         *estimate, part = pl.pallas_call(
             functools.partial(step_kernel, len(estimate), len(parts)),
             out_shape=[image, image],
@@ -550,7 +514,7 @@
         in_specs=[vmem] * (len(parts) + 3),
         out_specs=vmem,
         compiler_params=PARAMS,
-    )(limits, *estimate, *parts, haar)
+    )(limits, *estimate, *parts, const)
 
 
 def solution(mesh):

time: 72.6 us -> 71.6 us (0.986)
  waiting for transfers between devices: 8.59 us -> 11 us
  Pallas kernels: 38.9 us -> 36.5 us
  local copies, waits for them, and re-layouts: 5.79 us -> 4.93 us
    ppermute x2, waiting for transfers between devices: 0.01 us -> 2.76 us  [to_coil(): lax.ppermute(value, ('coil', 'spk'), onto)]
    pallas_call x2 -> x1, Pallas kernels: 9.96 us -> 7.51 us  [local(): pl.pallas_call(functools.partial(first_kernel, first_of, spoke_blocks, co...]
    unnamed x14 -> x12, local copies, waits for them, and re-layouts: 5.79 us -> 4.93 us
  transfers between devices with their start and end apart: 15 -> 15, of which waited for: 6 -> 7; matrix products, arithmetic and copies ran while one was open for 0% -> 0% of each run, Pallas kernels for 15% -> 11%
where the time goes in v5:
time: 71.6 us; the launch traced here: 71.3 us
  Pallas kernels  36.5 us (51%)
  starting transfers between devices  18.1 us (25%)
  waiting for transfers between devices  11 us (15%)
  local copies, waits for them, and re-layouts  4.93 us (7%)
  between operations  0.79 us (1%)
    pallas_call x3, Pallas kernels, local(): pl.pallas_call(functools.partial(step_kernel, len(estimate), len(parts)),...  25.8 us
    ppermute x6, starting transfers between devices, spread(): lax.ppermute(value, 'tile', [(i, i ^ shift) for i in range(n_tile)])  10.2 us
    pallas_call x1, Pallas kernels, local(): pl.pallas_call(functools.partial(first_kernel, first_of, spoke_blocks, co...  7.51 us
    ppermute x4, waiting for transfers between devices, parts_of(): return [part, lax.ppermute(part, 'spk', swap)]  6.15 us
    unnamed x12, local copies, waits for them, and re-layouts  4.93 us
    ppermute x4, starting transfers between devices, parts_of(): return [part, lax.ppermute(part, 'spk', swap)]  3.14 us
    ppermute x2, waiting for transfers between devices, to_coil(): lax.ppermute(value, ('coil', 'spk'), onto)  2.76 us
    ppermute x6, waiting for transfers between devices, spread(): lax.ppermute(value, 'tile', [(i, i ^ shift) for i in range(n_tile)])  2.05 us
  transfers between devices with their start and end apart: 15, of which 7 were waited for; matrix products, arithmetic and copies ran while one was open for 0% of the time, Pallas kernels for 11%

profile of v5, /device:TPU:0, one launch (start us, length us, event | category | flops | bytes accessed | tf_op | source)
XLA Modules:
  0.0 71.3 jit_solution(15891619580242927574)
XLA Ops:
  0.7 0.0 copy-start.2
  0.7 0.7 %copy-done.2 = bf16[8,6,256]{2,0,1:T(8,128)(2,1)S(1)} copy-done((bf16[8,6,256]{2,0,1:T(8,128)(2,1)S(1)}, bf16[8,6,256]{2,0,1:T(8,128)(2,1)}, u32[]{:S(2)}) %copy-start.2) | copy-done | bytes 24600
  1.4 0.0 copy-start.3
  1.4 0.7 copy-done.3
  2.1 0.0 copy-start.4
  2.1 0.7 copy-done.4
  2.8 5.1 %collective-permute-start.2 = (bf16[88,256]{1,0:T(8,128)(2,1)S(1)}, bf16[88,256]{1,0:T(8,128)(2,1)S(1)}, u32[]{:S(2)}, u32[]{:S(2)}) collective-permute-start(bf16[88,256]{1,0:T(8,128)(2,1)S(1)} %shard_map.73.refs_0_), channel_id=1, source_target_pairs={{0,12},{4,8},{8,4},{12,0},{1,13},{5,9},{9,5},{13,1},{2,14},{6,10},... | collective-permute-start | bytes 135176 | tf_op jit(solution)/shard_map/ppermute | solution.py:394
  8.0 0.1 collective-permute-start.5
  8.0 0.9 %collective-permute-start.4 = (f32[32,2,256]{2,1,0:T(2,128)}, f32[32,2,256]{2,1,0:T(2,128)S(1)}, u32[]{:S(2)}, u32[]{:S(2)}) collective-permute-start(f32[32,2,256]{2,1,0:T(2,128)} %bitcast.4), channel_id=1, source_target_pairs={{0,8},{4,12},{8,0},{12,4},{1,9},{5,13},{9,1},{13,5},{2,10},{6,14},... | collective-permute-start | bytes 196616 | tf_op jit(solution)/shard_map/ppermute | solution.py:394
  9.0 3.4 %collective-permute-start.3 = (f32[32,2,256]{2,1,0:T(2,128)}, f32[32,2,256]{2,1,0:T(2,128)S(1)}, u32[]{:S(2)}, u32[]{:S(2)}) collective-permute-start(f32[32,2,256]{2,1,0:T(2,128)} %bitcast.5), channel_id=1, source_target_pairs={{0,4},{4,0},{8,12},{12,8},{1,5},{5,1},{9,13},{13,9},{2,6},{6,2},{1... | collective-permute-start | bytes 196616 | tf_op jit(solution)/shard_map/ppermute | solution.py:394
  12.3 0.0 collective-permute-start.1
  12.3 0.0 collective-permute-done.2.refs_3_
  12.3 0.6 collective-permute-start
  13.0 0.0 copy-start
  13.0 1.3 %copy-done = bf16[10,256,256]{2,1,0:T(8,128)(2,1)S(1)} copy-done((bf16[10,256,256]{2,1,0:T(8,128)(2,1)S(1)}, bf16[10,256,256]{2,1,0:T(8,128)(2,1)}, u32[]{:S(2)}) %copy-start) | copy-done | bytes 1310744
  14.3 0.7 copy-done.5
  15.0 0.6 shard_map.74
  15.6 1.7 %collective-permute-done.1.refs_2_ = bf16[88,256]{1,0:T(8,128)(2,1)S(1)} collective-permute-done((bf16[88,256]{1,0:T(8,128)(2,1)S(1)}, bf16[88,256]{1,0:T(8,128)(2,1)S(1)}, u32[]{:S(2)}, u32[]{:S(2)}) %collective-permute-start.1) | collective-permute-done | bytes 45088 | tf_op jit(solution)/shard_map/ppermute | solution.py:394
  17.3 0.3 collective-permute-done.refs_1_
  17.7 0.0 collective-permute-done.5.refs_3_
  17.7 0.0 collective-permute-done.4.refs_2_
  17.7 0.0 collective-permute-done.3.refs_1_
  17.7 0.0 copy-start.1
  17.7 0.8 %copy-done.1 = f32[1,32,2,256]{3,2,1,0:T(2,128)S(1)} copy-done((f32[1,32,2,256]{3,2,1,0:T(2,128)S(1)}, f32[1,32,2,256]{3,2,1,0:T(2,128)}, u32[]{:S(2)}) %copy-start.1) | copy-done | bytes 65560
  18.5 1.5 %collective-permute-start.7 = (f32[4,32,2,256]{3,2,1,0:T(2,128)S(1)}, f32[4,32,2,256]{3,2,1,0:T(2,128)S(1)}, u32[]{:S(2)}, u32[]{:S(2)}) collective-permute-start(f32[4,32,2,256]{3,2,1,0:T(2,128)S(1)} %shard_map.76.refs_0_), channel_id=1, source_target_pairs={{0,2},{3,1},{1,0},{2,3},{4,6},{7,5},{5,4},{6,7},{8,10},{11,9},{9,8... | collective-permute-start | bytes 786440 | tf_op jit(solution)/shard_map/ppermute | solution.py:398
  20.1 0.7 collective-permute-start.6
  20.7 1.4 %collective-permute-start.8 = (bf16[4,72,256]{2,1,0:T(8,128)(2,1)S(1)}, bf16[4,72,256]{2,1,0:T(8,128)(2,1)S(1)}, u32[]{:S(2)}, u32[]{:S(2)}) collective-permute-start(bf16[4,72,256]{2,1,0:T(8,128)(2,1)S(1)} %get-tuple-element.47.refs_0_), channel_id=1, source_target_pairs={{0,1},{1,0},{2,3},{3,2},{4,5},{5,4},{6,7},{7,6},{8,9},{9,8},{10,11... | collective-permute-start | bytes 442376 | tf_op jit(solution)/shard_map/ppermute | solution.py:434
  22.2 0.5 collective-permute-start.10
  22.7 0.7 collective-permute-start.9
  23.4 2.8 %collective-permute-done.10.refs_4_ = bf16[4,16,256]{2,1,0:T(8,128)(2,1)S(1)} collective-permute-done((bf16[4,16,256]{2,1,0:T(8,128)(2,1)S(1)}, bf16[4,16,256]{2,1,0:T(8,128)(2,1)S(1)}, u32[]{:S(2)}, u32[]{:S(2)}) %collective-permute-start.10) | collective-permute-done | bytes 32800 | tf_op jit(solution)/shard_map/ppermute | solution.py:398
  26.1 0.0 collective-permute-done.9.refs_3_
  26.1 0.0 collective-permute-done.8.refs_1_
  26.1 7.5 %shard_map.77 = (bf16[4,256,2048]{2,1,0:T(8,128)(2,1)S(1)}, bf16[4,2,144,1024]{3,2,1,0:T(8,128)(2,1)S(1)}, f32[4,2,3,1024]{3,2,1,0:T(4,128)S(1)}, f32[512,256]{1,0:T(8,128)S(1)}) custom-call(bf16[4,72,256]{2,1,0:T(8,128)(2,1)S(1)} %get-tuple-element.47.refs_0_, bf16[4,72,256]{2,1,0:T(8,128)(2,1)S(1)} %collective-permute-done.8.refs_1_, ...), custom_call_target="tpu_custom_call" | custom-call | tf_op jit(solution)/shard_map/pallas_call | solution.py:471
  33.6 0.0 collective-permute-done.7.refs_2_
  33.7 0.0 collective-permute-done.6.refs_1_
  33.7 0.5 shard_map.78
  34.1 1.8 %collective-permute-start.11 = (f32[2,256,256]{2,1,0:T(8,128)S(1)}, f32[2,256,256]{2,1,0:T(8,128)S(1)}, u32[]{:S(2)}, u32[]{:S(2)}) collective-permute-start(f32[2,256,256]{2,1,0:T(8,128)S(1)} %get-tuple-element.50.refs_1_), channel_id=1, source_target_pairs={{0,1},{1,0},{2,3},{3,2},{4,5},{5,4},{6,7},{7,6},{8,9},{9,8},{10,11... | collective-permute-start | bytes 1572872 | tf_op jit(solution)/shard_map/ppermute | solution.py:449
  36.0 1.5 %collective-permute-done.11.refs_2_ = f32[2,256,256]{2,1,0:T(8,128)S(1)} collective-permute-done((f32[2,256,256]{2,1,0:T(8,128)S(1)}, f32[2,256,256]{2,1,0:T(8,128)S(1)}, u32[]{:S(2)}, u32[]{:S(2)}) %collective-permute-start.11) | collective-permute-done | bytes 524320 | tf_op jit(solution)/shard_map/ppermute | solution.py:449
  37.5 8.5 %shard_map.79 = (f32[2,256,256]{2,1,0:T(8,128)S(1)}, f32[2,256,256]{2,1,0:T(8,128)S(1)}) custom-call(f32[3,256]{1,0:T(4,128)S(1)} %get-tuple-element.35.refs_0_.thr_ref, f32[2,256,256]{2,1,0:T(8,128)S(1)} %get-tuple-element.50.refs_1_, f32[2,256,256]{2,1,0:T(8,128)S(1)} %collective-permute-done.11.refs_2_, ...), custom_call_target="tpu_custom_call" | custom-call | tf_op jit(solution)/shard_map/pallas_call | solution.py:501
  46.0 0.4 collective-permute-start.12
  46.5 1.5 %collective-permute-done.12.refs_3_ = f32[2,256,256]{2,1,0:T(8,128)S(1)} collective-permute-done((f32[2,256,256]{2,1,0:T(8,128)S(1)}, f32[2,256,256]{2,1,0:T(8,128)S(1)}, u32[]{:S(2)}, u32[]{:S(2)}) %collective-permute-start.12) | collective-permute-done | bytes 524320 | tf_op jit(solution)/shard_map/ppermute | solution.py:449
  48.0 8.7 %shard_map.80 = (f32[2,256,256]{2,1,0:T(8,128)S(1)}, f32[2,256,256]{2,1,0:T(8,128)S(1)}) custom-call(f32[3,256]{1,0:T(4,128)S(1)} %get-tuple-element.35.refs_0_.thr_ref, f32[2,256,256]{2,1,0:T(8,128)S(1)} %get-tuple-element.55.refs_1_, f32[2,256,256]{2,1,0:T(8,128)S(1)} %get-tuple-element.56.refs_2_, f32[2,256,256]{2,1,0:T(8,128)S(1)} %collective-permute-done.12.refs_3_, ...), custom_call_target="tpu_custom_call" | custom-call | tf_op jit(solution)/shard_map/pallas_call | solution.py:501
  56.7 0.4 collective-permute-start.13
  57.2 1.5 %collective-permute-done.13.refs_3_ = f32[2,256,256]{2,1,0:T(8,128)S(1)} collective-permute-done((f32[2,256,256]{2,1,0:T(8,128)S(1)}, f32[2,256,256]{2,1,0:T(8,128)S(1)}, u32[]{:S(2)}, u32[]{:S(2)}) %collective-permute-start.13) | collective-permute-done | bytes 524320 | tf_op jit(solution)/shard_map/ppermute | solution.py:449
  58.7 8.6 %shard_map.81 = (f32[2,256,256]{2,1,0:T(8,128)S(1)}, f32[2,256,256]{2,1,0:T(8,128)S(1)}) custom-call(f32[3,256]{1,0:T(4,128)S(1)} %get-tuple-element.35.refs_0_.thr_ref, f32[2,256,256]{2,1,0:T(8,128)S(1)} %get-tuple-element.57.refs_1_, f32[2,256,256]{2,1,0:T(8,128)S(1)} %get-tuple-element.58.refs_2_, f32[2,256,256]{2,1,0:T(8,128)S(1)} %collective-permute-done.13.refs_3_, ...), custom_call_target="tpu_custom_call" | custom-call | tf_op jit(solution)/shard_map/pallas_call | solution.py:501
  67.3 0.4 collective-permute-start.14
  67.7 1.5 %collective-permute-done.14.refs_1_ = f32[2,256,256]{2,1,0:T(8,128)S(1)} collective-permute-done((f32[2,256,256]{2,1,0:T(8,128)S(1)}, f32[2,256,256]{2,1,0:T(8,128)S(1)}, u32[]{:S(2)}, u32[]{:S(2)}) %collective-permute-start.14) | collective-permute-done | bytes 524320 | tf_op jit(solution)/shard_map/ppermute | solution.py:449
  69.2 2.0 %shard_map.82 = f32[32,2,256]{2,1,0:T(2,128)} custom-call(f32[3,256]{1,0:T(4,128)S(1)} %get-tuple-element.35.refs_0_.thr_ref, f32[2,256,256]{2,1,0:T(8,128)S(1)} %get-tuple-element.59.est_ref, f32[2,256,256]{2,1,0:T(8,128)S(1)} %get-tuple-element.60.refs_0_, f32[2,256,256]{2,1,0:T(8,128)S(1)} %collective-permute-done.14.refs_1_, ...), custom_call_target="tpu_custom_call" | custom-call | tf_op jit(solution)/shard_map/pallas_call | solution.py:511
  (4 shorter events, 0.1 us)
Async XLA Ops:
  0.7 0.7 %copy-start.2 = (bf16[8,6,256]{2,0,1:T(8,128)(2,1)S(1)}, bf16[8,6,256]{2,0,1:T(8,128)(2,1)}, u32[]{:S(2)}) copy-start(bf16[8,6,256]{2,0,1:T(8,128)(2,1)} %param.9) | copy-start | bytes 73732
  1.4 0.7 copy-start.3
  2.1 0.7 copy-start.4
  2.8 9.5 %collective-permute-start.2 = (bf16[88,256]{1,0:T(8,128)(2,1)S(1)}, bf16[88,256]{1,0:T(8,128)(2,1)S(1)}, u32[]{:S(2)}, u32[]{:S(2)}) collective-permute-start(bf16[88,256]{1,0:T(8,128)(2,1)S(1)} %shard_map.73.refs_0_), channel_id=1, source_target_pairs={{0,12},{4,8},{8,4},{12,0},{1,13},{5,9},{9,5},{13,1},{2,14},{6,10},... | collective-permute-start | bytes 135176 | tf_op jit(solution)/shard_map/ppermute | solution.py:394
  8.0 9.7 %collective-permute-start.5 = (f32[32,2,256]{2,1,0:T(2,128)}, f32[32,2,256]{2,1,0:T(2,128)S(1)}, u32[]{:S(2)}, u32[]{:S(2)}) collective-permute-start(f32[32,2,256]{2,1,0:T(2,128)} %bitcast.3), channel_id=1, source_target_pairs={{0,12},{4,8},{8,4},{12,0},{1,13},{5,9},{9,5},{13,1},{2,14},{6,10},... | collective-permute-start | bytes 196616 | tf_op jit(solution)/shard_map/ppermute | solution.py:394
  8.0 9.6 %collective-permute-start.4 = (f32[32,2,256]{2,1,0:T(2,128)}, f32[32,2,256]{2,1,0:T(2,128)S(1)}, u32[]{:S(2)}, u32[]{:S(2)}) collective-permute-start(f32[32,2,256]{2,1,0:T(2,128)} %bitcast.4), channel_id=1, source_target_pairs={{0,8},{4,12},{8,0},{12,4},{1,9},{5,13},{9,1},{13,5},{2,10},{6,14},... | collective-permute-start | bytes 196616 | tf_op jit(solution)/shard_map/ppermute | solution.py:394
  9.0 8.7 %collective-permute-start.3 = (f32[32,2,256]{2,1,0:T(2,128)}, f32[32,2,256]{2,1,0:T(2,128)S(1)}, u32[]{:S(2)}, u32[]{:S(2)}) collective-permute-start(f32[32,2,256]{2,1,0:T(2,128)} %bitcast.5), channel_id=1, source_target_pairs={{0,4},{4,0},{8,12},{12,8},{1,5},{5,1},{9,13},{13,9},{2,6},{6,2},{1... | collective-permute-start | bytes 196616 | tf_op jit(solution)/shard_map/ppermute | solution.py:394
  12.3 5.0 %collective-permute-start.1 = (bf16[88,256]{1,0:T(8,128)(2,1)S(1)}, bf16[88,256]{1,0:T(8,128)(2,1)S(1)}, u32[]{:S(2)}, u32[]{:S(2)}) collective-permute-start(bf16[88,256]{1,0:T(8,128)(2,1)S(1)} %shard_map.73.refs_0_), channel_id=1, source_target_pairs={{0,8},{4,12},{8,0},{12,4},{1,9},{5,13},{9,1},{13,5},{2,10},{6,14},... | collective-permute-start | bytes 135176 | tf_op jit(solution)/shard_map/ppermute | solution.py:394
  12.3 5.3 %collective-permute-start = (bf16[88,256]{1,0:T(8,128)(2,1)S(1)}, bf16[88,256]{1,0:T(8,128)(2,1)S(1)}, u32[]{:S(2)}, u32[]{:S(2)}) collective-permute-start(bf16[88,256]{1,0:T(8,128)(2,1)S(1)} %shard_map.73.refs_0_), channel_id=1, source_target_pairs={{0,4},{4,0},{8,12},{12,8},{1,5},{5,1},{9,13},{13,9},{2,6},{6,2},{1... | collective-permute-start | bytes 135176 | tf_op jit(solution)/shard_map/ppermute | solution.py:394
  13.0 1.3 %copy-start = (bf16[10,256,256]{2,1,0:T(8,128)(2,1)S(1)}, bf16[10,256,256]{2,1,0:T(8,128)(2,1)}, u32[]{:S(2)}) copy-start(bf16[10,256,256]{2,1,0:T(8,128)(2,1)} %constant.2.clone.const_ref) | copy-start | bytes 3932164
  14.3 0.7 copy-start.5
  17.7 0.8 %copy-start.1 = (f32[1,32,2,256]{3,2,1,0:T(2,128)S(1)}, f32[1,32,2,256]{3,2,1,0:T(2,128)}, u32[]{:S(2)}) copy-start(f32[1,32,2,256]{3,2,1,0:T(2,128)} %param.7) | copy-start | bytes 196612
  18.5 15.1 %collective-permute-start.7 = (f32[4,32,2,256]{3,2,1,0:T(2,128)S(1)}, f32[4,32,2,256]{3,2,1,0:T(2,128)S(1)}, u32[]{:S(2)}, u32[]{:S(2)}) collective-permute-start(f32[4,32,2,256]{3,2,1,0:T(2,128)S(1)} %shard_map.76.refs_0_), channel_id=1, source_target_pairs={{0,2},{3,1},{1,0},{2,3},{4,6},{7,5},{5,4},{6,7},{8,10},{11,9},{9,8... | collective-permute-start | bytes 786440 | tf_op jit(solution)/shard_map/ppermute | solution.py:398
  20.1 13.6 %collective-permute-start.6 = (f32[4,32,2,256]{3,2,1,0:T(2,128)S(1)}, f32[4,32,2,256]{3,2,1,0:T(2,128)S(1)}, u32[]{:S(2)}, u32[]{:S(2)}) collective-permute-start(f32[4,32,2,256]{3,2,1,0:T(2,128)S(1)} %shard_map.76.refs_0_), channel_id=1, source_target_pairs={{1,2},{2,1},{5,6},{6,5},{9,10},{10,9},{13,14},{14,13},{17,18},{18,... | collective-permute-start | bytes 786440 | tf_op jit(solution)/shard_map/ppermute | solution.py:398
  20.7 5.4 %collective-permute-start.8 = (bf16[4,72,256]{2,1,0:T(8,128)(2,1)S(1)}, bf16[4,72,256]{2,1,0:T(8,128)(2,1)S(1)}, u32[]{:S(2)}, u32[]{:S(2)}) collective-permute-start(bf16[4,72,256]{2,1,0:T(8,128)(2,1)S(1)} %get-tuple-element.47.refs_0_), channel_id=1, source_target_pairs={{0,1},{1,0},{2,3},{3,2},{4,5},{5,4},{6,7},{7,6},{8,9},{9,8},{10,11... | collective-permute-start | bytes 442376 | tf_op jit(solution)/shard_map/ppermute | solution.py:434
  22.2 4.0 %collective-permute-start.10 = (bf16[4,16,256]{2,1,0:T(8,128)(2,1)S(1)}, bf16[4,16,256]{2,1,0:T(8,128)(2,1)S(1)}, u32[]{:S(2)}, u32[]{:S(2)}) collective-permute-start(bf16[4,16,256]{2,1,0:T(8,128)(2,1)S(1)} %get-tuple-element.42.refs_2_), channel_id=1, source_target_pairs={{0,2},{3,1},{1,0},{2,3},{4,6},{7,5},{5,4},{6,7},{8,10},{11,9},{9,8... | collective-permute-start | bytes 98312 | tf_op jit(solution)/shard_map/ppermute | solution.py:398
  22.7 3.4 %collective-permute-start.9 = (bf16[4,16,256]{2,1,0:T(8,128)(2,1)S(1)}, bf16[4,16,256]{2,1,0:T(8,128)(2,1)S(1)}, u32[]{:S(2)}, u32[]{:S(2)}) collective-permute-start(bf16[4,16,256]{2,1,0:T(8,128)(2,1)S(1)} %get-tuple-element.42.refs_2_), channel_id=1, source_target_pairs={{1,2},{2,1},{5,6},{6,5},{9,10},{10,9},{13,14},{14,13},{17,18},{18,... | collective-permute-start | bytes 98312 | tf_op jit(solution)/shard_map/ppermute | solution.py:398
  34.1 3.4 %collective-permute-start.11 = (f32[2,256,256]{2,1,0:T(8,128)S(1)}, f32[2,256,256]{2,1,0:T(8,128)S(1)}, u32[]{:S(2)}, u32[]{:S(2)}) collective-permute-start(f32[2,256,256]{2,1,0:T(8,128)S(1)} %get-tuple-element.50.refs_1_), channel_id=1, source_target_pairs={{0,1},{1,0},{2,3},{3,2},{4,5},{5,4},{6,7},{7,6},{8,9},{9,8},{10,11... | collective-permute-start | bytes 1572872 | tf_op jit(solution)/shard_map/ppermute | solution.py:449
  46.0 2.0 %collective-permute-start.12 = (f32[2,256,256]{2,1,0:T(8,128)S(1)}, f32[2,256,256]{2,1,0:T(8,128)S(1)}, u32[]{:S(2)}, u32[]{:S(2)}) collective-permute-start(f32[2,256,256]{2,1,0:T(8,128)S(1)} %get-tuple-element.56.refs_2_), channel_id=1, source_target_pairs={{0,1},{1,0},{2,3},{3,2},{4,5},{5,4},{6,7},{7,6},{8,9},{9,8},{10,11... | collective-permute-start | bytes 1572872 | tf_op jit(solution)/shard_map/ppermute | solution.py:449
  56.7 2.0 %collective-permute-start.13 = (f32[2,256,256]{2,1,0:T(8,128)S(1)}, f32[2,256,256]{2,1,0:T(8,128)S(1)}, u32[]{:S(2)}, u32[]{:S(2)}) collective-permute-start(f32[2,256,256]{2,1,0:T(8,128)S(1)} %get-tuple-element.58.refs_2_), channel_id=1, source_target_pairs={{0,1},{1,0},{2,3},{3,2},{4,5},{5,4},{6,7},{7,6},{8,9},{9,8},{10,11... | collective-permute-start | bytes 1572872 | tf_op jit(solution)/shard_map/ppermute | solution.py:449
  67.3 2.0 %collective-permute-start.14 = (f32[2,256,256]{2,1,0:T(8,128)S(1)}, f32[2,256,256]{2,1,0:T(8,128)S(1)}, u32[]{:S(2)}, u32[]{:S(2)}) collective-permute-start(f32[2,256,256]{2,1,0:T(8,128)S(1)} %get-tuple-element.60.refs_0_), channel_id=1, source_target_pairs={{0,1},{1,0},{2,3},{3,2},{4,5},{5,4},{6,7},{7,6},{8,9},{9,8},{10,11... | collective-permute-start | bytes 1572872 | tf_op jit(solution)/shard_map/ppermute | solution.py:449

commit v6 on v5

--- a/solution.py
+++ b/solution.py
@@ -26,31 +26,40 @@
 
 
 def dft_tables(n):
+    half = n // 2
     idx = np.arange(n)
     angles = 2.0 * math.pi / n * (np.outer(idx, idx) % n)
     scale = 1.0 / math.sqrt(n)
-    parts = [np.cos(angles) * scale, np.sin(angles) * scale, -np.sin(angles) * scale]
-    pairs = [split_host(part) for part in parts]
-    return np.stack([pair[0] for pair in pairs] + [pair[1] for pair in pairs])
-
-
-def haar_signs(n):
-    mat = np.eye(n)
-    for level in range(LEVELS):
-        span, half = n >> level, n >> (level + 1)
-        step = np.eye(n)
-        step[:span] = 0.0
-        for i in range(half):
-            step[i, 2 * i] = step[i, 2 * i + 1] = 1.0
-            step[half + i, 2 * i], step[half + i, 2 * i + 1] = 1.0, -1.0
-        mat = step @ mat
-    return mat
-
-
-def haar_tables(n):
-    col = haar_signs(n)
-    row = np.kron(np.eye(n // 2**LEVELS), haar_signs(2**LEVELS))
-    return np.stack([col, col.T, row.T, row]).astype(BF16)
+    small = 2.0 * math.pi / half * (np.outer(idx[:half], idx[:half]) % half)
+    cos, sin = np.cos(small) * scale, np.sin(small) * scale
+    folded = np.block([[cos, -sin], [sin, cos]])
+    pairs = [split_host(part) for part in (np.cos(angles) * scale, np.sin(angles) * scale, folded)]
+    twiddle = np.zeros((n, n))
+    for i, values in enumerate((np.cos, np.sin)):
+        rest = values(2.0 * math.pi / n * idx)
+        for part in range(3):
+            twiddle[3 * i + part] = rest.astype(BF16)
+            rest = rest - twiddle[3 * i + part]
+    order = [pairs[0][0], pairs[1][0], pairs[0][1], pairs[1][1], *pairs[2], twiddle.astype(BF16)]
+    return np.stack(order)
+
+
+def haar_rows(positions, length):
+    block, within = positions // length * length, positions % length
+    hits = [(block + (within >> LEVELS), jnp.ones(positions.shape, F32))]
+    for level in range(1, LEVELS + 1):
+        sign = jnp.where((within >> (level - 1)) % 2 == 0, 1.0, -1.0)
+        hits.append((block + (length >> level) + (within >> level), sign))
+    return hits
+
+
+def haar_signs(n, length, flipped):
+    rows = lax.broadcasted_iota(jnp.int32, (1, n) if flipped else (n, 1), int(flipped))
+    positions = lax.broadcasted_iota(jnp.int32, (n, 1) if flipped else (1, n), int(not flipped))
+    out = jnp.zeros((n, n), F32)
+    for row, sign in haar_rows(positions, length):
+        out = jnp.where(rows == row, sign, out)
+    return out.astype(BF16)
 
 
 def split2(x):
@@ -70,27 +79,48 @@
     return jnp.concatenate(parts, axis=axis)
 
 
-def right_dft(re, im, dft, sign):
-    re_h, re_l = split2(re)
-    im_h, im_l = split2(im)
-    if sign > 0:
-        top, bottom = (re_h, im_h, re_l, im_l, re_h, im_h), (im_h, -re_h, im_l, -re_l, im_h, -re_h)
-    else:
-        top, bottom = (re_h, -im_h, re_l, -im_l, re_h, -im_h), (im_h, re_h, im_l, re_l, im_h, re_h)
-    values = joined([joined(top, 1), joined(bottom, 1)], 0)
-    return mm(values, joined([dft[0], dft[1], dft[0], dft[1], dft[3], dft[4]], 0))
-
-
-def left_dft(stacked, dft, sign):
-    plus, minus = (1, 2) if sign > 0 else (2, 1)
+def twiddles(const, half):
+    rows = const[6, 0:8, 0:half].astype(F32)
+    return rows[0:1] + rows[1:2] + rows[2:3], rows[3:4] + rows[4:5] + rows[5:6]
+
+
+def half_dfts(first, second, const):
+    high, low = split2(joined([first, second], 0))
+    return mm(joined([high, low, high], 1), joined([const[4], const[4], const[5]], 0))
+
+
+def right_dft(re, im, const):
+    n = re.shape[0]
+    half = n // 2
+    cos, sin = twiddles(const, half)
+    sum_re, sum_im = re[:, :half] + re[:, half:], im[:, :half] + im[:, half:]
+    dif_re, dif_im = re[:, :half] - re[:, half:], im[:, :half] - im[:, half:]
+    turned = joined([dif_re * cos + dif_im * sin, dif_im * cos - dif_re * sin], 1)
+    out = half_dfts(joined([sum_re, sum_im], 1), turned, const)
+    return joined([joined([out[:n, lo : lo + half], out[n:, lo : lo + half]], 1) for lo in (0, half)], 0)
+
+
+def right_idft(re, im, const):
+    n = re.shape[0]
+    half = n // 2
+    cos, sin = twiddles(const, half)
+    even, odd = (joined([re[:, lo : lo + half], -im[:, lo : lo + half]], 1) for lo in (0, half))
+    out = half_dfts(even, odd, const)
+    even_re, even_im, odd_re, odd_im = out[:n, :half], -out[:n, half:], out[n:, :half], -out[n:, half:]
+    turn_re, turn_im = odd_re * cos - odd_im * sin, odd_im * cos + odd_re * sin
+    out_re = joined([even_re + turn_re, even_re - turn_re], 1)
+    return joined([out_re, joined([even_im + turn_im, even_im - turn_im], 1)], 0)
+
+
+def left_dft(stacked, const, sign):
     high, low = split2(stacked)
 
     def table(base):
-        top = joined([dft[base], dft[base + plus]], 1)
-        bottom = joined([dft[base + minus], dft[base]], 1)
-        return joined([top, bottom], 0)
-
-    return mm(joined([table(0), table(0), table(3)], 1), joined([high, low, high], 0))
+        cos, sin = const[base], const[base + 1]
+        top, bottom = ((cos, sin), (-sin, cos)) if sign > 0 else ((cos, -sin), (sin, cos))
+        return joined([joined(top, 1), joined(bottom, 1)], 0)
+
+    return mm(joined([table(0), table(0), table(2)], 1), joined([high, low, high], 0))
 
 
 def labels(positions, length):
@@ -113,18 +143,18 @@
     for level in range(LEVELS):
         limits = jnp.where(band == level + 1, thr_ref[level : level + 1, :], limits)
     scale = col_scale * row_scale
-    half = mm(joined([const[6]] * 2, 1), joined(split2(joined([re, im], 1)), 0))
+    half = mm(joined([const[7]] * 2, 1), joined(split2(joined([re, im], 1)), 0))
     half = joined([half[:, :n], half[:, n:]], 0)
-    full = mm(joined(split2(half), 1), joined([const[8]] * 2, 0))
+    full = mm(joined(split2(half), 1), joined([const[9]] * 2, 0))
     coeffs = [full[:n] * scale, full[n:] * scale]
     magnitude = jnp.sqrt(coeffs[0] * coeffs[0] + coeffs[1] * coeffs[1])
     factor = jnp.maximum(magnitude - limits, 0.0) / jnp.maximum(magnitude, limits)
     factor = jnp.where(band <= LEVELS, factor, 1.0) * scale
     kept = joined([coeffs[0] * factor, coeffs[1] * factor], 1)
-    half = mm(joined([const[7]] * 2, 1), joined(split2(kept), 0))
+    half = mm(joined([const[8]] * 2, 1), joined(split2(kept), 0))
     half = joined([half[:, :n], half[:, n:]], 0)
     if last_rows is None:
-        full = mm(joined(split2(half), 1), joined([const[9]] * 2, 0))
+        full = mm(joined(split2(half), 1), joined([const[10]] * 2, 0))
         return full[:n], full[n:]
     full = mm_t(joined([last_rows] * 2, 1), joined(split2(half), 1))
     return full[:, :n], full[:, n:]
@@ -174,10 +204,10 @@
     return joined(out, 0)
 
 
-def adjoint(gridded, dft):
-    half = left_dft(gridded, dft, -1)
+def adjoint(gridded, const):
+    half = left_dft(gridded, const, -1)
     n = gridded.shape[0] // 2
-    return right_dft(half[:n], half[n:], dft, -1)
+    return right_idft(half[:n], half[n:], const)
 
 
 def pack_kernel(data_ref, weight_ref, bins_ref, count_ref, out_ref):
@@ -206,7 +236,10 @@
 def constants_kernel(thr_ref, const_ref, thr_out, const_out):
     for level in range(LEVELS):
         thr_out[level : level + 1, :] = jnp.full((1, thr_out.shape[1]), thr_ref[level])
-    const_out[...] = const_ref[...]
+    given, n = const_ref.shape[0], const_ref.shape[1]
+    const_out[0:given] = const_ref[...]
+    for i, (length, flipped) in enumerate(((n, False), (n, True), (2**LEVELS, True), (2**LEVELS, False))):
+        const_out[given + i] = haar_signs(n, length, flipped)
 
 
 def first_kernel(first_of, spoke_blocks, coil_blocks, live_total, counts, spk_dev, n, *refs):
@@ -229,7 +262,9 @@
             taken = taken + (depth < count).astype(jnp.int32)
     start = first_of()
     density = density_of(ro, n, live_total)
-    row_cells = lax.broadcasted_iota(jnp.int32, (n, ro), 0).astype(F32).astype(BF16)
+    row_order = lax.broadcasted_iota(jnp.int32, (n, ro), 0)
+    row_order = jnp.where(row_order < n // 2, 2 * row_order, 2 * row_order - n + 1)
+    row_cells = row_order.astype(F32).astype(BF16)
     side_rows = n // 2 + 2 * MARGIN
     low_cells = lax.broadcasted_iota(jnp.int32, (side_rows, half), 0) + (n - MARGIN)
     side_cells = [((low_cells + side * (n // 2)) % n).astype(F32).astype(BF16) for side in range(2)]
@@ -294,7 +329,7 @@
     est_out[0] = re
     est_out[1] = im
     mre, mim = map_ref[0], map_ref[1]
-    half = right_dft(mre * re - mim * im, mre * im + mim * re, const_ref, 1)
+    half = right_dft(mre * re - mim * im, mre * im + mim * re, const_ref)
     for side, values in enumerate(to_sides(left_dft(half, const_ref, 1))):
         sides_s[side] = values.astype(BF16)
     grid_s[...] = jnp.zeros_like(grid_s)
@@ -317,7 +352,7 @@
         sample_group(group)
         return carry
 
-    lax.fori_loop(1, groups, group_step, 0)
+    lax.fori_loop(1, groups, group_step, 0, unroll=True)
     grid_group(groups - 1, rows_s, cols_s, weighted_s, grid_s)
     back = adjoint(from_sides(grid_s), const_ref)
     conj_map(map_ref[0], map_ref[1], back, part_out)
@@ -349,7 +384,7 @@
     pick = lax.broadcasted_iota(jnp.int32, (rows, n), 1) == (
         lax.broadcasted_iota(jnp.int32, (rows, n), 0) + mine * rows
     )
-    own = mm(jnp.where(pick, 1.0, 0.0).astype(BF16), const_ref[8]).astype(BF16)
+    own = mm(jnp.where(pick, 1.0, 0.0).astype(BF16), const_ref[9]).astype(BF16)
     re, im = shrink(target[0], target[1], thr_ref, const_ref, own)
     out_ref[:, 0, :] = re
     out_ref[:, 1, :] = im
@@ -375,10 +410,10 @@
         compiler_params=PARAMS,
     )(kspace_data[0], jnp.swapaxes(interp_weights, 0, 1), sample_bins, spoke_count)
 
-    const = np.concatenate([dft_tables(n), haar_tables(n)])
+    const = dft_tables(n)
     limits, const = pl.pallas_call(
         constants_kernel,
-        out_shape=[jax.ShapeDtypeStruct((LEVELS, n), F32), jax.ShapeDtypeStruct(const.shape, BF16)],
+        out_shape=[jax.ShapeDtypeStruct((LEVELS, n), F32), jax.ShapeDtypeStruct((const.shape[0] + 4, n, n), BF16)],
         in_specs=[smem, vmem],
         out_specs=[vmem] * 2,
         compiler_params=PARAMS,

time: 71.6 us -> 69.6 us (0.972)
  Pallas kernels: 36.5 us -> 35 us
    pallas_call x3, Pallas kernels: 25.8 us -> 24.1 us  [local(): pl.pallas_call(functools.partial(step_kernel, len(estimate), len(parts)),...]
  transfers between devices with their start and end apart: 15 -> 15, of which waited for: 7 -> 7; matrix products, arithmetic and copies ran while one was open for 0% -> 0% of each run, Pallas kernels for 11% -> 12%
where the time goes in v6:
time: 69.6 us; the launch traced here: 69.3 us
  Pallas kernels  35 us (50%)
  starting transfers between devices  18.1 us (26%)
  waiting for transfers between devices  10.5 us (15%)
  local copies, waits for them, and re-layouts  4.79 us (7%)
  between operations  0.8 us (1%)
    pallas_call x3, Pallas kernels, local(): pl.pallas_call(functools.partial(step_kernel, len(estimate), len(parts)),...  24.1 us
    ppermute x6, starting transfers between devices, spread(): lax.ppermute(value, 'tile', [(i, i ^ shift) for i in range(n_tile)])  10.2 us
    pallas_call x1, Pallas kernels, local(): pl.pallas_call(functools.partial(first_kernel, first_of, spoke_blocks, co...  7.2 us
    ppermute x4, waiting for transfers between devices, parts_of(): return [part, lax.ppermute(part, 'spk', swap)]  6.15 us
    unnamed x12, local copies, waits for them, and re-layouts  4.79 us
    ppermute x4, starting transfers between devices, parts_of(): return [part, lax.ppermute(part, 'spk', swap)]  3.16 us
    ppermute x2, waiting for transfers between devices, to_coil(): lax.ppermute(value, ('coil', 'spk'), onto)  2.76 us
    ppermute x2, starting transfers between devices, to_coil(): lax.ppermute(value, ('coil', 'spk'), onto)  2.04 us
  transfers between devices with their start and end apart: 15, of which 7 were waited for; matrix products, arithmetic and copies ran while one was open for 0% of the time, Pallas kernels for 12%

profile of v6, /device:TPU:0, one launch (start us, length us, event | category | flops | bytes accessed | tf_op | source)
XLA Modules:
  0.0 69.3 jit_solution(11424849466654062110)
XLA Ops:
  0.7 0.0 copy-start.2
  0.7 0.7 %copy-done.2 = bf16[8,6,256]{2,0,1:T(8,128)(2,1)S(1)} copy-done((bf16[8,6,256]{2,0,1:T(8,128)(2,1)S(1)}, bf16[8,6,256]{2,0,1:T(8,128)(2,1)}, u32[]{:S(2)}) %copy-start.2) | copy-done | bytes 24600
  1.4 0.0 copy-start.3
  1.4 0.7 %copy-done.3 = bf16[1,8,2,256]{3,2,1,0:T(2,128)(2,1)S(1)} copy-done((bf16[1,8,2,256]{3,2,1,0:T(2,128)(2,1)S(1)}, bf16[1,8,2,256]{3,2,1,0:T(2,128)(2,1)}, u32[]{:S(2)}) %copy-start.3) | copy-done | bytes 8216
  2.1 0.0 copy-start.4
  2.1 0.7 %copy-done.4 = s32[8,256]{1,0:T(8,128)S(1)} copy-done((s32[8,256]{1,0:T(8,128)S(1)}, s32[8,256]{1,0:T(8,128)}, u32[]{:S(2)}) %copy-start.4) | copy-done | bytes 8216
  2.8 5.1 %collective-permute-start.2 = (bf16[88,256]{1,0:T(8,128)(2,1)S(1)}, bf16[88,256]{1,0:T(8,128)(2,1)S(1)}, u32[]{:S(2)}, u32[]{:S(2)}) collective-permute-start(bf16[88,256]{1,0:T(8,128)(2,1)S(1)} %shard_map.73.refs_0_), channel_id=1, source_target_pairs={{0,12},{4,8},{8,4},{12,0},{1,13},{5,9},{9,5},{13,1},{2,14},{6,10},... | collective-permute-start | bytes 135176 | tf_op jit(solution)/shard_map/ppermute | solution.py:429
  8.0 0.1 collective-permute-start.5
  8.0 0.9 %collective-permute-start.4 = (f32[32,2,256]{2,1,0:T(2,128)}, f32[32,2,256]{2,1,0:T(2,128)S(1)}, u32[]{:S(2)}, u32[]{:S(2)}) collective-permute-start(f32[32,2,256]{2,1,0:T(2,128)} %bitcast.4), channel_id=1, source_target_pairs={{0,8},{4,12},{8,0},{12,4},{1,9},{5,13},{9,1},{13,5},{2,10},{6,14},... | collective-permute-start | bytes 196616 | tf_op jit(solution)/shard_map/ppermute | solution.py:429
  9.0 3.4 %collective-permute-start.3 = (f32[32,2,256]{2,1,0:T(2,128)}, f32[32,2,256]{2,1,0:T(2,128)S(1)}, u32[]{:S(2)}, u32[]{:S(2)}) collective-permute-start(f32[32,2,256]{2,1,0:T(2,128)} %bitcast.5), channel_id=1, source_target_pairs={{0,4},{4,0},{8,12},{12,8},{1,5},{5,1},{9,13},{13,9},{2,6},{6,2},{1... | collective-permute-start | bytes 196616 | tf_op jit(solution)/shard_map/ppermute | solution.py:429
  12.3 0.0 collective-permute-start.1
  12.3 0.0 collective-permute-done.2.refs_3_
  12.3 0.6 collective-permute-start
  13.0 0.0 copy-start
  13.0 1.2 %copy-done = bf16[7,256,256]{2,1,0:T(8,128)(2,1)S(1)} copy-done((bf16[7,256,256]{2,1,0:T(8,128)(2,1)S(1)}, bf16[7,256,256]{2,1,0:T(8,128)(2,1)}, u32[]{:S(2)}) %copy-start) | copy-done | bytes 917528
  14.2 0.7 copy-done.5
  14.8 1.2 %shard_map.74 = (f32[3,256]{1,0:T(4,128)S(1)}, bf16[11,256,256]{2,1,0:T(8,128)(2,1)S(1)}) custom-call(f32[3]{0:T(128)S(1)} %copy-done.5, bf16[7,256,256]{2,1,0:T(8,128)(2,1)S(1)} %copy-done), custom_call_target="tpu_custom_call" | custom-call | tf_op jit(solution)/shard_map/pallas_call | solution.py:414
  16.1 1.2 %collective-permute-done.1.refs_2_ = bf16[88,256]{1,0:T(8,128)(2,1)S(1)} collective-permute-done((bf16[88,256]{1,0:T(8,128)(2,1)S(1)}, bf16[88,256]{1,0:T(8,128)(2,1)S(1)}, u32[]{:S(2)}, u32[]{:S(2)}) %collective-permute-start.1) | collective-permute-done | bytes 45088 | tf_op jit(solution)/shard_map/ppermute | solution.py:429
  17.3 0.3 collective-permute-done.refs_1_
  17.7 0.0 collective-permute-done.5.refs_3_
  17.7 0.0 collective-permute-done.4.refs_2_
  17.7 0.0 collective-permute-done.3.refs_1_
  17.7 0.0 copy-start.1
  17.7 0.8 %copy-done.1 = f32[1,32,2,256]{3,2,1,0:T(2,128)S(1)} copy-done((f32[1,32,2,256]{3,2,1,0:T(2,128)S(1)}, f32[1,32,2,256]{3,2,1,0:T(2,128)}, u32[]{:S(2)}) %copy-start.1) | copy-done | bytes 65560
  18.5 1.5 %collective-permute-start.7 = (f32[4,32,2,256]{3,2,1,0:T(2,128)S(1)}, f32[4,32,2,256]{3,2,1,0:T(2,128)S(1)}, u32[]{:S(2)}, u32[]{:S(2)}) collective-permute-start(f32[4,32,2,256]{3,2,1,0:T(2,128)S(1)} %shard_map.76.refs_0_), channel_id=1, source_target_pairs={{0,2},{3,1},{1,0},{2,3},{4,6},{7,5},{5,4},{6,7},{8,10},{11,9},{9,8... | collective-permute-start | bytes 786440 | tf_op jit(solution)/shard_map/ppermute | solution.py:433
  20.1 0.7 collective-permute-start.6
  20.7 1.4 %collective-permute-start.8 = (bf16[4,72,256]{2,1,0:T(8,128)(2,1)S(1)}, bf16[4,72,256]{2,1,0:T(8,128)(2,1)S(1)}, u32[]{:S(2)}, u32[]{:S(2)}) collective-permute-start(bf16[4,72,256]{2,1,0:T(8,128)(2,1)S(1)} %get-tuple-element.47.refs_0_), channel_id=1, source_target_pairs={{0,1},{1,0},{2,3},{3,2},{4,5},{5,4},{6,7},{7,6},{8,9},{9,8},{10,11... | collective-permute-start | bytes 442376 | tf_op jit(solution)/shard_map/ppermute | solution.py:469
  22.2 0.5 collective-permute-start.10
  22.7 0.7 collective-permute-start.9
  23.4 2.8 %collective-permute-done.10.refs_4_ = bf16[4,16,256]{2,1,0:T(8,128)(2,1)S(1)} collective-permute-done((bf16[4,16,256]{2,1,0:T(8,128)(2,1)S(1)}, bf16[4,16,256]{2,1,0:T(8,128)(2,1)S(1)}, u32[]{:S(2)}, u32[]{:S(2)}) %collective-permute-start.10) | collective-permute-done | bytes 32800 | tf_op jit(solution)/shard_map/ppermute | solution.py:433
  26.1 0.0 collective-permute-done.9.refs_3_
  26.1 0.0 collective-permute-done.8.refs_1_
  26.1 7.2 %shard_map.77 = (bf16[4,256,2048]{2,1,0:T(8,128)(2,1)S(1)}, bf16[4,2,144,1024]{3,2,1,0:T(8,128)(2,1)S(1)}, f32[4,2,3,1024]{3,2,1,0:T(4,128)S(1)}, f32[512,256]{1,0:T(8,128)S(1)}) custom-call(bf16[4,72,256]{2,1,0:T(8,128)(2,1)S(1)} %get-tuple-element.47.refs_0_, bf16[4,72,256]{2,1,0:T(8,128)(2,1)S(1)} %collective-permute-done.8.refs_1_, ...), custom_call_target="tpu_custom_call" | custom-call | tf_op jit(solution)/shard_map/pallas_call | solution.py:506
  33.3 0.0 collective-permute-done.7.refs_2_
  33.4 0.0 collective-permute-done.6.refs_1_
  33.4 0.5 shard_map.78
  33.8 1.8 %collective-permute-start.11 = (f32[2,256,256]{2,1,0:T(8,128)S(1)}, f32[2,256,256]{2,1,0:T(8,128)S(1)}, u32[]{:S(2)}, u32[]{:S(2)}) collective-permute-start(f32[2,256,256]{2,1,0:T(8,128)S(1)} %get-tuple-element.50.refs_1_), channel_id=1, source_target_pairs={{0,1},{1,0},{2,3},{3,2},{4,5},{5,4},{6,7},{7,6},{8,9},{9,8},{10,11... | collective-permute-start | bytes 1572872 | tf_op jit(solution)/shard_map/ppermute | solution.py:484
  35.7 1.5 %collective-permute-done.11.refs_2_ = f32[2,256,256]{2,1,0:T(8,128)S(1)} collective-permute-done((f32[2,256,256]{2,1,0:T(8,128)S(1)}, f32[2,256,256]{2,1,0:T(8,128)S(1)}, u32[]{:S(2)}, u32[]{:S(2)}) %collective-permute-start.11) | collective-permute-done | bytes 524320 | tf_op jit(solution)/shard_map/ppermute | solution.py:484
  37.2 8.0 %shard_map.79 = (f32[2,256,256]{2,1,0:T(8,128)S(1)}, f32[2,256,256]{2,1,0:T(8,128)S(1)}) custom-call(f32[3,256]{1,0:T(4,128)S(1)} %get-tuple-element.35.refs_0_.thr_ref, f32[2,256,256]{2,1,0:T(8,128)S(1)} %get-tuple-element.50.refs_1_, f32[2,256,256]{2,1,0:T(8,128)S(1)} %collective-permute-done.11.refs_2_, ...), custom_call_target="tpu_custom_call" | custom-call | tf_op jit(solution)/shard_map/pallas_call | solution.py:536
  45.2 0.4 collective-permute-start.12
  45.6 1.5 %collective-permute-done.12.refs_3_ = f32[2,256,256]{2,1,0:T(8,128)S(1)} collective-permute-done((f32[2,256,256]{2,1,0:T(8,128)S(1)}, f32[2,256,256]{2,1,0:T(8,128)S(1)}, u32[]{:S(2)}, u32[]{:S(2)}) %collective-permute-start.12) | collective-permute-done | bytes 524320 | tf_op jit(solution)/shard_map/ppermute | solution.py:484
  47.2 8.2 %shard_map.80 = (f32[2,256,256]{2,1,0:T(8,128)S(1)}, f32[2,256,256]{2,1,0:T(8,128)S(1)}) custom-call(f32[3,256]{1,0:T(4,128)S(1)} %get-tuple-element.35.refs_0_.thr_ref, f32[2,256,256]{2,1,0:T(8,128)S(1)} %get-tuple-element.55.refs_1_, f32[2,256,256]{2,1,0:T(8,128)S(1)} %get-tuple-element.56.refs_2_, f32[2,256,256]{2,1,0:T(8,128)S(1)} %collective-permute-done.12.refs_3_, ...), custom_call_target="tpu_custom_call" | custom-call | tf_op jit(solution)/shard_map/pallas_call | solution.py:536
  55.3 0.4 collective-permute-start.13
  55.8 1.5 %collective-permute-done.13.refs_3_ = f32[2,256,256]{2,1,0:T(8,128)S(1)} collective-permute-done((f32[2,256,256]{2,1,0:T(8,128)S(1)}, f32[2,256,256]{2,1,0:T(8,128)S(1)}, u32[]{:S(2)}, u32[]{:S(2)}) %collective-permute-start.13) | collective-permute-done | bytes 524320 | tf_op jit(solution)/shard_map/ppermute | solution.py:484
  57.3 8.0 %shard_map.81 = (f32[2,256,256]{2,1,0:T(8,128)S(1)}, f32[2,256,256]{2,1,0:T(8,128)S(1)}) custom-call(f32[3,256]{1,0:T(4,128)S(1)} %get-tuple-element.35.refs_0_.thr_ref, f32[2,256,256]{2,1,0:T(8,128)S(1)} %get-tuple-element.57.refs_1_, f32[2,256,256]{2,1,0:T(8,128)S(1)} %get-tuple-element.58.refs_2_, f32[2,256,256]{2,1,0:T(8,128)S(1)} %collective-permute-done.13.refs_3_, ...), custom_call_target="tpu_custom_call" | custom-call | tf_op jit(solution)/shard_map/pallas_call | solution.py:536
  65.3 0.4 collective-permute-start.14
  65.7 1.5 %collective-permute-done.14.refs_1_ = f32[2,256,256]{2,1,0:T(8,128)S(1)} collective-permute-done((f32[2,256,256]{2,1,0:T(8,128)S(1)}, f32[2,256,256]{2,1,0:T(8,128)S(1)}, u32[]{:S(2)}, u32[]{:S(2)}) %collective-permute-start.14) | collective-permute-done | bytes 524320 | tf_op jit(solution)/shard_map/ppermute | solution.py:484
  67.2 2.0 %shard_map.82 = f32[32,2,256]{2,1,0:T(2,128)} custom-call(f32[3,256]{1,0:T(4,128)S(1)} %get-tuple-element.35.refs_0_.thr_ref, f32[2,256,256]{2,1,0:T(8,128)S(1)} %get-tuple-element.59.est_ref, f32[2,256,256]{2,1,0:T(8,128)S(1)} %get-tuple-element.60.refs_0_, f32[2,256,256]{2,1,0:T(8,128)S(1)} %collective-permute-done.14.refs_1_, ...), custom_call_target="tpu_custom_call" | custom-call | tf_op jit(solution)/shard_map/pallas_call | solution.py:546
  (4 shorter events, 0.1 us)
Async XLA Ops:
  0.7 0.7 %copy-start.2 = (bf16[8,6,256]{2,0,1:T(8,128)(2,1)S(1)}, bf16[8,6,256]{2,0,1:T(8,128)(2,1)}, u32[]{:S(2)}) copy-start(bf16[8,6,256]{2,0,1:T(8,128)(2,1)} %param.9) | copy-start | bytes 73732
  1.4 0.7 %copy-start.3 = (bf16[1,8,2,256]{3,2,1,0:T(2,128)(2,1)S(1)}, bf16[1,8,2,256]{3,2,1,0:T(2,128)(2,1)}, u32[]{:S(2)}) copy-start(bf16[1,8,2,256]{3,2,1,0:T(2,128)(2,1)} %param.8) | copy-start | bytes 24580
  2.1 0.7 %copy-start.4 = (s32[8,256]{1,0:T(8,128)S(1)}, s32[8,256]{1,0:T(8,128)}, u32[]{:S(2)}) copy-start(s32[8,256]{1,0:T(8,128)} %bins_ref.1) | copy-start | bytes 24580
  2.8 9.5 %collective-permute-start.2 = (bf16[88,256]{1,0:T(8,128)(2,1)S(1)}, bf16[88,256]{1,0:T(8,128)(2,1)S(1)}, u32[]{:S(2)}, u32[]{:S(2)}) collective-permute-start(bf16[88,256]{1,0:T(8,128)(2,1)S(1)} %shard_map.73.refs_0_), channel_id=1, source_target_pairs={{0,12},{4,8},{8,4},{12,0},{1,13},{5,9},{9,5},{13,1},{2,14},{6,10},... | collective-permute-start | bytes 135176 | tf_op jit(solution)/shard_map/ppermute | solution.py:429
  8.0 9.7 %collective-permute-start.5 = (f32[32,2,256]{2,1,0:T(2,128)}, f32[32,2,256]{2,1,0:T(2,128)S(1)}, u32[]{:S(2)}, u32[]{:S(2)}) collective-permute-start(f32[32,2,256]{2,1,0:T(2,128)} %bitcast.3), channel_id=1, source_target_pairs={{0,12},{4,8},{8,4},{12,0},{1,13},{5,9},{9,5},{13,1},{2,14},{6,10},... | collective-permute-start | bytes 196616 | tf_op jit(solution)/shard_map/ppermute | solution.py:429
  8.0 9.6 %collective-permute-start.4 = (f32[32,2,256]{2,1,0:T(2,128)}, f32[32,2,256]{2,1,0:T(2,128)S(1)}, u32[]{:S(2)}, u32[]{:S(2)}) collective-permute-start(f32[32,2,256]{2,1,0:T(2,128)} %bitcast.4), channel_id=1, source_target_pairs={{0,8},{4,12},{8,0},{12,4},{1,9},{5,13},{9,1},{13,5},{2,10},{6,14},... | collective-permute-start | bytes 196616 | tf_op jit(solution)/shard_map/ppermute | solution.py:429
  9.0 8.7 %collective-permute-start.3 = (f32[32,2,256]{2,1,0:T(2,128)}, f32[32,2,256]{2,1,0:T(2,128)S(1)}, u32[]{:S(2)}, u32[]{:S(2)}) collective-permute-start(f32[32,2,256]{2,1,0:T(2,128)} %bitcast.5), channel_id=1, source_target_pairs={{0,4},{4,0},{8,12},{12,8},{1,5},{5,1},{9,13},{13,9},{2,6},{6,2},{1... | collective-permute-start | bytes 196616 | tf_op jit(solution)/shard_map/ppermute | solution.py:429
  12.3 5.0 %collective-permute-start.1 = (bf16[88,256]{1,0:T(8,128)(2,1)S(1)}, bf16[88,256]{1,0:T(8,128)(2,1)S(1)}, u32[]{:S(2)}, u32[]{:S(2)}) collective-permute-start(bf16[88,256]{1,0:T(8,128)(2,1)S(1)} %shard_map.73.refs_0_), channel_id=1, source_target_pairs={{0,8},{4,12},{8,0},{12,4},{1,9},{5,13},{9,1},{13,5},{2,10},{6,14},... | collective-permute-start | bytes 135176 | tf_op jit(solution)/shard_map/ppermute | solution.py:429
  12.3 5.3 %collective-permute-start = (bf16[88,256]{1,0:T(8,128)(2,1)S(1)}, bf16[88,256]{1,0:T(8,128)(2,1)S(1)}, u32[]{:S(2)}, u32[]{:S(2)}) collective-permute-start(bf16[88,256]{1,0:T(8,128)(2,1)S(1)} %shard_map.73.refs_0_), channel_id=1, source_target_pairs={{0,4},{4,0},{8,12},{12,8},{1,5},{5,1},{9,13},{13,9},{2,6},{6,2},{1... | collective-permute-start | bytes 135176 | tf_op jit(solution)/shard_map/ppermute | solution.py:429
  13.0 1.2 %copy-start = (bf16[7,256,256]{2,1,0:T(8,128)(2,1)S(1)}, bf16[7,256,256]{2,1,0:T(8,128)(2,1)}, u32[]{:S(2)}) copy-start(bf16[7,256,256]{2,1,0:T(8,128)(2,1)} %constant.2.clone.const_ref) | copy-start | bytes 2752516
  14.2 0.7 copy-start.5
  17.7 0.8 %copy-start.1 = (f32[1,32,2,256]{3,2,1,0:T(2,128)S(1)}, f32[1,32,2,256]{3,2,1,0:T(2,128)}, u32[]{:S(2)}) copy-start(f32[1,32,2,256]{3,2,1,0:T(2,128)} %param.7) | copy-start | bytes 196612
  18.5 14.8 %collective-permute-start.7 = (f32[4,32,2,256]{3,2,1,0:T(2,128)S(1)}, f32[4,32,2,256]{3,2,1,0:T(2,128)S(1)}, u32[]{:S(2)}, u32[]{:S(2)}) collective-permute-start(f32[4,32,2,256]{3,2,1,0:T(2,128)S(1)} %shard_map.76.refs_0_), channel_id=1, source_target_pairs={{0,2},{3,1},{1,0},{2,3},{4,6},{7,5},{5,4},{6,7},{8,10},{11,9},{9,8... | collective-permute-start | bytes 786440 | tf_op jit(solution)/shard_map/ppermute | solution.py:433
  20.1 13.3 %collective-permute-start.6 = (f32[4,32,2,256]{3,2,1,0:T(2,128)S(1)}, f32[4,32,2,256]{3,2,1,0:T(2,128)S(1)}, u32[]{:S(2)}, u32[]{:S(2)}) collective-permute-start(f32[4,32,2,256]{3,2,1,0:T(2,128)S(1)} %shard_map.76.refs_0_), channel_id=1, source_target_pairs={{1,2},{2,1},{5,6},{6,5},{9,10},{10,9},{13,14},{14,13},{17,18},{18,... | collective-permute-start | bytes 786440 | tf_op jit(solution)/shard_map/ppermute | solution.py:433
  20.7 5.4 %collective-permute-start.8 = (bf16[4,72,256]{2,1,0:T(8,128)(2,1)S(1)}, bf16[4,72,256]{2,1,0:T(8,128)(2,1)S(1)}, u32[]{:S(2)}, u32[]{:S(2)}) collective-permute-start(bf16[4,72,256]{2,1,0:T(8,128)(2,1)S(1)} %get-tuple-element.47.refs_0_), channel_id=1, source_target_pairs={{0,1},{1,0},{2,3},{3,2},{4,5},{5,4},{6,7},{7,6},{8,9},{9,8},{10,11... | collective-permute-start | bytes 442376 | tf_op jit(solution)/shard_map/ppermute | solution.py:469
  22.2 4.0 %collective-permute-start.10 = (bf16[4,16,256]{2,1,0:T(8,128)(2,1)S(1)}, bf16[4,16,256]{2,1,0:T(8,128)(2,1)S(1)}, u32[]{:S(2)}, u32[]{:S(2)}) collective-permute-start(bf16[4,16,256]{2,1,0:T(8,128)(2,1)S(1)} %get-tuple-element.42.refs_2_), channel_id=1, source_target_pairs={{0,2},{3,1},{1,0},{2,3},{4,6},{7,5},{5,4},{6,7},{8,10},{11,9},{9,8... | collective-permute-start | bytes 98312 | tf_op jit(solution)/shard_map/ppermute | solution.py:433
  22.7 3.4 %collective-permute-start.9 = (bf16[4,16,256]{2,1,0:T(8,128)(2,1)S(1)}, bf16[4,16,256]{2,1,0:T(8,128)(2,1)S(1)}, u32[]{:S(2)}, u32[]{:S(2)}) collective-permute-start(bf16[4,16,256]{2,1,0:T(8,128)(2,1)S(1)} %get-tuple-element.42.refs_2_), channel_id=1, source_target_pairs={{1,2},{2,1},{5,6},{6,5},{9,10},{10,9},{13,14},{14,13},{17,18},{18,... | collective-permute-start | bytes 98312 | tf_op jit(solution)/shard_map/ppermute | solution.py:433
  33.8 3.4 %collective-permute-start.11 = (f32[2,256,256]{2,1,0:T(8,128)S(1)}, f32[2,256,256]{2,1,0:T(8,128)S(1)}, u32[]{:S(2)}, u32[]{:S(2)}) collective-permute-start(f32[2,256,256]{2,1,0:T(8,128)S(1)} %get-tuple-element.50.refs_1_), channel_id=1, source_target_pairs={{0,1},{1,0},{2,3},{3,2},{4,5},{5,4},{6,7},{7,6},{8,9},{9,8},{10,11... | collective-permute-start | bytes 1572872 | tf_op jit(solution)/shard_map/ppermute | solution.py:484
  45.2 2.0 %collective-permute-start.12 = (f32[2,256,256]{2,1,0:T(8,128)S(1)}, f32[2,256,256]{2,1,0:T(8,128)S(1)}, u32[]{:S(2)}, u32[]{:S(2)}) collective-permute-start(f32[2,256,256]{2,1,0:T(8,128)S(1)} %get-tuple-element.56.refs_2_), channel_id=1, source_target_pairs={{0,1},{1,0},{2,3},{3,2},{4,5},{5,4},{6,7},{7,6},{8,9},{9,8},{10,11... | collective-permute-start | bytes 1572872 | tf_op jit(solution)/shard_map/ppermute | solution.py:484
  55.3 2.0 %collective-permute-start.13 = (f32[2,256,256]{2,1,0:T(8,128)S(1)}, f32[2,256,256]{2,1,0:T(8,128)S(1)}, u32[]{:S(2)}, u32[]{:S(2)}) collective-permute-start(f32[2,256,256]{2,1,0:T(8,128)S(1)} %get-tuple-element.58.refs_2_), channel_id=1, source_target_pairs={{0,1},{1,0},{2,3},{3,2},{4,5},{5,4},{6,7},{7,6},{8,9},{9,8},{10,11... | collective-permute-start | bytes 1572872 | tf_op jit(solution)/shard_map/ppermute | solution.py:484
  65.3 2.0 %collective-permute-start.14 = (f32[2,256,256]{2,1,0:T(8,128)S(1)}, f32[2,256,256]{2,1,0:T(8,128)S(1)}, u32[]{:S(2)}, u32[]{:S(2)}) collective-permute-start(f32[2,256,256]{2,1,0:T(8,128)S(1)} %get-tuple-element.60.refs_0_), channel_id=1, source_target_pairs={{0,1},{1,0},{2,3},{3,2},{4,5},{5,4},{6,7},{7,6},{8,9},{9,8},{10,11... | collective-permute-start | bytes 1572872 | tf_op jit(solution)/shard_map/ppermute | solution.py:484

commit v7 on v6

--- a/solution.py
+++ b/solution.py
@@ -19,29 +19,40 @@
 BF16 = jnp.bfloat16
 
 
-def split_host(table):
-    high = table.astype(BF16)
-    low = (table - high.astype(np.float64)).astype(BF16)
-    return high, low
-
-
-def dft_tables(n):
-    half = n // 2
-    idx = np.arange(n)
-    angles = 2.0 * math.pi / n * (np.outer(idx, idx) % n)
-    scale = 1.0 / math.sqrt(n)
-    small = 2.0 * math.pi / half * (np.outer(idx[:half], idx[:half]) % half)
-    cos, sin = np.cos(small) * scale, np.sin(small) * scale
-    folded = np.block([[cos, -sin], [sin, cos]])
-    pairs = [split_host(part) for part in (np.cos(angles) * scale, np.sin(angles) * scale, folded)]
-    twiddle = np.zeros((n, n))
-    for i, values in enumerate((np.cos, np.sin)):
-        rest = values(2.0 * math.pi / n * idx)
-        for part in range(3):
-            twiddle[3 * i + part] = rest.astype(BF16)
-            rest = rest - twiddle[3 * i + part]
-    order = [pairs[0][0], pairs[1][0], pairs[0][1], pairs[1][1], *pairs[2], twiddle.astype(BF16)]
-    return np.stack(order)
+STRIDE = 16
+
+
+def dft_seeds(n):
+    coarse, fine = STRIDE * np.arange(n // STRIDE), np.arange(STRIDE)
+    rows = []
+    for positions, scale in ((coarse, 1.0), (fine, 1.0 / math.sqrt(n)), (2 * fine, 1.0 / math.sqrt(n))):
+        angles = 2.0 * math.pi / n * (np.outer(positions, np.arange(n)) % n)
+        rows += [np.cos(angles) * scale, np.sin(angles) * scale]
+    return np.concatenate(rows).astype(np.float32)
+
+
+def dft_kernel(seed_ref, out_ref):
+    n = seed_ref.shape[1]
+    half, coarse = n // 2, n // STRIDE
+    at = [0, coarse, 2 * coarse, 2 * coarse + STRIDE, 2 * coarse + 2 * STRIDE, 2 * coarse + 3 * STRIDE]
+    fine = [seed_ref[start : start + STRIDE, :] for start in at[2:]]
+
+    def turned(i, cos, sin):
+        big_cos, big_sin = (seed_ref[start + i : start + i + 1, :] for start in at[:2])
+        return big_cos * cos - big_sin * sin, big_sin * cos + big_cos * sin
+
+    for i in range(coarse):
+        rows = slice(i * STRIDE, (i + 1) * STRIDE)
+        for plane, values in enumerate(turned(i, fine[0], fine[1])):
+            out_ref[plane, rows, :], out_ref[plane + 2, rows, :] = split2(values)
+    for i in range(coarse // 2):
+        cos, sin = (values[:, :half] for values in turned(2 * i, fine[2], fine[3]))
+        for start, values in ((0, (cos, -sin)), (half, (sin, cos))):
+            rows = slice(start + i * STRIDE, start + (i + 1) * STRIDE)
+            out_ref[4, rows, :], out_ref[5, rows, :] = split2(joined(values, 1))
+    parts = [part.astype(F32) for values in fine[:2] for part in split3(values[1:2] * math.sqrt(n))]
+    parts.append(jnp.zeros((STRIDE - len(parts), n), F32))
+    out_ref[6, 0:STRIDE, :] = joined(parts, 0).astype(BF16)
 
 
 def haar_rows(positions, length):
@@ -65,6 +76,11 @@
 def split2(x):
     high = x.astype(BF16)
     return high, (x - high.astype(F32)).astype(BF16)
+
+
+def split3(x):
+    high, mid = split2(x)
+    return high, mid, (x - high.astype(F32) - mid.astype(F32)).astype(BF16)
 
 
 def mm(a, b):
@@ -130,7 +146,7 @@
     return out
 
 
-def shrink(re, im, thr_ref, const, last_rows=None):
+def shrink(re, im, thr_ref, haar, last_rows=None):
     n = re.shape[0]
     block = 2**LEVELS
     col_pos = lax.broadcasted_iota(jnp.int32, (n, 1), 0)
@@ -143,18 +159,18 @@
     for level in range(LEVELS):
         limits = jnp.where(band == level + 1, thr_ref[level : level + 1, :], limits)
     scale = col_scale * row_scale
-    half = mm(joined([const[7]] * 2, 1), joined(split2(joined([re, im], 1)), 0))
+    half = mm(joined([haar[0]] * 2, 1), joined(split2(joined([re, im], 1)), 0))
     half = joined([half[:, :n], half[:, n:]], 0)
-    full = mm(joined(split2(half), 1), joined([const[9]] * 2, 0))
+    full = mm(joined(split2(half), 1), joined([haar[2]] * 2, 0))
     coeffs = [full[:n] * scale, full[n:] * scale]
     magnitude = jnp.sqrt(coeffs[0] * coeffs[0] + coeffs[1] * coeffs[1])
     factor = jnp.maximum(magnitude - limits, 0.0) / jnp.maximum(magnitude, limits)
     factor = jnp.where(band <= LEVELS, factor, 1.0) * scale
     kept = joined([coeffs[0] * factor, coeffs[1] * factor], 1)
-    half = mm(joined([const[8]] * 2, 1), joined(split2(kept), 0))
+    half = mm(joined([haar[1]] * 2, 1), joined(split2(kept), 0))
     half = joined([half[:, :n], half[:, n:]], 0)
     if last_rows is None:
-        full = mm(joined(split2(half), 1), joined([const[10]] * 2, 0))
+        full = mm(joined(split2(half), 1), joined([haar[3]] * 2, 0))
         return full[:n], full[n:]
     full = mm_t(joined([last_rows] * 2, 1), joined(split2(half), 1))
     return full[:, :n], full[:, n:]
@@ -233,13 +249,12 @@
         refs[-1][i] = piece[...]
 
 
-def constants_kernel(thr_ref, const_ref, thr_out, const_out):
+def haar_kernel(thr_ref, thr_out, haar_out):
+    n = haar_out.shape[1]
     for level in range(LEVELS):
-        thr_out[level : level + 1, :] = jnp.full((1, thr_out.shape[1]), thr_ref[level])
-    given, n = const_ref.shape[0], const_ref.shape[1]
-    const_out[0:given] = const_ref[...]
+        thr_out[level : level + 1, :] = jnp.full((1, n), thr_ref[level])
     for i, (length, flipped) in enumerate(((n, False), (n, True), (2**LEVELS, True), (2**LEVELS, False))):
-        const_out[given + i] = haar_signs(n, length, flipped)
+        haar_out[i] = haar_signs(n, length, flipped)
 
 
 def first_kernel(first_of, spoke_blocks, coil_blocks, live_total, counts, spk_dev, n, *refs):
@@ -321,11 +336,11 @@
     thr_ref, refs = refs[0], refs[1:]
     est_ref, refs = refs[0] if n_est else None, refs[n_est:]
     part_refs, refs = refs[:n_parts], refs[n_parts:]
-    map_ref, data_ref, const_ref, rows_s, cols_s, est_out, part_out, sides_s, weighted_s, grid_s = refs
+    map_ref, data_ref, const_ref, haar_ref, rows_s, cols_s, est_out, part_out, sides_s, weighted_s, grid_s = refs
     groups, _, _, span = weighted_s.shape
     n, rows = map_ref.shape[1], cols_s.shape[2]
     target = target_of(est_ref, part_refs)
-    re, im = shrink(target[0], target[1], thr_ref, const_ref)
+    re, im = shrink(target[0], target[1], thr_ref, haar_ref)
     est_out[0] = re
     est_out[1] = im
     mre, mim = map_ref[0], map_ref[1]
@@ -377,15 +392,15 @@
 
 
 def last_kernel(n_parts, rows, mine_of, thr_ref, est_ref, *refs):
-    part_refs, (const_ref, out_ref) = refs[:n_parts], refs[n_parts:]
+    part_refs, (haar_ref, out_ref) = refs[:n_parts], refs[n_parts:]
     n = est_ref.shape[1]
     target = target_of(est_ref, part_refs)
     mine = mine_of()
     pick = lax.broadcasted_iota(jnp.int32, (rows, n), 1) == (
         lax.broadcasted_iota(jnp.int32, (rows, n), 0) + mine * rows
     )
-    own = mm(jnp.where(pick, 1.0, 0.0).astype(BF16), const_ref[9]).astype(BF16)
-    re, im = shrink(target[0], target[1], thr_ref, const_ref, own)
+    own = mm(jnp.where(pick, 1.0, 0.0).astype(BF16), haar_ref[2]).astype(BF16)
+    re, im = shrink(target[0], target[1], thr_ref, haar_ref, own)
     out_ref[:, 0, :] = re
     out_ref[:, 1, :] = im
 
@@ -410,14 +425,13 @@
         compiler_params=PARAMS,
     )(kspace_data[0], jnp.swapaxes(interp_weights, 0, 1), sample_bins, spoke_count)
 
-    const = dft_tables(n)
-    limits, const = pl.pallas_call(
-        constants_kernel,
-        out_shape=[jax.ShapeDtypeStruct((LEVELS, n), F32), jax.ShapeDtypeStruct((const.shape[0] + 4, n, n), BF16)],
-        in_specs=[smem, vmem],
-        out_specs=[vmem] * 2,
+    const = pl.pallas_call(
+        dft_kernel,
+        out_shape=jax.ShapeDtypeStruct((7, n, n), BF16),
+        in_specs=[vmem],
+        out_specs=vmem,
         compiler_params=PARAMS,
-    )(thresholds, jnp.asarray(const))
+    )(jnp.asarray(dft_seeds(n)))
 
     if by_core:
         onto = [(0, 2), (3, 1), (1, 0), (2, 3)]
@@ -455,7 +469,7 @@
         pieces = spread(bundle)
         own_map, bundle = lax.optimization_barrier((own_map, bundle))
         map_pieces = spread(own_map)
-        pieces, limits, const = lax.optimization_barrier((pieces, limits, const))
+        pieces, const = lax.optimization_barrier((pieces, const))
         own_data, own_spokes = pl.pallas_call(
             functools.partial(join_kernel, data_rows),
             out_shape=[
@@ -530,9 +544,17 @@
         compiler_params=PARAMS,
     )(*maps, back)
     estimate = []
+    part, thresholds = lax.optimization_barrier((part, thresholds))
+    limits, haar = pl.pallas_call(
+        haar_kernel,
+        out_shape=[jax.ShapeDtypeStruct((LEVELS, n), F32), jax.ShapeDtypeStruct((4, n, n), BF16)],
+        in_specs=[smem],
+        out_specs=[vmem] * 2,
+        compiler_params=PARAMS,
+    )(thresholds)
     parts = parts_of(part)
     for _ in range(1, ITERS):
-        inputs = (*estimate, *parts, map_t, data, const, row_tab, col_tab)
+        inputs = (*estimate, *parts, map_t, data, const, haar, row_tab, col_tab)
         *estimate, part = pl.pallas_call(
             functools.partial(step_kernel, len(estimate), len(parts)),
             out_shape=[image, image],
@@ -549,7 +571,7 @@
         in_specs=[vmem] * (len(parts) + 3),
         out_specs=vmem,
         compiler_params=PARAMS,
-    )(limits, *estimate, *parts, const)
+    )(limits, *estimate, *parts, haar)
 
 
 def solution(mesh):

time: 69.6 us -> 69.5 us (level)
  local copies, waits for them, and re-layouts: 4.79 us -> 3.85 us
  waiting for transfers between devices: 10.5 us -> 11.3 us
    ppermute x6, waiting for transfers between devices: 1.58 us -> 3.59 us  [spread(): lax.ppermute(value, 'tile', [(i, i ^ shift) for i in range(n_tile)])]
    ppermute x4, waiting for transfers between devices: 6.15 us -> 4.94 us  [parts_of(): return [part, lax.ppermute(part, 'spk', swap)]]
    unnamed x12, local copies, waits for them, and re-layouts: 4.79 us -> 3.85 us
where the time goes in v7:
time: 69.5 us; the launch traced here: 69.1 us
  Pallas kernels  35.1 us (51%)
  starting transfers between devices  18.1 us (26%)
  waiting for transfers between devices  11.3 us (16%)
  local copies, waits for them, and re-layouts  3.85 us (6%)
  between operations  0.81 us (1%)
    pallas_call x3, Pallas kernels, local(): pl.pallas_call(functools.partial(step_kernel, len(estimate), len(parts)),...  24 us
    ppermute x6, starting transfers between devices, spread(): lax.ppermute(value, 'tile', [(i, i ^ shift) for i in range(n_tile)])  10.2 us
    pallas_call x1, Pallas kernels, local(): pl.pallas_call(functools.partial(first_kernel, first_of, spoke_blocks, co...  7.11 us
    ppermute x4, waiting for transfers between devices, parts_of(): return [part, lax.ppermute(part, 'spk', swap)]  4.94 us
    unnamed x12, local copies, waits for them, and re-layouts  3.85 us
    ppermute x6, waiting for transfers between devices, spread(): lax.ppermute(value, 'tile', [(i, i ^ shift) for i in range(n_tile)])  3.59 us
    ppermute x4, starting transfers between devices, parts_of(): return [part, lax.ppermute(part, 'spk', swap)]  3.13 us
    ppermute x2, waiting for transfers between devices, to_coil(): lax.ppermute(value, ('coil', 'spk'), onto)  2.76 us
  transfers between devices with their start and end apart: 15, of which 7 were waited for; matrix products, arithmetic and copies ran while one was open for 0% of the time, Pallas kernels for 12%

profile of v7, /device:TPU:0, one launch (start us, length us, event | category | flops | bytes accessed | tf_op | source)
XLA Modules:
  0.0 69.1 jit_solution(1499258157640414041)
XLA Ops:
  0.0 0.0 copy-start.5
  0.7 0.0 copy-start.2
  0.7 0.7 %copy-done.2 = bf16[8,6,256]{2,0,1:T(8,128)(2,1)S(1)} copy-done((bf16[8,6,256]{2,0,1:T(8,128)(2,1)S(1)}, bf16[8,6,256]{2,0,1:T(8,128)(2,1)}, u32[]{:S(2)}) %copy-start.2) | copy-done | bytes 24600
  1.4 0.0 copy-start.3
  1.4 0.7 %copy-done.3 = bf16[1,8,2,256]{3,2,1,0:T(2,128)(2,1)S(1)} copy-done((bf16[1,8,2,256]{3,2,1,0:T(2,128)(2,1)S(1)}, bf16[1,8,2,256]{3,2,1,0:T(2,128)(2,1)}, u32[]{:S(2)}) %copy-start.3) | copy-done | bytes 8216
  2.1 0.7 %copy-done.4 = s32[8,256]{1,0:T(8,128)S(1)} copy-done((s32[8,256]{1,0:T(8,128)S(1)}, s32[8,256]{1,0:T(8,128)}, u32[]{:S(2)}) %copy-start.4) | copy-done | bytes 8216
  2.8 5.1 %collective-permute-start.5 = (bf16[88,256]{1,0:T(8,128)(2,1)S(1)}, bf16[88,256]{1,0:T(8,128)(2,1)S(1)}, u32[]{:S(2)}, u32[]{:S(2)}) collective-permute-start(bf16[88,256]{1,0:T(8,128)(2,1)S(1)} %shard_map.73.refs_0_), channel_id=1, source_target_pairs={{0,12},{4,8},{8,4},{12,0},{1,13},{5,9},{9,5},{13,1},{2,14},{6,10},... | collective-permute-start | bytes 135176 | tf_op jit(solution)/shard_map/ppermute | solution.py:443
  8.0 0.1 collective-permute-start.2
  8.0 0.9 %collective-permute-start.1 = (f32[32,2,256]{2,1,0:T(2,128)}, f32[32,2,256]{2,1,0:T(2,128)S(1)}, u32[]{:S(2)}, u32[]{:S(2)}) collective-permute-start(f32[32,2,256]{2,1,0:T(2,128)} %bitcast.4), channel_id=1, source_target_pairs={{0,8},{4,12},{8,0},{12,4},{1,9},{5,13},{9,1},{13,5},{2,10},{6,14},... | collective-permute-start | bytes 196616 | tf_op jit(solution)/shard_map/ppermute | solution.py:443
  9.0 3.4 %collective-permute-start = (f32[32,2,256]{2,1,0:T(2,128)}, f32[32,2,256]{2,1,0:T(2,128)S(1)}, u32[]{:S(2)}, u32[]{:S(2)}) collective-permute-start(f32[32,2,256]{2,1,0:T(2,128)} %bitcast.5), channel_id=1, source_target_pairs={{0,4},{4,0},{8,12},{12,8},{1,5},{5,1},{9,13},{13,9},{2,6},{6,2},{1... | collective-permute-start | bytes 196616 | tf_op jit(solution)/shard_map/ppermute | solution.py:443
  12.4 0.0 collective-permute-start.4
  12.4 0.0 collective-permute-done.5.refs_3_
  12.4 0.6 collective-permute-start.3
  13.0 0.9 %copy-done = f32[96,256]{1,0:T(8,128)S(1)} copy-done((f32[96,256]{1,0:T(8,128)S(1)}, f32[96,256]{1,0:T(8,128)}, u32[]{:S(2)}) %copy-start) | copy-done | bytes 98328
  13.9 0.2 shard_map.74.refs_5_.refs_6_
  14.1 3.2 %collective-permute-done.4.refs_2_ = bf16[88,256]{1,0:T(8,128)(2,1)S(1)} collective-permute-done((bf16[88,256]{1,0:T(8,128)(2,1)S(1)}, bf16[88,256]{1,0:T(8,128)(2,1)S(1)}, u32[]{:S(2)}, u32[]{:S(2)}) %collective-permute-start.4) | collective-permute-done | bytes 45088 | tf_op jit(solution)/shard_map/ppermute | solution.py:443
  17.3 0.3 collective-permute-done.3.refs_1_
  17.7 0.0 collective-permute-done.2.refs_3_
  17.7 0.0 collective-permute-done.1.refs_2_
  17.7 0.0 collective-permute-done.refs_1_
  17.7 0.0 copy-start.1
  17.7 0.8 %copy-done.1 = f32[1,32,2,256]{3,2,1,0:T(2,128)S(1)} copy-done((f32[1,32,2,256]{3,2,1,0:T(2,128)S(1)}, f32[1,32,2,256]{3,2,1,0:T(2,128)}, u32[]{:S(2)}) %copy-start.1) | copy-done | bytes 65560
  18.6 1.5 %collective-permute-start.7 = (f32[4,32,2,256]{3,2,1,0:T(2,128)S(1)}, f32[4,32,2,256]{3,2,1,0:T(2,128)S(1)}, u32[]{:S(2)}, u32[]{:S(2)}) collective-permute-start(f32[4,32,2,256]{3,2,1,0:T(2,128)S(1)} %shard_map.76.refs_0_), channel_id=1, source_target_pairs={{0,2},{3,1},{1,0},{2,3},{4,6},{7,5},{5,4},{6,7},{8,10},{11,9},{9,8... | collective-permute-start | bytes 786440 | tf_op jit(solution)/shard_map/ppermute | solution.py:447
  20.1 0.7 collective-permute-start.6
  20.7 1.4 %collective-permute-start.8 = (bf16[4,72,256]{2,1,0:T(8,128)(2,1)S(1)}, bf16[4,72,256]{2,1,0:T(8,128)(2,1)S(1)}, u32[]{:S(2)}, u32[]{:S(2)}) collective-permute-start(bf16[4,72,256]{2,1,0:T(8,128)(2,1)S(1)} %get-tuple-element.45.refs_0_), channel_id=1, source_target_pairs={{0,1},{1,0},{2,3},{3,2},{4,5},{5,4},{6,7},{7,6},{8,9},{9,8},{10,11... | collective-permute-start | bytes 442376 | tf_op jit(solution)/shard_map/ppermute | solution.py:483
  22.2 0.5 collective-permute-start.10
  22.7 0.7 collective-permute-start.9
  23.4 2.8 %collective-permute-done.10.refs_4_ = bf16[4,16,256]{2,1,0:T(8,128)(2,1)S(1)} collective-permute-done((bf16[4,16,256]{2,1,0:T(8,128)(2,1)S(1)}, bf16[4,16,256]{2,1,0:T(8,128)(2,1)S(1)}, u32[]{:S(2)}, u32[]{:S(2)}) %collective-permute-start.10) | collective-permute-done | bytes 32800 | tf_op jit(solution)/shard_map/ppermute | solution.py:447
  26.1 0.0 collective-permute-done.9.refs_3_
  26.1 0.0 collective-permute-done.8.refs_1_
  26.1 7.1 %shard_map.77 = (bf16[4,256,2048]{2,1,0:T(8,128)(2,1)S(1)}, bf16[4,2,144,1024]{3,2,1,0:T(8,128)(2,1)S(1)}, f32[4,2,3,1024]{3,2,1,0:T(4,128)S(1)}, f32[512,256]{1,0:T(8,128)S(1)}) custom-call(bf16[4,72,256]{2,1,0:T(8,128)(2,1)S(1)} %get-tuple-element.45.refs_0_, bf16[4,72,256]{2,1,0:T(8,128)(2,1)S(1)} %collective-permute-done.8.refs_1_, ...), custom_call_target="tpu_custom_call" | custom-call | tf_op jit(solution)/shard_map/pallas_call | solution.py:520
  33.3 0.0 collective-permute-done.7.refs_2_
  33.3 0.0 collective-permute-done.6.refs_1_
  33.3 0.5 shard_map.78
  33.8 1.8 %collective-permute-start.11 = (f32[2,256,256]{2,1,0:T(8,128)S(1)}, f32[2,256,256]{2,1,0:T(8,128)S(1)}, u32[]{:S(2)}, u32[]{:S(2)}) collective-permute-start(f32[2,256,256]{2,1,0:T(8,128)S(1)} %get-tuple-element.51.refs_1_), channel_id=1, source_target_pairs={{0,1},{1,0},{2,3},{3,2},{4,5},{5,4},{6,7},{7,6},{8,9},{9,8},{10,11... | collective-permute-start | bytes 1572872 | tf_op jit(solution)/shard_map/ppermute | solution.py:498
  35.6 0.0 copy-done.5
  35.6 1.2 %shard_map.79 = (f32[3,256]{1,0:T(4,128)S(1)}, bf16[4,256,256]{2,1,0:T(8,128)(2,1)S(1)}) custom-call(f32[3]{0:T(128)S(1)} %copy-done.5), custom_call_target="tpu_custom_call" | custom-call | tf_op jit(solution)/shard_map/pallas_call | solution.py:548
  36.8 0.3 collective-permute-done.11.refs_2_
  37.1 7.9 %shard_map.80 = (f32[2,256,256]{2,1,0:T(8,128)S(1)}, f32[2,256,256]{2,1,0:T(8,128)S(1)}) custom-call(f32[3,256]{1,0:T(4,128)S(1)} %get-tuple-element.50.refs_0_.thr_ref, f32[2,256,256]{2,1,0:T(8,128)S(1)} %get-tuple-element.51.refs_1_, f32[2,256,256]{2,1,0:T(8,128)S(1)} %collective-permute-done.11.refs_2_, ...), custom_call_target="tpu_custom_call" | custom-call | tf_op jit(solution)/shard_map/pallas_call | solution.py:558
  45.1 0.4 collective-permute-start.12
  45.5 1.5 %collective-permute-done.12.refs_3_ = f32[2,256,256]{2,1,0:T(8,128)S(1)} collective-permute-done((f32[2,256,256]{2,1,0:T(8,128)S(1)}, f32[2,256,256]{2,1,0:T(8,128)S(1)}, u32[]{:S(2)}, u32[]{:S(2)}) %collective-permute-start.12) | collective-permute-done | bytes 524320 | tf_op jit(solution)/shard_map/ppermute | solution.py:498
  47.0 8.2 %shard_map.81 = (f32[2,256,256]{2,1,0:T(8,128)S(1)}, f32[2,256,256]{2,1,0:T(8,128)S(1)}) custom-call(f32[3,256]{1,0:T(4,128)S(1)} %get-tuple-element.50.refs_0_.thr_ref, f32[2,256,256]{2,1,0:T(8,128)S(1)} %get-tuple-element.57.refs_1_, f32[2,256,256]{2,1,0:T(8,128)S(1)} %get-tuple-element.58.refs_2_, f32[2,256,256]{2,1,0:T(8,128)S(1)} %collective-permute-done.12.refs_3_, ...), custom_call_target="tpu_custom_call" | custom-call | tf_op jit(solution)/shard_map/pallas_call | solution.py:558
  55.2 0.4 collective-permute-start.13
  55.6 1.5 %collective-permute-done.13.refs_3_ = f32[2,256,256]{2,1,0:T(8,128)S(1)} collective-permute-done((f32[2,256,256]{2,1,0:T(8,128)S(1)}, f32[2,256,256]{2,1,0:T(8,128)S(1)}, u32[]{:S(2)}, u32[]{:S(2)}) %collective-permute-start.13) | collective-permute-done | bytes 524320 | tf_op jit(solution)/shard_map/ppermute | solution.py:498
  57.2 7.9 %shard_map.82 = (f32[2,256,256]{2,1,0:T(8,128)S(1)}, f32[2,256,256]{2,1,0:T(8,128)S(1)}) custom-call(f32[3,256]{1,0:T(4,128)S(1)} %get-tuple-element.50.refs_0_.thr_ref, f32[2,256,256]{2,1,0:T(8,128)S(1)} %get-tuple-element.59.refs_1_, f32[2,256,256]{2,1,0:T(8,128)S(1)} %get-tuple-element.60.refs_2_, f32[2,256,256]{2,1,0:T(8,128)S(1)} %collective-permute-done.13.refs_3_, ...), custom_call_target="tpu_custom_call" | custom-call | tf_op jit(solution)/shard_map/pallas_call | solution.py:558
  65.1 0.4 collective-permute-start.14
  65.6 1.5 %collective-permute-done.14.refs_1_ = f32[2,256,256]{2,1,0:T(8,128)S(1)} collective-permute-done((f32[2,256,256]{2,1,0:T(8,128)S(1)}, f32[2,256,256]{2,1,0:T(8,128)S(1)}, u32[]{:S(2)}, u32[]{:S(2)}) %collective-permute-start.14) | collective-permute-done | bytes 524320 | tf_op jit(solution)/shard_map/ppermute | solution.py:498
  67.1 2.0 %shard_map.83 = f32[32,2,256]{2,1,0:T(2,128)} custom-call(f32[3,256]{1,0:T(4,128)S(1)} %get-tuple-element.50.refs_0_.thr_ref, f32[2,256,256]{2,1,0:T(8,128)S(1)} %get-tuple-element.61.est_ref, f32[2,256,256]{2,1,0:T(8,128)S(1)} %get-tuple-element.62.refs_0_, f32[2,256,256]{2,1,0:T(8,128)S(1)} %collective-permute-done.14.refs_1_, ...), custom_call_target="tpu_custom_call" | custom-call | tf_op jit(solution)/shard_map/pallas_call | solution.py:568
  (5 shorter events, 0.1 us)
Async XLA Ops:
  0.0 35.6 %copy-start.5 = (f32[3]{0:T(128)S(1)}, f32[3]{0:T(128)}, u32[]{:S(2)}) copy-start(f32[3]{0:T(128)} %thr_ref) | copy-start | bytes 40
  0.7 0.7 %copy-start.2 = (bf16[8,6,256]{2,0,1:T(8,128)(2,1)S(1)}, bf16[8,6,256]{2,0,1:T(8,128)(2,1)}, u32[]{:S(2)}) copy-start(bf16[8,6,256]{2,0,1:T(8,128)(2,1)} %param.9) | copy-start | bytes 73732
  1.4 0.7 %copy-start.3 = (bf16[1,8,2,256]{3,2,1,0:T(2,128)(2,1)S(1)}, bf16[1,8,2,256]{3,2,1,0:T(2,128)(2,1)}, u32[]{:S(2)}) copy-start(bf16[1,8,2,256]{3,2,1,0:T(2,128)(2,1)} %param.8) | copy-start | bytes 24580
  2.1 0.7 %copy-start.4 = (s32[8,256]{1,0:T(8,128)S(1)}, s32[8,256]{1,0:T(8,128)}, u32[]{:S(2)}) copy-start(s32[8,256]{1,0:T(8,128)} %bins_ref.1) | copy-start | bytes 24580
  2.8 9.5 %collective-permute-start.5 = (bf16[88,256]{1,0:T(8,128)(2,1)S(1)}, bf16[88,256]{1,0:T(8,128)(2,1)S(1)}, u32[]{:S(2)}, u32[]{:S(2)}) collective-permute-start(bf16[88,256]{1,0:T(8,128)(2,1)S(1)} %shard_map.73.refs_0_), channel_id=1, source_target_pairs={{0,12},{4,8},{8,4},{12,0},{1,13},{5,9},{9,5},{13,1},{2,14},{6,10},... | collective-permute-start | bytes 135176 | tf_op jit(solution)/shard_map/ppermute | solution.py:443
  8.0 9.7 %collective-permute-start.2 = (f32[32,2,256]{2,1,0:T(2,128)}, f32[32,2,256]{2,1,0:T(2,128)S(1)}, u32[]{:S(2)}, u32[]{:S(2)}) collective-permute-start(f32[32,2,256]{2,1,0:T(2,128)} %bitcast.3), channel_id=1, source_target_pairs={{0,12},{4,8},{8,4},{12,0},{1,13},{5,9},{9,5},{13,1},{2,14},{6,10},... | collective-permute-start | bytes 196616 | tf_op jit(solution)/shard_map/ppermute | solution.py:443
  8.0 9.6 %collective-permute-start.1 = (f32[32,2,256]{2,1,0:T(2,128)}, f32[32,2,256]{2,1,0:T(2,128)S(1)}, u32[]{:S(2)}, u32[]{:S(2)}) collective-permute-start(f32[32,2,256]{2,1,0:T(2,128)} %bitcast.4), channel_id=1, source_target_pairs={{0,8},{4,12},{8,0},{12,4},{1,9},{5,13},{9,1},{13,5},{2,10},{6,14},... | collective-permute-start | bytes 196616 | tf_op jit(solution)/shard_map/ppermute | solution.py:443
  9.0 8.7 %collective-permute-start = (f32[32,2,256]{2,1,0:T(2,128)}, f32[32,2,256]{2,1,0:T(2,128)S(1)}, u32[]{:S(2)}, u32[]{:S(2)}) collective-permute-start(f32[32,2,256]{2,1,0:T(2,128)} %bitcast.5), channel_id=1, source_target_pairs={{0,4},{4,0},{8,12},{12,8},{1,5},{5,1},{9,13},{13,9},{2,6},{6,2},{1... | collective-permute-start | bytes 196616 | tf_op jit(solution)/shard_map/ppermute | solution.py:443
  12.4 5.0 %collective-permute-start.4 = (bf16[88,256]{1,0:T(8,128)(2,1)S(1)}, bf16[88,256]{1,0:T(8,128)(2,1)S(1)}, u32[]{:S(2)}, u32[]{:S(2)}) collective-permute-start(bf16[88,256]{1,0:T(8,128)(2,1)S(1)} %shard_map.73.refs_0_), channel_id=1, source_target_pairs={{0,8},{4,12},{8,0},{12,4},{1,9},{5,13},{9,1},{13,5},{2,10},{6,14},... | collective-permute-start | bytes 135176 | tf_op jit(solution)/shard_map/ppermute | solution.py:443
  12.4 5.3 %collective-permute-start.3 = (bf16[88,256]{1,0:T(8,128)(2,1)S(1)}, bf16[88,256]{1,0:T(8,128)(2,1)S(1)}, u32[]{:S(2)}, u32[]{:S(2)}) collective-permute-start(bf16[88,256]{1,0:T(8,128)(2,1)S(1)} %shard_map.73.refs_0_), channel_id=1, source_target_pairs={{0,4},{4,0},{8,12},{12,8},{1,5},{5,1},{9,13},{13,9},{2,6},{6,2},{1... | collective-permute-start | bytes 135176 | tf_op jit(solution)/shard_map/ppermute | solution.py:443
  13.0 0.9 %copy-start = (f32[96,256]{1,0:T(8,128)S(1)}, f32[96,256]{1,0:T(8,128)}, u32[]{:S(2)}) copy-start(f32[96,256]{1,0:T(8,128)} %constant.2.clone.seed_ref) | copy-start | bytes 294916
  17.7 0.8 %copy-start.1 = (f32[1,32,2,256]{3,2,1,0:T(2,128)S(1)}, f32[1,32,2,256]{3,2,1,0:T(2,128)}, u32[]{:S(2)}) copy-start(f32[1,32,2,256]{3,2,1,0:T(2,128)} %param.7) | copy-start | bytes 196612
  18.6 14.7 %collective-permute-start.7 = (f32[4,32,2,256]{3,2,1,0:T(2,128)S(1)}, f32[4,32,2,256]{3,2,1,0:T(2,128)S(1)}, u32[]{:S(2)}, u32[]{:S(2)}) collective-permute-start(f32[4,32,2,256]{3,2,1,0:T(2,128)S(1)} %shard_map.76.refs_0_), channel_id=1, source_target_pairs={{0,2},{3,1},{1,0},{2,3},{4,6},{7,5},{5,4},{6,7},{8,10},{11,9},{9,8... | collective-permute-start | bytes 786440 | tf_op jit(solution)/shard_map/ppermute | solution.py:447
  20.1 13.2 %collective-permute-start.6 = (f32[4,32,2,256]{3,2,1,0:T(2,128)S(1)}, f32[4,32,2,256]{3,2,1,0:T(2,128)S(1)}, u32[]{:S(2)}, u32[]{:S(2)}) collective-permute-start(f32[4,32,2,256]{3,2,1,0:T(2,128)S(1)} %shard_map.76.refs_0_), channel_id=1, source_target_pairs={{1,2},{2,1},{5,6},{6,5},{9,10},{10,9},{13,14},{14,13},{17,18},{18,... | collective-permute-start | bytes 786440 | tf_op jit(solution)/shard_map/ppermute | solution.py:447
  20.7 5.4 %collective-permute-start.8 = (bf16[4,72,256]{2,1,0:T(8,128)(2,1)S(1)}, bf16[4,72,256]{2,1,0:T(8,128)(2,1)S(1)}, u32[]{:S(2)}, u32[]{:S(2)}) collective-permute-start(bf16[4,72,256]{2,1,0:T(8,128)(2,1)S(1)} %get-tuple-element.45.refs_0_), channel_id=1, source_target_pairs={{0,1},{1,0},{2,3},{3,2},{4,5},{5,4},{6,7},{7,6},{8,9},{9,8},{10,11... | collective-permute-start | bytes 442376 | tf_op jit(solution)/shard_map/ppermute | solution.py:483
  22.2 4.0 %collective-permute-start.10 = (bf16[4,16,256]{2,1,0:T(8,128)(2,1)S(1)}, bf16[4,16,256]{2,1,0:T(8,128)(2,1)S(1)}, u32[]{:S(2)}, u32[]{:S(2)}) collective-permute-start(bf16[4,16,256]{2,1,0:T(8,128)(2,1)S(1)} %get-tuple-element.40.refs_2_), channel_id=1, source_target_pairs={{0,2},{3,1},{1,0},{2,3},{4,6},{7,5},{5,4},{6,7},{8,10},{11,9},{9,8... | collective-permute-start | bytes 98312 | tf_op jit(solution)/shard_map/ppermute | solution.py:447
  22.7 3.4 %collective-permute-start.9 = (bf16[4,16,256]{2,1,0:T(8,128)(2,1)S(1)}, bf16[4,16,256]{2,1,0:T(8,128)(2,1)S(1)}, u32[]{:S(2)}, u32[]{:S(2)}) collective-permute-start(bf16[4,16,256]{2,1,0:T(8,128)(2,1)S(1)} %get-tuple-element.40.refs_2_), channel_id=1, source_target_pairs={{1,2},{2,1},{5,6},{6,5},{9,10},{10,9},{13,14},{14,13},{17,18},{18,... | collective-permute-start | bytes 98312 | tf_op jit(solution)/shard_map/ppermute | solution.py:447
  33.8 3.4 %collective-permute-start.11 = (f32[2,256,256]{2,1,0:T(8,128)S(1)}, f32[2,256,256]{2,1,0:T(8,128)S(1)}, u32[]{:S(2)}, u32[]{:S(2)}) collective-permute-start(f32[2,256,256]{2,1,0:T(8,128)S(1)} %get-tuple-element.51.refs_1_), channel_id=1, source_target_pairs={{0,1},{1,0},{2,3},{3,2},{4,5},{5,4},{6,7},{7,6},{8,9},{9,8},{10,11... | collective-permute-start | bytes 1572872 | tf_op jit(solution)/shard_map/ppermute | solution.py:498
  45.1 2.0 %collective-permute-start.12 = (f32[2,256,256]{2,1,0:T(8,128)S(1)}, f32[2,256,256]{2,1,0:T(8,128)S(1)}, u32[]{:S(2)}, u32[]{:S(2)}) collective-permute-start(f32[2,256,256]{2,1,0:T(8,128)S(1)} %get-tuple-element.58.refs_2_), channel_id=1, source_target_pairs={{0,1},{1,0},{2,3},{3,2},{4,5},{5,4},{6,7},{7,6},{8,9},{9,8},{10,11... | collective-permute-start | bytes 1572872 | tf_op jit(solution)/shard_map/ppermute | solution.py:498
  55.2 2.0 %collective-permute-start.13 = (f32[2,256,256]{2,1,0:T(8,128)S(1)}, f32[2,256,256]{2,1,0:T(8,128)S(1)}, u32[]{:S(2)}, u32[]{:S(2)}) collective-permute-start(f32[2,256,256]{2,1,0:T(8,128)S(1)} %get-tuple-element.60.refs_2_), channel_id=1, source_target_pairs={{0,1},{1,0},{2,3},{3,2},{4,5},{5,4},{6,7},{7,6},{8,9},{9,8},{10,11... | collective-permute-start | bytes 1572872 | tf_op jit(solution)/shard_map/ppermute | solution.py:498
  65.1 2.0 %collective-permute-start.14 = (f32[2,256,256]{2,1,0:T(8,128)S(1)}, f32[2,256,256]{2,1,0:T(8,128)S(1)}, u32[]{:S(2)}, u32[]{:S(2)}) collective-permute-start(f32[2,256,256]{2,1,0:T(8,128)S(1)} %get-tuple-element.62.refs_0_), channel_id=1, source_target_pairs={{0,1},{1,0},{2,3},{3,2},{4,5},{5,4},{6,7},{7,6},{8,9},{9,8},{10,11... | collective-permute-start | bytes 1572872 | tf_op jit(solution)/shard_map/ppermute | solution.py:498

commit v8 on v7

--- a/solution.py
+++ b/solution.py
@@ -146,34 +146,37 @@
     return out
 
 
-def shrink(re, im, thr_ref, haar, last_rows=None):
+def band_tables(col_pos, row_pos, n, thr_ref, thr_lanes):
+    col_label, row_label = labels(col_pos, n), labels(row_pos % 2**LEVELS, 2**LEVELS)
+    scale = jnp.exp2(-0.5 * jnp.minimum(col_label, LEVELS)) * jnp.exp2(-0.5 * jnp.minimum(row_label, LEVELS))
+    band = jnp.minimum(col_label, row_label)
+    limits = jnp.full(band.shape, 1.0, F32)
+    for level in range(LEVELS):
+        limits = jnp.where(band == level + 1, thr_ref[level : level + 1, :thr_lanes], limits)
+    return limits, scale, band
+
+
+def shrunk(re, im, limits, scale, band):
+    re, im = re * scale, im * scale
+    magnitude = jnp.sqrt(re * re + im * im)
+    factor = jnp.maximum(magnitude - limits, 0.0) / jnp.maximum(magnitude, limits)
+    factor = jnp.where(band <= LEVELS, factor, 1.0) * scale
+    return re * factor, im * factor
+
+
+def shrink(re, im, thr_ref, haar):
     n = re.shape[0]
-    block = 2**LEVELS
     col_pos = lax.broadcasted_iota(jnp.int32, (n, 1), 0)
-    row_pos = lax.broadcasted_iota(jnp.int32, (1, n), 1) % block
-    col_label, row_label = labels(col_pos, n), labels(row_pos, block)
-    col_scale = jnp.exp2(-0.5 * jnp.minimum(col_label, LEVELS))
-    row_scale = jnp.exp2(-0.5 * jnp.minimum(row_label, LEVELS))
-    band = jnp.minimum(col_label, row_label)
-    limits = jnp.full((n, n), 1.0, F32)
-    for level in range(LEVELS):
-        limits = jnp.where(band == level + 1, thr_ref[level : level + 1, :], limits)
-    scale = col_scale * row_scale
+    row_pos = lax.broadcasted_iota(jnp.int32, (1, n), 1)
+    tables = band_tables(col_pos, row_pos, n, thr_ref, n)
     half = mm(joined([haar[0]] * 2, 1), joined(split2(joined([re, im], 1)), 0))
     half = joined([half[:, :n], half[:, n:]], 0)
     full = mm(joined(split2(half), 1), joined([haar[2]] * 2, 0))
-    coeffs = [full[:n] * scale, full[n:] * scale]
-    magnitude = jnp.sqrt(coeffs[0] * coeffs[0] + coeffs[1] * coeffs[1])
-    factor = jnp.maximum(magnitude - limits, 0.0) / jnp.maximum(magnitude, limits)
-    factor = jnp.where(band <= LEVELS, factor, 1.0) * scale
-    kept = joined([coeffs[0] * factor, coeffs[1] * factor], 1)
+    kept = joined(shrunk(full[:n], full[n:], *tables), 1)
     half = mm(joined([haar[1]] * 2, 1), joined(split2(kept), 0))
     half = joined([half[:, :n], half[:, n:]], 0)
-    if last_rows is None:
-        full = mm(joined(split2(half), 1), joined([haar[3]] * 2, 0))
-        return full[:n], full[n:]
-    full = mm_t(joined([last_rows] * 2, 1), joined(split2(half), 1))
-    return full[:, :n], full[:, n:]
+    full = mm(joined(split2(half), 1), joined([haar[3]] * 2, 0))
+    return full[:n], full[n:]
 
 
 def density_of(ro, n, live_total):
@@ -319,7 +322,7 @@
         build(group)
         return carry
 
-    lax.fori_loop(1, groups, group_step, 0)
+    lax.fori_loop(1, groups, group_step, 0, unroll=True)
     grid_group(groups - 1, rows_s, cols_s, weighted_s, grid_s)
     back_out[...] = adjoint(from_sides(grid_s), const_ref)
 
@@ -395,14 +398,27 @@
     part_refs, (haar_ref, out_ref) = refs[:n_parts], refs[n_parts:]
     n = est_ref.shape[1]
     target = target_of(est_ref, part_refs)
-    mine = mine_of()
     pick = lax.broadcasted_iota(jnp.int32, (rows, n), 1) == (
-        lax.broadcasted_iota(jnp.int32, (rows, n), 0) + mine * rows
+        lax.broadcasted_iota(jnp.int32, (rows, n), 0) + mine_of() * rows
     )
-    own = mm(jnp.where(pick, 1.0, 0.0).astype(BF16), haar_ref[2]).astype(BF16)
-    re, im = shrink(target[0], target[1], thr_ref, haar_ref, own)
-    out_ref[:, 0, :] = re
-    out_ref[:, 1, :] = im
+    pick = jnp.where(pick, 1.0, 0.0).astype(BF16)
+    own = mm_t(joined([pick] * 3, 1), joined(split3(joined(target, 0)), 1))
+    row_pos = lax.broadcasted_iota(jnp.int32, (rows, 1), 0)
+    col_pos = lax.broadcasted_iota(jnp.int32, (1, n), 1)
+    tables = band_tables(col_pos, row_pos, n, thr_ref, n)
+    row_haar, row_back = haar_ref[3][:rows, :rows], haar_ref[2][:rows, :rows]
+
+    def by_rows(signs, wide):
+        return mm(signs, split2(wide)[0]) + mm(signs, split2(wide)[1])
+
+    half = by_rows(row_haar, own)
+    half = joined([half[:, :n], half[:, n:]], 0)
+    full = mm(joined(split2(half), 1), joined([haar_ref[1]] * 2, 0))
+    kept = joined(shrunk(full[:rows], full[rows:], *tables), 0)
+    half = mm(joined(split2(kept), 1), joined([haar_ref[0]] * 2, 0))
+    full = by_rows(row_back, joined([half[:rows], half[rows:]], 1))
+    out_ref[:, 0, :] = full[:, :n]
+    out_ref[:, 1, :] = full[:, n:]
 
 
 def local(coil_maps, kspace_data, interp_weights, sample_bins, spoke_count, thresholds):

time: 69.5 us -> 68.5 us (0.986)
  Pallas kernels: 35.1 us -> 34.1 us
where the time goes in v8:
time: 68.5 us; the launch traced here: 68.1 us
  Pallas kernels  34.1 us (50%)
  starting transfers between devices  18.1 us (26%)
  waiting for transfers between devices  11.3 us (16%)
  local copies, waits for them, and re-layouts  3.85 us (6%)
  between operations  0.81 us (1%)
    pallas_call x3, Pallas kernels, local(): pl.pallas_call(functools.partial(step_kernel, len(estimate), len(parts)),...  24 us
    ppermute x6, starting transfers between devices, spread(): lax.ppermute(value, 'tile', [(i, i ^ shift) for i in range(n_tile)])  10.2 us
    pallas_call x1, Pallas kernels, local(): pl.pallas_call(functools.partial(first_kernel, first_of, spoke_blocks, co...  6.54 us
    ppermute x4, waiting for transfers between devices, parts_of(): return [part, lax.ppermute(part, 'spk', swap)]  4.93 us
    unnamed x12, local copies, waits for them, and re-layouts  3.85 us
    ppermute x6, waiting for transfers between devices, spread(): lax.ppermute(value, 'tile', [(i, i ^ shift) for i in range(n_tile)])  3.59 us
    ppermute x4, starting transfers between devices, parts_of(): return [part, lax.ppermute(part, 'spk', swap)]  3.15 us
    ppermute x2, waiting for transfers between devices, to_coil(): lax.ppermute(value, ('coil', 'spk'), onto)  2.76 us
  transfers between devices with their start and end apart: 15, of which 7 were waited for; matrix products, arithmetic and copies ran while one was open for 0% of the time, Pallas kernels for 12%

profile of v8, /device:TPU:0, one launch (start us, length us, event | category | flops | bytes accessed | tf_op | source)
XLA Modules:
  0.0 68.1 jit_solution(4917454589442627873)
XLA Ops:
  0.0 0.0 copy-start.5
  0.7 0.0 copy-start.2
  0.7 0.7 %copy-done.2 = bf16[8,6,256]{2,0,1:T(8,128)(2,1)S(1)} copy-done((bf16[8,6,256]{2,0,1:T(8,128)(2,1)S(1)}, bf16[8,6,256]{2,0,1:T(8,128)(2,1)}, u32[]{:S(2)}) %copy-start.2) | copy-done | bytes 24600
  1.4 0.0 copy-start.3
  1.4 0.7 %copy-done.3 = bf16[1,8,2,256]{3,2,1,0:T(2,128)(2,1)S(1)} copy-done((bf16[1,8,2,256]{3,2,1,0:T(2,128)(2,1)S(1)}, bf16[1,8,2,256]{3,2,1,0:T(2,128)(2,1)}, u32[]{:S(2)}) %copy-start.3) | copy-done | bytes 8216
  2.1 0.7 %copy-done.4 = s32[8,256]{1,0:T(8,128)S(1)} copy-done((s32[8,256]{1,0:T(8,128)S(1)}, s32[8,256]{1,0:T(8,128)}, u32[]{:S(2)}) %copy-start.4) | copy-done | bytes 8216
  2.8 5.1 %collective-permute-start.5 = (bf16[88,256]{1,0:T(8,128)(2,1)S(1)}, bf16[88,256]{1,0:T(8,128)(2,1)S(1)}, u32[]{:S(2)}, u32[]{:S(2)}) collective-permute-start(bf16[88,256]{1,0:T(8,128)(2,1)S(1)} %shard_map.73.refs_0_), channel_id=1, source_target_pairs={{0,12},{4,8},{8,4},{12,0},{1,13},{5,9},{9,5},{13,1},{2,14},{6,10},... | collective-permute-start | bytes 135176 | tf_op jit(solution)/shard_map/ppermute | solution.py:459
  8.0 0.1 collective-permute-start.2
  8.0 0.9 %collective-permute-start.1 = (f32[32,2,256]{2,1,0:T(2,128)}, f32[32,2,256]{2,1,0:T(2,128)S(1)}, u32[]{:S(2)}, u32[]{:S(2)}) collective-permute-start(f32[32,2,256]{2,1,0:T(2,128)} %bitcast.4), channel_id=1, source_target_pairs={{0,8},{4,12},{8,0},{12,4},{1,9},{5,13},{9,1},{13,5},{2,10},{6,14},... | collective-permute-start | bytes 196616 | tf_op jit(solution)/shard_map/ppermute | solution.py:459
  9.0 3.4 %collective-permute-start = (f32[32,2,256]{2,1,0:T(2,128)}, f32[32,2,256]{2,1,0:T(2,128)S(1)}, u32[]{:S(2)}, u32[]{:S(2)}) collective-permute-start(f32[32,2,256]{2,1,0:T(2,128)} %bitcast.5), channel_id=1, source_target_pairs={{0,4},{4,0},{8,12},{12,8},{1,5},{5,1},{9,13},{13,9},{2,6},{6,2},{1... | collective-permute-start | bytes 196616 | tf_op jit(solution)/shard_map/ppermute | solution.py:459
  12.4 0.0 collective-permute-start.4
  12.4 0.0 collective-permute-done.5.refs_3_
  12.4 0.6 collective-permute-start.3
  13.0 0.9 %copy-done = f32[96,256]{1,0:T(8,128)S(1)} copy-done((f32[96,256]{1,0:T(8,128)S(1)}, f32[96,256]{1,0:T(8,128)}, u32[]{:S(2)}) %copy-start) | copy-done | bytes 98328
  13.9 0.2 shard_map.74.refs_5_.refs_6_
  14.1 3.2 %collective-permute-done.4.refs_2_ = bf16[88,256]{1,0:T(8,128)(2,1)S(1)} collective-permute-done((bf16[88,256]{1,0:T(8,128)(2,1)S(1)}, bf16[88,256]{1,0:T(8,128)(2,1)S(1)}, u32[]{:S(2)}, u32[]{:S(2)}) %collective-permute-start.4) | collective-permute-done | bytes 45088 | tf_op jit(solution)/shard_map/ppermute | solution.py:459
  17.3 0.3 collective-permute-done.3.refs_1_
  17.7 0.0 collective-permute-done.2.refs_3_
  17.7 0.0 collective-permute-done.1.refs_2_
  17.7 0.0 collective-permute-done.refs_1_
  17.7 0.0 copy-start.1
  17.7 0.8 %copy-done.1 = f32[1,32,2,256]{3,2,1,0:T(2,128)S(1)} copy-done((f32[1,32,2,256]{3,2,1,0:T(2,128)S(1)}, f32[1,32,2,256]{3,2,1,0:T(2,128)}, u32[]{:S(2)}) %copy-start.1) | copy-done | bytes 65560
  18.6 1.5 %collective-permute-start.7 = (f32[4,32,2,256]{3,2,1,0:T(2,128)S(1)}, f32[4,32,2,256]{3,2,1,0:T(2,128)S(1)}, u32[]{:S(2)}, u32[]{:S(2)}) collective-permute-start(f32[4,32,2,256]{3,2,1,0:T(2,128)S(1)} %shard_map.76.refs_0_), channel_id=1, source_target_pairs={{0,2},{3,1},{1,0},{2,3},{4,6},{7,5},{5,4},{6,7},{8,10},{11,9},{9,8... | collective-permute-start | bytes 786440 | tf_op jit(solution)/shard_map/ppermute | solution.py:463
  20.1 0.7 collective-permute-start.6
  20.7 1.4 %collective-permute-start.8 = (bf16[4,72,256]{2,1,0:T(8,128)(2,1)S(1)}, bf16[4,72,256]{2,1,0:T(8,128)(2,1)S(1)}, u32[]{:S(2)}, u32[]{:S(2)}) collective-permute-start(bf16[4,72,256]{2,1,0:T(8,128)(2,1)S(1)} %get-tuple-element.45.refs_0_), channel_id=1, source_target_pairs={{0,1},{1,0},{2,3},{3,2},{4,5},{5,4},{6,7},{7,6},{8,9},{9,8},{10,11... | collective-permute-start | bytes 442376 | tf_op jit(solution)/shard_map/ppermute | solution.py:499
  22.2 0.5 collective-permute-start.10
  22.7 0.7 collective-permute-start.9
  23.4 2.8 %collective-permute-done.10.refs_4_ = bf16[4,16,256]{2,1,0:T(8,128)(2,1)S(1)} collective-permute-done((bf16[4,16,256]{2,1,0:T(8,128)(2,1)S(1)}, bf16[4,16,256]{2,1,0:T(8,128)(2,1)S(1)}, u32[]{:S(2)}, u32[]{:S(2)}) %collective-permute-start.10) | collective-permute-done | bytes 32800 | tf_op jit(solution)/shard_map/ppermute | solution.py:463
  26.1 0.0 collective-permute-done.9.refs_3_
  26.1 0.0 collective-permute-done.8.refs_1_
  26.1 6.5 %shard_map.77 = (bf16[4,256,2048]{2,1,0:T(8,128)(2,1)S(1)}, bf16[4,2,144,1024]{3,2,1,0:T(8,128)(2,1)S(1)}, f32[4,2,3,1024]{3,2,1,0:T(4,128)S(1)}, f32[512,256]{1,0:T(8,128)S(1)}) custom-call(bf16[4,72,256]{2,1,0:T(8,128)(2,1)S(1)} %get-tuple-element.45.refs_0_, bf16[4,72,256]{2,1,0:T(8,128)(2,1)S(1)} %collective-permute-done.8.refs_1_, ...), custom_call_target="tpu_custom_call" | custom-call | tf_op jit(solution)/shard_map/pallas_call | solution.py:536
  32.7 0.0 collective-permute-done.7.refs_2_
  32.7 0.0 collective-permute-done.6.refs_1_
  32.7 0.5 shard_map.78
  33.2 1.8 %collective-permute-start.11 = (f32[2,256,256]{2,1,0:T(8,128)S(1)}, f32[2,256,256]{2,1,0:T(8,128)S(1)}, u32[]{:S(2)}, u32[]{:S(2)}) collective-permute-start(f32[2,256,256]{2,1,0:T(8,128)S(1)} %get-tuple-element.51.refs_1_), channel_id=1, source_target_pairs={{0,1},{1,0},{2,3},{3,2},{4,5},{5,4},{6,7},{7,6},{8,9},{9,8},{10,11... | collective-permute-start | bytes 1572872 | tf_op jit(solution)/shard_map/ppermute | solution.py:514
  35.0 0.0 copy-done.5
  35.0 1.2 %shard_map.79 = (f32[3,256]{1,0:T(4,128)S(1)}, bf16[4,256,256]{2,1,0:T(8,128)(2,1)S(1)}) custom-call(f32[3]{0:T(128)S(1)} %copy-done.5), custom_call_target="tpu_custom_call" | custom-call | tf_op jit(solution)/shard_map/pallas_call | solution.py:564
  36.3 0.3 collective-permute-done.11.refs_2_
  36.6 8.1 %shard_map.80 = (f32[2,256,256]{2,1,0:T(8,128)S(1)}, f32[2,256,256]{2,1,0:T(8,128)S(1)}) custom-call(f32[3,256]{1,0:T(4,128)S(1)} %get-tuple-element.50.refs_0_.thr_ref, f32[2,256,256]{2,1,0:T(8,128)S(1)} %get-tuple-element.51.refs_1_, f32[2,256,256]{2,1,0:T(8,128)S(1)} %collective-permute-done.11.refs_2_, ...), custom_call_target="tpu_custom_call" | custom-call | tf_op jit(solution)/shard_map/pallas_call | solution.py:574
  44.7 0.4 collective-permute-start.12
  45.1 1.5 %collective-permute-done.12.refs_3_ = f32[2,256,256]{2,1,0:T(8,128)S(1)} collective-permute-done((f32[2,256,256]{2,1,0:T(8,128)S(1)}, f32[2,256,256]{2,1,0:T(8,128)S(1)}, u32[]{:S(2)}, u32[]{:S(2)}) %collective-permute-start.12) | collective-permute-done | bytes 524320 | tf_op jit(solution)/shard_map/ppermute | solution.py:514
  46.7 7.9 %shard_map.81 = (f32[2,256,256]{2,1,0:T(8,128)S(1)}, f32[2,256,256]{2,1,0:T(8,128)S(1)}) custom-call(f32[3,256]{1,0:T(4,128)S(1)} %get-tuple-element.50.refs_0_.thr_ref, f32[2,256,256]{2,1,0:T(8,128)S(1)} %get-tuple-element.57.refs_1_, f32[2,256,256]{2,1,0:T(8,128)S(1)} %get-tuple-element.58.refs_2_, f32[2,256,256]{2,1,0:T(8,128)S(1)} %collective-permute-done.12.refs_3_, ...), custom_call_target="tpu_custom_call" | custom-call | tf_op jit(solution)/shard_map/pallas_call | solution.py:574
  54.6 0.4 collective-permute-start.13
  55.0 1.5 %collective-permute-done.13.refs_3_ = f32[2,256,256]{2,1,0:T(8,128)S(1)} collective-permute-done((f32[2,256,256]{2,1,0:T(8,128)S(1)}, f32[2,256,256]{2,1,0:T(8,128)S(1)}, u32[]{:S(2)}, u32[]{:S(2)}) %collective-permute-start.13) | collective-permute-done | bytes 524320 | tf_op jit(solution)/shard_map/ppermute | solution.py:514
  56.6 8.0 %shard_map.82 = (f32[2,256,256]{2,1,0:T(8,128)S(1)}, f32[2,256,256]{2,1,0:T(8,128)S(1)}) custom-call(f32[3,256]{1,0:T(4,128)S(1)} %get-tuple-element.50.refs_0_.thr_ref, f32[2,256,256]{2,1,0:T(8,128)S(1)} %get-tuple-element.59.refs_1_, f32[2,256,256]{2,1,0:T(8,128)S(1)} %get-tuple-element.60.refs_2_, f32[2,256,256]{2,1,0:T(8,128)S(1)} %collective-permute-done.13.refs_3_, ...), custom_call_target="tpu_custom_call" | custom-call | tf_op jit(solution)/shard_map/pallas_call | solution.py:574
  64.5 0.4 collective-permute-start.14
  65.0 1.5 %collective-permute-done.14.refs_1_ = f32[2,256,256]{2,1,0:T(8,128)S(1)} collective-permute-done((f32[2,256,256]{2,1,0:T(8,128)S(1)}, f32[2,256,256]{2,1,0:T(8,128)S(1)}, u32[]{:S(2)}, u32[]{:S(2)}) %collective-permute-start.14) | collective-permute-done | bytes 524320 | tf_op jit(solution)/shard_map/ppermute | solution.py:514
  66.5 1.6 %shard_map.83 = f32[32,2,256]{2,1,0:T(2,128)} custom-call(f32[3,256]{1,0:T(4,128)S(1)} %get-tuple-element.50.refs_0_.thr_ref, f32[2,256,256]{2,1,0:T(8,128)S(1)} %get-tuple-element.61.est_ref, f32[2,256,256]{2,1,0:T(8,128)S(1)} %get-tuple-element.62.refs_0_, f32[2,256,256]{2,1,0:T(8,128)S(1)} %collective-permute-done.14.refs_1_, ...), custom_call_target="tpu_custom_call" | custom-call | tf_op jit(solution)/shard_map/pallas_call | solution.py:584
  (5 shorter events, 0.1 us)
Async XLA Ops:
  0.0 35.0 %copy-start.5 = (f32[3]{0:T(128)S(1)}, f32[3]{0:T(128)}, u32[]{:S(2)}) copy-start(f32[3]{0:T(128)} %thr_ref) | copy-start | bytes 40
  0.7 0.7 %copy-start.2 = (bf16[8,6,256]{2,0,1:T(8,128)(2,1)S(1)}, bf16[8,6,256]{2,0,1:T(8,128)(2,1)}, u32[]{:S(2)}) copy-start(bf16[8,6,256]{2,0,1:T(8,128)(2,1)} %param.9) | copy-start | bytes 73732
  1.4 0.7 %copy-start.3 = (bf16[1,8,2,256]{3,2,1,0:T(2,128)(2,1)S(1)}, bf16[1,8,2,256]{3,2,1,0:T(2,128)(2,1)}, u32[]{:S(2)}) copy-start(bf16[1,8,2,256]{3,2,1,0:T(2,128)(2,1)} %param.8) | copy-start | bytes 24580
  2.1 0.7 %copy-start.4 = (s32[8,256]{1,0:T(8,128)S(1)}, s32[8,256]{1,0:T(8,128)}, u32[]{:S(2)}) copy-start(s32[8,256]{1,0:T(8,128)} %bins_ref.1) | copy-start | bytes 24580
  2.8 9.5 %collective-permute-start.5 = (bf16[88,256]{1,0:T(8,128)(2,1)S(1)}, bf16[88,256]{1,0:T(8,128)(2,1)S(1)}, u32[]{:S(2)}, u32[]{:S(2)}) collective-permute-start(bf16[88,256]{1,0:T(8,128)(2,1)S(1)} %shard_map.73.refs_0_), channel_id=1, source_target_pairs={{0,12},{4,8},{8,4},{12,0},{1,13},{5,9},{9,5},{13,1},{2,14},{6,10},... | collective-permute-start | bytes 135176 | tf_op jit(solution)/shard_map/ppermute | solution.py:459
  8.0 9.7 %collective-permute-start.2 = (f32[32,2,256]{2,1,0:T(2,128)}, f32[32,2,256]{2,1,0:T(2,128)S(1)}, u32[]{:S(2)}, u32[]{:S(2)}) collective-permute-start(f32[32,2,256]{2,1,0:T(2,128)} %bitcast.3), channel_id=1, source_target_pairs={{0,12},{4,8},{8,4},{12,0},{1,13},{5,9},{9,5},{13,1},{2,14},{6,10},... | collective-permute-start | bytes 196616 | tf_op jit(solution)/shard_map/ppermute | solution.py:459
  8.0 9.6 %collective-permute-start.1 = (f32[32,2,256]{2,1,0:T(2,128)}, f32[32,2,256]{2,1,0:T(2,128)S(1)}, u32[]{:S(2)}, u32[]{:S(2)}) collective-permute-start(f32[32,2,256]{2,1,0:T(2,128)} %bitcast.4), channel_id=1, source_target_pairs={{0,8},{4,12},{8,0},{12,4},{1,9},{5,13},{9,1},{13,5},{2,10},{6,14},... | collective-permute-start | bytes 196616 | tf_op jit(solution)/shard_map/ppermute | solution.py:459
  9.0 8.7 %collective-permute-start = (f32[32,2,256]{2,1,0:T(2,128)}, f32[32,2,256]{2,1,0:T(2,128)S(1)}, u32[]{:S(2)}, u32[]{:S(2)}) collective-permute-start(f32[32,2,256]{2,1,0:T(2,128)} %bitcast.5), channel_id=1, source_target_pairs={{0,4},{4,0},{8,12},{12,8},{1,5},{5,1},{9,13},{13,9},{2,6},{6,2},{1... | collective-permute-start | bytes 196616 | tf_op jit(solution)/shard_map/ppermute | solution.py:459
  12.4 5.0 %collective-permute-start.4 = (bf16[88,256]{1,0:T(8,128)(2,1)S(1)}, bf16[88,256]{1,0:T(8,128)(2,1)S(1)}, u32[]{:S(2)}, u32[]{:S(2)}) collective-permute-start(bf16[88,256]{1,0:T(8,128)(2,1)S(1)} %shard_map.73.refs_0_), channel_id=1, source_target_pairs={{0,8},{4,12},{8,0},{12,4},{1,9},{5,13},{9,1},{13,5},{2,10},{6,14},... | collective-permute-start | bytes 135176 | tf_op jit(solution)/shard_map/ppermute | solution.py:459
  12.4 5.3 %collective-permute-start.3 = (bf16[88,256]{1,0:T(8,128)(2,1)S(1)}, bf16[88,256]{1,0:T(8,128)(2,1)S(1)}, u32[]{:S(2)}, u32[]{:S(2)}) collective-permute-start(bf16[88,256]{1,0:T(8,128)(2,1)S(1)} %shard_map.73.refs_0_), channel_id=1, source_target_pairs={{0,4},{4,0},{8,12},{12,8},{1,5},{5,1},{9,13},{13,9},{2,6},{6,2},{1... | collective-permute-start | bytes 135176 | tf_op jit(solution)/shard_map/ppermute | solution.py:459
  13.0 0.9 %copy-start = (f32[96,256]{1,0:T(8,128)S(1)}, f32[96,256]{1,0:T(8,128)}, u32[]{:S(2)}) copy-start(f32[96,256]{1,0:T(8,128)} %constant.2.clone.seed_ref) | copy-start | bytes 294916
  17.7 0.8 %copy-start.1 = (f32[1,32,2,256]{3,2,1,0:T(2,128)S(1)}, f32[1,32,2,256]{3,2,1,0:T(2,128)}, u32[]{:S(2)}) copy-start(f32[1,32,2,256]{3,2,1,0:T(2,128)} %param.7) | copy-start | bytes 196612
  18.6 14.1 %collective-permute-start.7 = (f32[4,32,2,256]{3,2,1,0:T(2,128)S(1)}, f32[4,32,2,256]{3,2,1,0:T(2,128)S(1)}, u32[]{:S(2)}, u32[]{:S(2)}) collective-permute-start(f32[4,32,2,256]{3,2,1,0:T(2,128)S(1)} %shard_map.76.refs_0_), channel_id=1, source_target_pairs={{0,2},{3,1},{1,0},{2,3},{4,6},{7,5},{5,4},{6,7},{8,10},{11,9},{9,8... | collective-permute-start | bytes 786440 | tf_op jit(solution)/shard_map/ppermute | solution.py:463
  20.1 12.6 %collective-permute-start.6 = (f32[4,32,2,256]{3,2,1,0:T(2,128)S(1)}, f32[4,32,2,256]{3,2,1,0:T(2,128)S(1)}, u32[]{:S(2)}, u32[]{:S(2)}) collective-permute-start(f32[4,32,2,256]{3,2,1,0:T(2,128)S(1)} %shard_map.76.refs_0_), channel_id=1, source_target_pairs={{1,2},{2,1},{5,6},{6,5},{9,10},{10,9},{13,14},{14,13},{17,18},{18,... | collective-permute-start | bytes 786440 | tf_op jit(solution)/shard_map/ppermute | solution.py:463
  20.7 5.4 %collective-permute-start.8 = (bf16[4,72,256]{2,1,0:T(8,128)(2,1)S(1)}, bf16[4,72,256]{2,1,0:T(8,128)(2,1)S(1)}, u32[]{:S(2)}, u32[]{:S(2)}) collective-permute-start(bf16[4,72,256]{2,1,0:T(8,128)(2,1)S(1)} %get-tuple-element.45.refs_0_), channel_id=1, source_target_pairs={{0,1},{1,0},{2,3},{3,2},{4,5},{5,4},{6,7},{7,6},{8,9},{9,8},{10,11... | collective-permute-start | bytes 442376 | tf_op jit(solution)/shard_map/ppermute | solution.py:499
  22.2 4.0 %collective-permute-start.10 = (bf16[4,16,256]{2,1,0:T(8,128)(2,1)S(1)}, bf16[4,16,256]{2,1,0:T(8,128)(2,1)S(1)}, u32[]{:S(2)}, u32[]{:S(2)}) collective-permute-start(bf16[4,16,256]{2,1,0:T(8,128)(2,1)S(1)} %get-tuple-element.40.refs_2_), channel_id=1, source_target_pairs={{0,2},{3,1},{1,0},{2,3},{4,6},{7,5},{5,4},{6,7},{8,10},{11,9},{9,8... | collective-permute-start | bytes 98312 | tf_op jit(solution)/shard_map/ppermute | solution.py:463
  22.7 3.4 %collective-permute-start.9 = (bf16[4,16,256]{2,1,0:T(8,128)(2,1)S(1)}, bf16[4,16,256]{2,1,0:T(8,128)(2,1)S(1)}, u32[]{:S(2)}, u32[]{:S(2)}) collective-permute-start(bf16[4,16,256]{2,1,0:T(8,128)(2,1)S(1)} %get-tuple-element.40.refs_2_), channel_id=1, source_target_pairs={{1,2},{2,1},{5,6},{6,5},{9,10},{10,9},{13,14},{14,13},{17,18},{18,... | collective-permute-start | bytes 98312 | tf_op jit(solution)/shard_map/ppermute | solution.py:463
  33.2 3.4 %collective-permute-start.11 = (f32[2,256,256]{2,1,0:T(8,128)S(1)}, f32[2,256,256]{2,1,0:T(8,128)S(1)}, u32[]{:S(2)}, u32[]{:S(2)}) collective-permute-start(f32[2,256,256]{2,1,0:T(8,128)S(1)} %get-tuple-element.51.refs_1_), channel_id=1, source_target_pairs={{0,1},{1,0},{2,3},{3,2},{4,5},{5,4},{6,7},{7,6},{8,9},{9,8},{10,11... | collective-permute-start | bytes 1572872 | tf_op jit(solution)/shard_map/ppermute | solution.py:514
  44.7 2.0 %collective-permute-start.12 = (f32[2,256,256]{2,1,0:T(8,128)S(1)}, f32[2,256,256]{2,1,0:T(8,128)S(1)}, u32[]{:S(2)}, u32[]{:S(2)}) collective-permute-start(f32[2,256,256]{2,1,0:T(8,128)S(1)} %get-tuple-element.58.refs_2_), channel_id=1, source_target_pairs={{0,1},{1,0},{2,3},{3,2},{4,5},{5,4},{6,7},{7,6},{8,9},{9,8},{10,11... | collective-permute-start | bytes 1572872 | tf_op jit(solution)/shard_map/ppermute | solution.py:514
  54.6 2.0 %collective-permute-start.13 = (f32[2,256,256]{2,1,0:T(8,128)S(1)}, f32[2,256,256]{2,1,0:T(8,128)S(1)}, u32[]{:S(2)}, u32[]{:S(2)}) collective-permute-start(f32[2,256,256]{2,1,0:T(8,128)S(1)} %get-tuple-element.60.refs_2_), channel_id=1, source_target_pairs={{0,1},{1,0},{2,3},{3,2},{4,5},{5,4},{6,7},{7,6},{8,9},{9,8},{10,11... | collective-permute-start | bytes 1572872 | tf_op jit(solution)/shard_map/ppermute | solution.py:514
  64.5 2.0 %collective-permute-start.14 = (f32[2,256,256]{2,1,0:T(8,128)S(1)}, f32[2,256,256]{2,1,0:T(8,128)S(1)}, u32[]{:S(2)}, u32[]{:S(2)}) collective-permute-start(f32[2,256,256]{2,1,0:T(8,128)S(1)} %get-tuple-element.62.refs_0_), channel_id=1, source_target_pairs={{0,1},{1,0},{2,3},{3,2},{4,5},{5,4},{6,7},{7,6},{8,9},{9,8},{10,11... | collective-permute-start | bytes 1572872 | tf_op jit(solution)/shard_map/ppermute | solution.py:514
